TPU v7x, 256 devices: a whole 4x4x8 slice. The times are simulated.
256 devices in a mesh: scen: 32 (over y, x, core), row: 4 (over z_hi), col: 2 (over z_lo).
Axes of the slice: x: 4, y: 4, z: 8 (z_hi: 4, z_lo: 2; z = z_hi * 2 + z_lo), core: 2. Of those that a mesh axis runs over, the one named last changes fastest.
Arguments:
- border: bfloat16 [128, 32, 512, 512], P('scen', None, ('row', 'col')), may hold values from -4.5 to 4.5, as said below
- panel_border: bfloat16 [128, 512, 512], P('scen'), may hold values from -0.09375 to 0.09375
- kinv: bfloat16 [128, 512, 512], P('scen'), may hold values from -1 to 4, as said below
- factor: bfloat16 [16384, 4096], P(('scen', 'row'), 'col'), may hold values from -4.5 to 4.5
- root_block: float32 [16384, 512], P(('scen', 'row', 'col')), may hold values from -9 to 43, as said below
Outputs:
- panel_factor: float32 [16384, 512], P(('scen', 'row', 'col'))
Inputs may be any that keep to these rules, and one draw needn't show every extreme that they name: border[s, 0] is panel_border[s] transposed. `kinv`: each scenario's matrix is symmetric positive definite up to rounding, with eigenvalues 0.5 or more. `root_block`: its first 512 rows form a symmetric matrix; schur[0:512] is positive definite.
All inputs are finite; a program needn't handle non-finite values.
Results may differ from a plain program's by a relative error of at most 0.0025.
Values may be sent and summed in bfloat16 or wider, within the bound.
No kernel may reach another device: no remote copies, remote signals or barrier semaphores. Data moves between devices by JAX's collectives and lax.ppermute only.
A program may use at most 128 MiB of HBM per device.

v0:
```python
import jax
import jax.numpy as jnp
from jax import lax
from jax.sharding import Mesh
from jax.sharding import PartitionSpec as P

SCEN = ("scen_0", "scen_1", "scen_2")
SCEN_ROW = ("scen_0", "scen_1", "scen_2", "row")
SCEN_ROW_COL = ("scen_0", "scen_1", "scen_2", "row", "col")


def in_blocks(value, dim, peers):
    lengths = value.shape
    pieces = value.reshape(*lengths[:dim], peers, lengths[dim] // peers, *lengths[dim + 1 :])
    return jnp.moveaxis(pieces, dim, 0)


def summed_rows_2(value, chips, core, dim):
    sizes = (lax.axis_size(chips), lax.axis_size(core))
    pieces = in_blocks(value, dim, sizes[0] * sizes[1])
    inside = pieces.shape[1:]
    pieces = pieces.reshape(*sizes, *inside).swapaxes(0, 1).reshape(-1, *inside)
    pieces = lax.psum_scatter(pieces, core, scatter_dimension=0, tiled=True)
    return lax.psum_scatter(pieces, chips, scatter_dimension=0, tiled=True)[0]


def broadcast(value, axis, root):
    return lax.dynamic_index_in_dim(lax.all_gather(value, axis), root, 0, keepdims=False)


def from_everyone(value, axis):
    copies = jnp.broadcast_to(value, (lax.axis_size(axis), *value.shape))
    return lax.all_to_all(copies, axis, split_axis=0, concat_axis=0, tiled=True)


def in_order(pieces, dim):
    pieces = jnp.moveaxis(pieces, 0, dim)
    lengths = pieces.shape
    return pieces.reshape(*lengths[:dim], lengths[dim] * lengths[dim + 1], *lengths[dim + 2 :])


def gathered_copies(value, axis, dim):
    pieces = from_everyone(value, axis)
    return in_order(pieces, dim)


def sum_at_owner(value, axis, dim):
    peers = lax.axis_size(axis)
    pieces = lax.all_to_all(in_blocks(value, dim, peers), axis, 0, 0, tiled=True)
    return jnp.sum(pieces, axis=0)


def per_device(border, panel_border, kinv, factor, root_block):
    solved = jnp.einsum(
        "snm,smp->snp", kinv, panel_border, preferred_element_type=jnp.float32
    ).astype(jnp.bfloat16)
    flat = border.reshape(border.shape[0], border.shape[1] * border.shape[2], border.shape[3])
    coupling = summed_rows_2(
        jnp.einsum("srn,snp->rp", flat, solved, preferred_element_type=jnp.float32),
        ("scen_0", "scen_1"),
        "scen_2",
        0,
    )
    heading = broadcast(factor, SCEN, 0)
    leading = gathered_copies(heading, "row", 0)
    update = sum_at_owner(
        lax.dot_general(
            factor, leading, (((1,), (1,)), ((), ())), preferred_element_type=jnp.float32
        ),
        "col",
        0,
    )
    schur = root_block + coupling - update
    topmost = broadcast(schur, SCEN, 0)
    diagonal_block = gathered_copies(topmost, ("row", "col"), 0)
    lower = jnp.linalg.cholesky(diagonal_block)
    return jax.scipy.linalg.solve_triangular(lower, schur.T, lower=True).T


def solution(mesh):
    split = Mesh(
        mesh.devices.reshape(4, 4, 2, mesh.shape["row"], mesh.shape["col"]),
        ("scen_0", "scen_1", "scen_2", "row", "col"),
    )
    in_specs = (
        P(SCEN, None, ("row", "col"), None),
        P(SCEN, None, None),
        P(SCEN, None, None),
        P(SCEN_ROW, "col"),
        P(SCEN_ROW_COL, None),
    )
    out_specs = P(SCEN_ROW_COL, None)
    return jax.shard_map(
        per_device, mesh=split, in_specs=in_specs, out_specs=out_specs, check_vma=False
    )
```

profile of v0, /device:TPU:1, one launch (start us, length us, event | category | flops | bytes accessed | tf_op | source)
XLA Modules:
  0.0 429.6 jit_solution(12433448312266242336)
XLA Ops:
  7.4 1.6 copy-done
  9.0 11.6 %convolution_bitcast_fusion = f32[2048,512]{0,1:T(8,128)} fusion(bf16[4,2048,512]{2,1,0:T(8,128)(2,1)} %bitcast.85, bf16[4,512,512]{2,1,0:T(8,128)(2,1)S(1)} %copy-done, bf16[4,512,512]{2,1,0:T(8,128)(2,1)} %param.6), kind=kOutput, calls=%fused_computation.2 | convolution fusion | flops 5369757696 | bytes 16777216 | tf_op jit(solution)/shard_map/srn,snp->rp/dot_general | solution.py:59
  20.5 5.3 %copy.16 = f32[2048,512]{1,0:T(8,128)} copy(f32[2048,512]{0,1:T(8,128)} %convolution_bitcast_fusion) | data formatting | bytes 8388608 | tf_op jit(solution)/shard_map/srn,snp->rp/dot_general | solution.py:59
  25.9 4.8 %copy.17 = f32[2,16,64,512]{3,2,1,0:T(8,128)} copy(f32[2,16,64,512]{3,2,0,1:T(8,128)} %bitcast.77) | data formatting | bytes 8388608 | tf_op jit(solution)/shard_map/transpose | solution.py:22
  31.4 21.5 %reduce-scatter.5.cloned.1.call-done = f32[16,64,512]{2,1,0:T(8,128)} async-done(((f32[32,64,512]{2,1,0:T(8,128)}), f32[16,64,512]{2,1,0:T(8,128)}) %reduce-scatter.5.cloned.1.call-update) | async-done | bytes 2097168 | tf_op jit(solution)/shard_map/reduce_scatter | solution.py:23
  52.9 64.1 %all-gather.5.cloned.1.call-done = bf16[4096,2048]{1,0:T(8,128)(2,1)} async-done(((bf16[128,2048]{1,0:T(8,128)(2,1)}), bf16[4096,2048]{1,0:T(8,128)(2,1)}) %all-gather.5.cloned.1.call-update) | async-done | bytes 16777232 | tf_op jit(solution)/shard_map/all_gather | solution.py:28
  117.0 1.1 slice.129
  118.3 55.9 %all_to_all.15 = bf16[4,128,2048]{2,1,0:T(8,128)(2,1)S(1)} all-to-all(bf16[4,128,2048]{2,1,0:T(8,128)(2,1)S(1)} %broadcast_in_dim.8), channel_id=1, replica_groups=mesh['scen_0'=4,'scen_1'=4,'scen_2'=2,'row'=4,'col'=2] {'row'}, dimensions={0} | all-to-all | bytes 4194304 | tf_op jit(solution)/shard_map/all_to_all | solution.py:33
  174.2 0.8 fusion.35
  175.1 6.4 %all_to_all.16 = f32[2,64,512]{2,1,0:T(8,128)S(1)} all-to-all(f32[2,64,512]{2,1,0:T(8,128)S(1)} %fusion.35), channel_id=1, replica_groups=mesh['scen_0'=4,'scen_1'=4,'scen_2'=2,'row'=4,'col'=2] {'col'}, dimensions={0} | all-to-all | bytes 524288 | tf_op jit(solution)/shard_map/all_to_all | solution.py:49
  181.5 1.6 fusion.12
  183.1 49.9 %all-gather.7.cloned.1.call-done = f32[2048,512]{1,0:T(8,128)} async-done(((f32[64,512]{1,0:T(8,128)}), f32[2048,512]{1,0:T(8,128)}) %all-gather.7.cloned.1.call-update) | async-done | bytes 4194320 | tf_op jit(solution)/shard_map/all_gather | solution.py:28
  233.1 0.9 slice.130
  234.0 1.1 broadcast_in_dim.9
  235.1 6.7 %all-to-all-start.2 = ((f32[8,64,512]{2,1,0:T(8,128)}), f32[8,64,512]{2,1,0:T(8,128)S(1)}, u32[]{:S(2)}, u32[]{:S(2)}) async-start(f32[8,64,512]{2,1,0:T(8,128)} %broadcast_in_dim.9), calls=%async_computation.3 | async-start | bytes 2097152 | tf_op jit(solution)/shard_map/all_to_all | solution.py:33
  241.8 29.2 %all-to-all-done.2 = f32[8,64,512]{2,1,0:T(8,128)S(1)} async-done(((f32[8,64,512]{2,1,0:T(8,128)}), f32[8,64,512]{2,1,0:T(8,128)S(1)}, u32[]{:S(2)}, u32[]{:S(2)}) %all-to-all-start.2) | async-done | bytes 1048608 | tf_op jit(solution)/shard_map/all_to_all | solution.py:33
  271.1 1.3 copy.18
  272.4 1.4 fusion.3
  273.8 1.0 copy-done.1
  274.8 11.7 %cholesky.104 = f32[128,128]{1,0:T(8,128)S(1)} custom-call(f32[128,128]{1,0:T(8,128)S(1)} %cholesky.266), custom_call_target="Cholesky" | custom-call | tf_op jit(solution)/shard_map/jit(cholesky)/cholesky | solution.py:76
  286.6 9.8 %custom-call.31 = f32[1,128,128]{1,2,0:T(8,128)S(1)} custom-call(f32[1,128,128]{2,1,0:T(8,128)S(1)} %get-tuple-element.32), custom_call_target="InvertDiagBlocksLowerTriangular" | custom-call | tf_op jit(solution)/shard_map/jit(cholesky)/cholesky | solution.py:76
  296.5 1.2 constant_dynamic-update-slice_fusion.3
  297.7 1.3 convolution_subtract_fusion
  299.0 11.7 %cholesky.217 = f32[128,128]{1,0:T(8,128)S(1)} custom-call(f32[128,128]{1,0:T(8,128)S(1)} %cholesky.270), custom_call_target="Cholesky" | custom-call | tf_op jit(solution)/shard_map/jit(cholesky)/cholesky | solution.py:76
  310.7 10.0 %custom-call.32 = f32[1,128,128]{1,2,0:T(8,128)S(1)} custom-call(f32[1,128,128]{2,1,0:T(8,128)S(1)} %get-tuple-element.29), custom_call_target="InvertDiagBlocksLowerTriangular" | custom-call | tf_op jit(solution)/shard_map/jit(cholesky)/cholesky | solution.py:76
  321.0 1.3 convolution_subtract_fusion.1
  322.3 11.7 %cholesky.238 = f32[128,128]{1,0:T(8,128)S(1)} custom-call(f32[128,128]{1,0:T(8,128)S(1)} %cholesky.275), custom_call_target="Cholesky" | custom-call | tf_op jit(solution)/shard_map/jit(cholesky)/cholesky | solution.py:76
  334.1 9.8 %custom-call.33 = f32[1,128,128]{1,2,0:T(8,128)S(1)} custom-call(f32[1,128,128]{2,1,0:T(8,128)S(1)} %get-tuple-element.26), custom_call_target="InvertDiagBlocksLowerTriangular" | custom-call | tf_op jit(solution)/shard_map/jit(cholesky)/cholesky | solution.py:76
  344.1 1.2 convolution_subtract_fusion.2
  345.3 11.7 %cholesky.255 = f32[128,128]{1,0:T(8,128)S(1)} custom-call(f32[128,128]{1,0:T(8,128)S(1)} %convolution_subtract_fusion.2), custom_call_target="Cholesky" | custom-call | tf_op jit(solution)/shard_map/jit(cholesky)/cholesky | solution.py:76
  357.1 0.7 compare_reduce_fusion.1
  357.8 0.6 compare_reduce_fusion
  358.4 0.7 compare_reduce_fusion.2
  361.6 1.1 select_select_fusion
  362.8 14.2 %while.1 = (s32[]{:T(128)}, f32[512,512]{1,0:T(8,128)}, s32[4,2]{0,1:T(2,128)S(1)}, f32[4,128,128]{2,1,0:T(8,128)}, s32[]{:T(128)}) while((s32[]{:T(128)}, f32[512,512]{1,0:T(8,128)}, s32[4,2]{0,1:T(2,128)S(1)}, f32[4,128,128]{2,1,0:T(8,128)}, s32[]{:T(128)}) %tuple.27), condition=%wide.while_cond, body=%wide.while_body.sunk | while | flops 2 | bytes 132205 | solution.py:77
  362.8 0.6 fusion.47
  363.4 2.9 bitcast_dynamic-update-slice_fusion.2
  366.4 0.6 fusion.47
  367.0 2.9 bitcast_dynamic-update-slice_fusion.2
  370.0 0.6 fusion.47
  370.6 2.9 bitcast_dynamic-update-slice_fusion.2
  373.6 0.6 fusion.47
  374.1 2.9 bitcast_dynamic-update-slice_fusion.2
  377.0 40.1 %custom-call.34 = f32[4,128,128]{1,2,0:T(8,128)S(1)} custom-call(f32[4,128,128]{2,1,0:T(8,128)} %get-tuple-element.12), custom_call_target="InvertDiagBlocksLowerTriangular" | custom-call | tf_op jit(solution)/shard_map/jit(_solve_triangular)/triangular_solve | solution.py:77
  417.3 1.1 convolution_subtract_fusion.5
  418.6 1.2 convolution_subtract_fusion.4
  420.0 1.3 convolution_subtract_fusion.3
  421.5 0.7 maximum_bitcast_fusion
  (40 shorter events, 2.8 us)
Async XLA Ops:
  7.4 1.6 copy-start
  7.4 45.4 %reduce-scatter.5.cloned.1.call-start = ((), (), s32[]{:S(2)}) async-start(), calls=%async_computation.5 | async-start | bytes 6291456 | tf_op jit(solution)/shard_map/reduce_scatter | solution.py:23
  30.7 86.2 %all-gather.5.cloned.1.call-start = ((), (), s32[]{:S(2)}) async-start(), calls=%async_computation.6 | async-start | bytes 17301504 | tf_op jit(solution)/shard_map/all_gather | solution.py:28
  31.3 150.2 %reduce-scatter.7.cloned.1.call-start = ((), (), s32[]{:S(2)}) async-start(), calls=%async_computation.8 | async-start | bytes 2228224
  52.8 180.2 %all-gather.7.cloned.1.call-start = ((), (), s32[]{:S(2)}) async-start(), calls=%async_computation.7 | async-start | bytes 4325376 | tf_op jit(solution)/shard_map/all_gather | solution.py:28
  118.3 55.9 %copy-start.2 = (bf16[128,2048]{1,0:T(8,128)(2,1)S(1)}, bf16[128,2048]{1,0:T(8,128)(2,1)}, u32[]{:S(2)}) copy-start(bf16[128,2048]{1,0:T(8,128)(2,1)} %param.8) | copy-start | bytes 1572868
  174.2 7.3 %copy-start.4 = (f32[64,512]{1,0:T(8,128)S(1)}, f32[64,512]{1,0:T(8,128)}, u32[]{:S(2)}) copy-start(f32[64,512]{1,0:T(8,128)} %param.9) | copy-start | bytes 393220
  235.1 36.0 %all-to-all-start.2 = ((f32[8,64,512]{2,1,0:T(8,128)}), f32[8,64,512]{2,1,0:T(8,128)S(1)}, u32[]{:S(2)}, u32[]{:S(2)}) async-start(f32[8,64,512]{2,1,0:T(8,128)} %broadcast_in_dim.9), calls=%async_computation.3 | async-start | bytes 2097152 | tf_op jit(solution)/shard_map/all_to_all | solution.py:33
  273.8 1.0 copy-start.1
  322.3 94.8 %copy-start.3 = (f32[64,512]{1,0:T(8,128)S(1)}, f32[64,512]{1,0:T(8,128)}, u32[]{:S(2)}) copy-start(f32[64,512]{1,0:T(8,128)} %fusion.12) | copy-start | bytes 393220
Sparse Core Ops, SparseCore 0:
  30.8 21.9 reduce-scatter.4
  56.4 107.0 reduce-scatter.6
Sparse Core Ops, SparseCore 1:
  33.8 83.1 all-gather.4
  183.2 49.8 all-gather.6
where the time goes:
time: 430 us
  waiting for transfers between devices  165 us (38%)
  other arithmetic  124 us (29%)
  blocking collectives  62.3 us (14%)
  local copies, waits for them, and re-layouts  31.8 us (7%)
  matrix products  22.2 us (5%)
  between operations  17.6 us (4%)
  starting transfers between devices  6.86 us (2%)
    all_gather x2, waiting for transfers between devices, broadcast(): lax.all_gather(value, axis)  114 us
    another operation x14, other arithmetic, per_device(): lower = jnp.linalg.cholesky(diagonal_block)  78.7 us
    all_to_all x1, blocking collectives, from_everyone(): return lax.all_to_all(copies, axis, split_axis=0, concat_axis=0, tiled=True)  55.9 us
    another operation x3, other arithmetic, per_device(): return jax.scipy.linalg.solve_triangular(lower, schur.T, lower=True).T  41.2 us
    all_to_all x1, waiting for transfers between devices, from_everyone(): return lax.all_to_all(copies, axis, split_axis=0, concat_axis=0, tiled=True)  29.2 us
    reduce_scatter x1, waiting for transfers between devices, summed_rows_2(): pieces = lax.psum_scatter(pieces, core, scatter_dimension=0, tiled=True)  21.5 us
    another operation x12, local copies, waits for them, and re-layouts  14.2 us
    dot_general x1, matrix products, per_device(): jnp.einsum('srn,snp->rp', flat, solved, preferred_element_type=jnp.float32)  11.6 us
  transfers between devices with their start and end apart: 5, of which 4 were waited for; matrix products, arithmetic and copies ran while one was open for 1% of the time, Pallas kernels for 0%

commit v1 on v0

v1 whole, which is shorter than its diff:
```python
import jax
import jax.numpy as jnp
from jax import lax
from jax.experimental import pallas as pl
from jax.experimental.pallas import tpu as pltpu
from jax.sharding import Mesh
from jax.sharding import PartitionSpec as P

CHIPS = ("scen_0", "scen_1")
CORE = "scen_2"
SCEN = ("scen_0", "scen_1", "scen_2")
SCEN_ROW = ("scen_0", "scen_1", "scen_2", "row")
SCEN_ROW_COL = ("scen_0", "scen_1", "scen_2", "row", "col")
BF16 = jnp.bfloat16

BLOCK = 128
F32 = jnp.float32


def spread_row(value, row):
    return jnp.broadcast_to(value[row : row + 1, :], value.shape)


def spread_lane(value, lane):
    return jnp.broadcast_to(value[:, lane : lane + 1], value.shape)


def factor_block(rows):
    groups = len(rows)
    tile = rows[0].shape
    sub = lax.broadcasted_iota(jnp.int32, tile, 0)
    lane = lax.broadcasted_iota(jnp.int32, tile, 1)
    inverse = [jnp.where(lane == sub + 8 * g, 1.0, 0.0).astype(F32) for g in range(groups)]
    rows = list(rows)
    done = []
    for t in range(groups):
        cols = [spread_lane(rows[t], 8 * t + j) for j in range(8)]
        left, right = rows[t], inverse[t]
        ahead = inverse[t]
        scale = jnp.zeros(tile, F32)
        square = jnp.zeros(tile, F32)
        for k in range(8):
            root = lax.rsqrt(spread_row(cols[k], k))
            recip = root * root
            scale = jnp.where(sub == k, root, scale)
            square = jnp.where(sub == k, recip, square)
            full = jnp.where(sub == k, 0.0, cols[k] * recip)
            below = jnp.where(sub > k, full, 0.0)
            for j in range(k + 1, 8):
                cols[j] = cols[j] - full * spread_row(cols[j], k)
            left = left - full * spread_row(left, k)
            right = right - full * spread_row(right, k)
            ahead = ahead - below * spread_row(ahead, k)
        done.append(ahead * scale)
        if t == groups - 1:
            break
        left, right = left * square, right * square
        lefts = [spread_row(left, j) for j in range(8)]
        rights = [spread_row(right, j) for j in range(8)]
        for g in range(t + 1, groups):
            coef = [spread_lane(rows[g], 8 * t + j) for j in range(8)]
            a = [coef[j] * lefts[j] for j in range(8)]
            b = [coef[j] * rights[j] for j in range(8)]
            while len(a) > 1:
                a = [a[i] + a[i + 1] for i in range(0, len(a), 2)]
                b = [b[i] + b[i + 1] for i in range(0, len(b), 2)]
            rows[g] = rows[g] - a[0]
            inverse[g] = inverse[g] - b[0]
    return done


def dot(a, b, dims=((1,), (0,))):
    return lax.dot_general(a, b, (dims, ((), ())), precision=lax.Precision.HIGHEST, preferred_element_type=F32)


def inverse_kernel(core_ref, own_ref, other_ref, w_ref, s_ref, d_ref):
    n = w_ref.shape[0]
    blocks = n // BLOCK
    planes = own_ref.shape[1]
    half = n // planes // 2
    own = pl.multiple_of(core_ref[0] * half, half)
    other = pl.multiple_of(half - core_ref[0] * half, half)
    for piece in range(own_ref.shape[0]):
        down, across = divmod(piece, n // BLOCK)
        for plane in range(planes):
            at = plane * 2 * half + down * 8
            lanes = slice(across * BLOCK, (across + 1) * BLOCK)
            s_ref[pl.ds(own + at, 8), lanes] = own_ref[piece, plane]
            s_ref[pl.ds(other + at, 8), lanes] = other_ref[piece, plane]
    for k in range(blocks):
        lo, hi = k * BLOCK, (k + 1) * BLOCK
        done = factor_block([s_ref[lo + 8 * g : lo + 8 * g + 8, lo:hi] for g in range(BLOCK // 8)])
        for g in range(BLOCK // 8):
            d_ref[8 * g : 8 * g + 8, :] = done[g]
        w = d_ref[...]
        if k > 0:
            w_ref[lo:hi, 0:lo] = dot(w, w_ref[lo:hi, 0:lo])
        w_ref[lo:hi, lo:hi] = w
        if hi < n:
            w_ref[lo:hi, hi:n] = jnp.zeros((BLOCK, n - hi), F32)
            u = dot(w, s_ref[lo:hi, hi:n])
            for i in range(k + 1, blocks):
                il, ih = i * BLOCK, (i + 1) * BLOCK
                ui = u[:, il - hi : ih - hi]
                s_ref[il:ih, il:n] = s_ref[il:ih, il:n] - dot(ui, u[:, il - hi :], ((0,), (0,)))
                new = dot(ui, w_ref[lo:hi, 0:hi], ((0,), (0,)))
                if k > 0:
                    w_ref[il:ih, 0:lo] = w_ref[il:ih, 0:lo] - new[:, 0:lo]
                w_ref[il:ih, lo:hi] = -new[:, lo:hi]


def inverse_factor(core, own, other, n):
    return pl.pallas_call(
        inverse_kernel,
        out_shape=jax.ShapeDtypeStruct((n, n), F32),
        in_specs=[
            pl.BlockSpec(memory_space=pltpu.SMEM),
            pl.BlockSpec(memory_space=pltpu.VMEM),
            pl.BlockSpec(memory_space=pltpu.VMEM),
        ],
        out_specs=pl.BlockSpec(memory_space=pltpu.VMEM),
        scratch_shapes=[pltpu.VMEM((n, n), F32), pltpu.VMEM((BLOCK, BLOCK), F32)],
        cost_estimate=pl.CostEstimate(flops=40_000_000, bytes_accessed=2 * n * n * 4, transcendentals=n),
        name="inverse_factor",
    )(core, own, other)


def swapped(value, axis):
    return lax.ppermute(value, axis, [(0, 1), (1, 0)])


def gathered(value, axis):
    peers = lax.axis_size(axis)
    place = lax.axis_index(axis)
    pieces = [value]
    for step in range(1, peers):
        pieces.append(lax.ppermute(value, axis, [(i, (i + step) % peers) for i in range(peers)]))
    pieces = jnp.stack(pieces)
    return jnp.stack(
        [lax.dynamic_index_in_dim(pieces, (place - q) % peers, 0, keepdims=False) for q in range(peers)]
    )


def all_planes(value):
    pieces = gathered(gathered(value, "col"), "row")
    return pieces.reshape(-1, *value.shape)


def exchanged(pieces, axis):
    return lax.all_to_all(pieces, axis, 0, 0, tiled=True)


def half_of(value, dim, which, parts=2):
    size = value.shape[dim] // parts
    return lax.dynamic_slice_in_dim(value, which * size, size, dim)


def factor_slices(factor):
    col = lax.axis_index("col")
    chips = lax.axis_size(SCEN) // 2
    mine = half_of(factor, 0, col)
    theirs = swapped(half_of(factor, 0, 1 - col), "col")
    mine, theirs = (
        jnp.moveaxis(v.reshape(v.shape[0], chips, -1), 1, 0) for v in (mine, theirs)
    )
    first = jnp.where(col == 0, mine, theirs)
    second = jnp.where(col == 0, theirs, mine)
    return exchanged(jnp.concatenate([first, second]), SCEN)


def per_device(border, panel_border, kinv, factor, root_block):
    core = lax.axis_index(CORE)
    scen = lax.axis_index(SCEN)
    plane = lax.axis_index(("row", "col"))
    chips = lax.axis_size(CHIPS)
    groups, rows, n = border.shape[1], border.shape[2], border.shape[3]

    slices = factor_slices(factor)
    leading = all_planes(slices[0])
    leading = leading.reshape(-1, leading.shape[-1])

    solved = jnp.einsum(
        "snm,smp->snp", kinv, panel_border, preferred_element_type=F32
    ).astype(BF16)

    own_solved = lax.dynamic_slice_in_dim(solved, plane * rows, rows, 2)
    panel = jnp.einsum("snr,snp->rp", own_solved, panel_border, preferred_element_type=F32)
    panel = panel - lax.dot_general(
        slices[0], leading, (((1,), (1,)), ((), ())), preferred_element_type=F32
    )
    panel = panel + jnp.where(scen == 0, root_block, 0.0)
    panel = half_of(panel, 0, core) + swapped(half_of(panel, 0, 1 - core), CORE)
    width = panel.shape[1]
    tiles = panel.reshape(panel.shape[0] // 8, 8, width // BLOCK, BLOCK)
    tiles = tiles.transpose(0, 2, 1, 3).reshape(-1, 8, BLOCK)
    tile = jnp.sum(exchanged(tiles, CHIPS), axis=0)
    tile = all_planes(tile)
    own = exchanged(jnp.broadcast_to(tile, (chips, *tile.shape)), CHIPS)
    other = swapped(own, CORE)
    inverse = inverse_factor(core.astype(jnp.int32).reshape(1), own, other, width)

    coupling = jnp.einsum("sgrn,snp->grp", border, solved, preferred_element_type=F32)
    update = lax.dot_general(
        slices, leading, (((2,), (1,)), ((), ())), preferred_element_type=F32
    )
    partial = (coupling - update).reshape(chips, 2, rows, width)
    mine = half_of(partial, 1, core)[:, 0] + swapped(half_of(partial, 1, 1 - core), CORE)[:, 0]
    pieces = exchanged(mine.astype(BF16), CHIPS)
    schur = root_block + jnp.sum(pieces.astype(F32), axis=0)
    return lax.dot_general(
        schur, inverse, (((1,), (1,)), ((), ())),
        precision=lax.Precision.HIGHEST, preferred_element_type=F32,
    )


def solution(mesh):
    split = Mesh(
        mesh.devices.reshape(4, 4, 2, mesh.shape["row"], mesh.shape["col"]),
        ("scen_0", "scen_1", "scen_2", "row", "col"),
    )
    in_specs = (
        P(SCEN, None, ("row", "col"), None),
        P(SCEN, None, None),
        P(SCEN, None, None),
        P(SCEN_ROW, "col"),
        P(SCEN_ROW_COL, None),
    )
    out_specs = P(SCEN_ROW_COL, None)
    return jax.shard_map(
        per_device, mesh=split, in_specs=in_specs, out_specs=out_specs, check_vma=False
    )
```

time: 430 us -> 141 us (0.33)
  waiting for transfers between devices: 165 us -> 19.5 us
  other arithmetic: 124 us -> 4.94 us
  blocking collectives: 62.3 us -> 30 us
  starting transfers between devices: 6.86 us -> 35.2 us
  Pallas kernels: 0 us -> 26.8 us
  local copies, waits for them, and re-layouts: 31.8 us -> 6.43 us
  between operations: 17.6 us -> 0.24 us
  matrix products: 22.2 us -> 17.2 us
    another operation x17 -> x8, other arithmetic: 120 us -> 0.09 us  [the longest x6 0.06 us: gathered(): pieces = jnp.stack(pieces)]
    all_gather x2 -> x0, waiting for transfers between devices: 114 us -> none  [broadcast(): lax.all_gather(value, axis)]
    all_to_all x2, blocking collectives: 62.3 us -> 30 us  [exchanged(): return lax.all_to_all(pieces, axis, 0, 0, tiled=True)]
    ppermute x0 -> x12, starting transfers between devices: none -> 28 us  [the longest x8 17 us: gathered(): lax.ppermute(value, axis, [(i, (i + step) % peers) for i in range(peers)])]
    pallas_call x0 -> x1, Pallas kernels: none -> 26.8 us  [inverse_factor(): pl.pallas_call(inverse_kernel, out_shape=jax.ShapeDtypeStruct((n, n), F32...]
    all_to_all x1 -> x2, waiting for transfers between devices: 29.2 us -> 5.41 us  [exchanged(): return lax.all_to_all(pieces, axis, 0, 0, tiled=True)]
    reduce_scatter x1 -> x0, waiting for transfers between devices: 21.5 us -> none  [summed_rows_2(): pieces = lax.psum_scatter(pieces, core, scatter_dimension=0, tiled=True)]
    another operation x17 -> x0, local copies, waits for them, and re-layouts: 14.4 us -> none
  transfers between devices with their start and end apart: 5 -> 14, of which waited for: 4 -> 8; matrix products, arithmetic and copies ran while one was open for 1% -> 8% of each run, Pallas kernels for 0% -> 19%
where the time goes in v1:
time: 141 us; the launch traced here: 140 us
  starting transfers between devices  35.2 us (25%)
  blocking collectives  30 us (21%)
  Pallas kernels  26.8 us (19%)
  waiting for transfers between devices  19.5 us (14%)
  matrix products  17.2 us (12%)
  local copies, waits for them, and re-layouts  6.43 us (5%)
  other arithmetic  4.94 us (4%)
    all_to_all x2, blocking collectives, exchanged(): return lax.all_to_all(pieces, axis, 0, 0, tiled=True)  30 us
    pallas_call x1, Pallas kernels, inverse_factor(): pl.pallas_call(inverse_kernel, out_shape=jax.ShapeDtypeStruct((n, n), F32...  26.8 us
    ppermute x8, starting transfers between devices, gathered(): lax.ppermute(value, axis, [(i, (i + step) % peers) for i in range(peers)])  17 us
    ppermute x4, starting transfers between devices, swapped(): return lax.ppermute(value, axis, [(0, 1), (1, 0)])  11.1 us
    ppermute x4, waiting for transfers between devices, swapped(): return lax.ppermute(value, axis, [(0, 1), (1, 0)])  8.54 us
    all_to_all x2, starting transfers between devices, exchanged(): return lax.all_to_all(pieces, axis, 0, 0, tiled=True)  7.22 us
    dot_general x1, matrix products, per_device(): jnp.einsum('sgrn,snp->grp', border, solved, preferred_element_type=F32)  6.95 us
    ppermute x8, waiting for transfers between devices, gathered(): lax.ppermute(value, axis, [(i, (i + step) % peers) for i in range(peers)])  5.6 us
  transfers between devices with their start and end apart: 14, of which 8 were waited for; matrix products, arithmetic and copies ran while one was open for 8% of the time, Pallas kernels for 19%

profile of v1, /device:TPU:1, one launch (start us, length us, event | category | flops | bytes accessed | tf_op | source)
XLA Modules:
  0.0 140.4 jit_solution(11957075089159190307)
XLA Ops:
  0.0 1.1 constant_dynamic-slice_fusion.10
  1.1 2.5 %collective-permute-start = (bf16[64,2048]{1,0:T(8,128)(2,1)S(1)}, bf16[64,2048]{1,0:T(8,128)(2,1)S(1)}, u32[]{:S(2)}, u32[]{:S(2)}) collective-permute-start(bf16[64,2048]{1,0:T(8,128)(2,1)S(1)} %constant_dynamic-slice_fusion.10), channel_id=1, source_target_pairs={{0,1},{1,0},{2,3},{3,2},{4,5},{5,4},{6,7},{7,6},{8,9},{9,8},{10,11... | collective-permute-start | bytes 786440 | tf_op jit(solution)/shard_map/ppermute | solution.py:129
  3.7 5.0 %collective-permute-done = bf16[64,2048]{1,0:T(8,128)(2,1)S(1)} collective-permute-done((bf16[64,2048]{1,0:T(8,128)(2,1)S(1)}, bf16[64,2048]{1,0:T(8,128)(2,1)S(1)}, u32[]{:S(2)}, u32[]{:S(2)}) %collective-permute-start) | collective-permute-done | bytes 262176 | tf_op jit(solution)/shard_map/ppermute | solution.py:129
  8.7 1.1 select_bitcast_fusion.1
  9.7 0.1 bitcast_bitcast_fusion
  9.9 20.6 %all_to_all.20 = bf16[32,64,128]{2,1,0:T(8,128)(2,1)S(1)} all-to-all(bf16[32,64,128]{2,1,0:T(8,128)(2,1)S(1)} %pad_maximum_fusion), channel_id=1, replica_groups=mesh['scen_0'=4,'scen_1'=4,'scen_2'=2,'row'=4,'col'=2] {'scen_0','scen_1..., dimensions={0} | all-to-all | bytes 1048576 | tf_op jit(solution)/shard_map/all_to_all | solution.py:150
  30.5 1.5 %collective-permute-start.1 = (bf16[64,128]{1,0:T(8,128)(2,1)S(1)}, bf16[64,128]{1,0:T(8,128)(2,1)S(1)}, u32[]{:S(2)}, u32[]{:S(2)}) collective-permute-start(bf16[64,128]{1,0:T(8,128)(2,1)S(1)} %get-tuple-element.7), channel_id=1, source_target_pairs={{0,1},{1,0},{2,3},{3,2},{4,5},{5,4},{6,7},{7,6},{8,9},{9,8},{10,11... | collective-permute-start | bytes 49160 | tf_op jit(solution)/shard_map/ppermute | solution.py:137
  32.0 1.1 collective-permute-done.1
  33.2 6.8 %collective-permute-start.3 = (bf16[2,64,128]{2,1,0:T(8,128)(2,1)S(1)}, bf16[2,64,128]{2,1,0:T(8,128)(2,1)S(1)}, u32[]{:S(2)}, u32[]{:S(2)}) collective-permute-start(bf16[2,64,128]{2,1,0:T(8,128)(2,1)S(1)} %get-tuple-element.18), channel_id=1, source_target_pairs={{0,4},{2,6},{4,0},{6,2},{1,5},{3,7},{5,1},{7,3},{8,12},{10,14},{12... | collective-permute-start | bytes 98312 | tf_op jit(solution)/shard_map/ppermute | solution.py:137
  40.0 1.2 collective-permute-start.2
  41.2 2.4 %collective-permute-start.4 = (bf16[2,64,128]{2,1,0:T(8,128)(2,1)S(1)}, bf16[2,64,128]{2,1,0:T(8,128)(2,1)S(1)}, u32[]{:S(2)}, u32[]{:S(2)}) collective-permute-start(bf16[2,64,128]{2,1,0:T(8,128)(2,1)S(1)} %get-tuple-element.18), channel_id=1, source_target_pairs={{0,6},{2,0},{4,2},{6,4},{1,7},{3,1},{5,3},{7,5},{8,14},{10,8},{12,... | collective-permute-start | bytes 98312 | tf_op jit(solution)/shard_map/ppermute | solution.py:137
  43.6 4.3 %convolution_convert_fusion = bf16[4,512,512]{1,2,0:T(8,128)(2,1)} fusion(bf16[4,512,512]{2,1,0:T(8,128)(2,1)} %param.7, bf16[4,512,512]{2,1,0:T(8,128)(2,1)S(1)} %copy-done), kind=kOutput, calls=%fused_computation.4 | convolution fusion | flops 1074790400 | bytes 6291456 | tf_op jit(solution)/shard_map/snm,smp->snp/dot_general | solution.py:182
  47.8 0.0 collective-permute-done.3
  47.8 0.0 collective-permute-done.2
  47.8 0.0 collective-permute-done.4
  47.9 0.0 copy-start.5
  48.0 0.7 fusion.17
  48.7 0.9 copy-done.2
  49.6 7.0 %bitcast_subtract_fusion = f32[32,64,512]{2,1,0:T(8,128)S(1)} fusion(f32[32,64,512]{2,1,0:T(8,128)S(1)} %fusion.17, bf16[4,32,64,512]{3,2,1,0:T(8,128)(2,1)} %param.5, bf16[4,512,512]{1,2,0:T(8,128)(2,1)S(1)} %copy-done.2), kind=kOutput, calls=%fused_computation | convolution fusion | flops 4296015872 | bytes 18874368 | tf_op jit(solution)/shard_map/sgrn,snp->grp/dot_general | solution.py:202
  56.6 0.0 copy-start.6
  56.6 0.0 copy-start.7
  56.6 1.6 %constant_dynamic-slice_fusion.5 = f32[16,1,64,512]{3,2,1,0:T(8,128)} fusion(f32[16,2,64,512]{3,2,1,0:T(8,128)S(1)} %bitcast.68, s32[]{:T(128)S(6)} %select_n.142), kind=kLoop, calls=%fused_computation.40 | loop fusion | bytes 4194308 | tf_op jit(solution)/shard_map/dynamic_slice | solution.py:155
  58.2 1.0 copy-done.1
  59.1 2.4 %collective-permute-start.5 = (f32[16,1,64,512]{3,2,1,0:T(8,128)}, f32[16,1,64,512]{3,2,1,0:T(8,128)}, u32[]{:S(2)}, u32[]{:S(2)}) collective-permute-start(f32[16,1,64,512]{3,2,1,0:T(8,128)} %constant_dynamic-slice_fusion.5), channel_id=1, source_target_pairs={{0,8},{8,0},{1,9},{9,1},{2,10},{10,2},{3,11},{11,3},{4,12},{12,4},... | collective-permute-start | bytes 6291464 | tf_op jit(solution)/shard_map/ppermute | solution.py:129
  61.5 0.9 fusion.12
  62.4 1.4 %fusion.2 = f32[64,512]{1,0:T(8,128)S(1)} fusion(f32[64,512]{1,0:T(8,128)S(1)} %fusion.12, bf16[4,512,512]{2,1,0:T(8,128)(2,1)S(1)} %copy-done, bf16[4,512,512]{1,2,0:T(8,128)(2,1)} %convolution_convert_fusion, s32[]{:T(128)S(6)} %select_n.143, f32[64,512]{1,0:T(8,128)S(1)} %copy-done.7, pred[]{:T(512)S(6)} %eq.21), kind=kOutput, calls=%fused_computation.7 | convolution fusion | flops 134316032 | bytes 2752517 | tf_op jit(solution)/shard_map/snr,snp->rp/dot_general | solution.py:187
  63.9 0.1 collective-permute-start.6
  64.0 1.7 %collective-permute-done.6 = f32[32,512]{1,0:T(8,128)S(1)} collective-permute-done((f32[32,512]{1,0:T(8,128)S(1)}, f32[32,512]{1,0:T(8,128)S(1)}, u32[]{:S(2)}, u32[]{:S(2)}) %collective-permute-start.6) | collective-permute-done | bytes 65568 | tf_op jit(solution)/shard_map/ppermute | solution.py:129
  65.7 9.4 %all_to_all.21 = f32[16,8,128]{2,1,0:T(8,128)S(1)} all-to-all(f32[16,8,128]{2,1,0:T(8,128)S(1)} %bitcast.72), channel_id=1, replica_groups=mesh['scen_0'=4,'scen_1'=4,'scen_2'=2,'row'=4,'col'=2] {'scen_0','scen_1'}, dimensions={0} | all-to-all | bytes 131072 | tf_op jit(solution)/shard_map/all_to_all | solution.py:150
  75.1 0.8 collective-permute-start.7
  75.9 1.7 %collective-permute-done.7 = f32[8,128]{1,0:T(8,128)S(1)} collective-permute-done((f32[8,128]{1,0:T(8,128)S(1)}, f32[8,128]{1,0:T(8,128)S(1)}, u32[]{:S(2)}, u32[]{:S(2)}) %collective-permute-start.7) | collective-permute-done | bytes 4128 | tf_op jit(solution)/shard_map/ppermute | solution.py:137
  77.7 0.7 collective-permute-start.9
  78.4 2.9 %collective-permute-start.8 = (f32[2,8,128]{2,1,0:T(8,128)S(1)}, f32[2,8,128]{2,1,0:T(8,128)S(1)}, u32[]{:S(2)}, u32[]{:S(2)}) collective-permute-start(f32[2,8,128]{2,1,0:T(8,128)S(1)} %get-tuple-element.22), channel_id=1, source_target_pairs={{0,2},{2,4},{4,6},{6,0},{1,3},{3,5},{5,7},{7,1},{8,10},{10,12},{12... | collective-permute-start | bytes 24584 | tf_op jit(solution)/shard_map/ppermute | solution.py:137
  81.3 0.7 collective-permute-start.10
  82.0 2.2 %collective-permute-done.9 = f32[2,8,128]{2,1,0:T(8,128)S(1)} collective-permute-done((f32[2,8,128]{2,1,0:T(8,128)S(1)}, f32[2,8,128]{2,1,0:T(8,128)S(1)}, u32[]{:S(2)}, u32[]{:S(2)}) %collective-permute-start.9) | collective-permute-done | bytes 8224 | tf_op jit(solution)/shard_map/ppermute | solution.py:137
  84.2 0.0 collective-permute-done.8
  84.2 0.5 collective-permute-done.10
  84.7 0.8 broadcast_in_dim.8
  85.6 3.6 %all-to-all-start.3 = ((f32[16,8,8,128]{3,2,1,0:T(8,128)}), f32[16,8,8,128]{3,2,1,0:T(8,128)S(1)}, u32[]{:S(2)}, u32[]{:S(2)}) async-start(f32[16,8,8,128]{3,2,1,0:T(8,128)} %broadcast_in_dim.8), calls=%async_computation.3 | async-start | bytes 1048576 | tf_op jit(solution)/shard_map/all_to_all | solution.py:150
  89.2 3.6 %fusion.3 = bf16[16,64,512]{2,1,0:T(8,128)(2,1)} fusion(f32[16,1,64,512]{3,2,1,0:T(8,128)} %collective-permute-done.5, f32[16,2,64,512]{3,2,1,0:T(8,128)} %bitcast.69, s32[]{:T(128)S(6)} %select_n.141), kind=kLoop, calls=%fused_computation.8 | loop fusion | flops 1048576 | bytes 5242884 | tf_op jit(solution)/shard_map/convert_element_type | solution.py:208
  92.7 5.4 %all-to-all-done.3.own_ref = f32[16,8,8,128]{3,2,1,0:T(8,128)S(1)} async-done(((f32[16,8,8,128]{3,2,1,0:T(8,128)}), f32[16,8,8,128]{3,2,1,0:T(8,128)S(1)}, u32[]{:S(2)}, u32[]{:S(2)}) %all-to-all-start.3) | async-done | bytes 524320 | tf_op jit(solution)/shard_map/all_to_all | solution.py:150
  98.1 0.8 copy-done.4
  98.9 3.7 %all-to-all-start.1 = ((bf16[16,64,512]{2,1,0:T(8,128)(2,1)}), bf16[16,64,512]{2,1,0:T(8,128)(2,1)S(1)}, u32[]{:S(2)}, u32[]{:S(2)}) async-start(bf16[16,64,512]{2,1,0:T(8,128)(2,1)} %fusion.3), calls=%async_computation.1 | async-start | bytes 2097152 | tf_op jit(solution)/shard_map/all_to_all | solution.py:150
  102.6 6.0 %collective-permute-start.11 = (f32[16,8,8,128]{3,2,1,0:T(8,128)}, f32[16,8,8,128]{3,2,1,0:T(8,128)}, u32[]{:S(2)}, u32[]{:S(2)}) collective-permute-start(f32[16,8,8,128]{3,2,1,0:T(8,128)} %copy-done.4), channel_id=1, source_target_pairs={{0,8},{8,0},{1,9},{9,1},{2,10},{10,2},{3,11},{11,3},{4,12},{12,4},... | collective-permute-start | bytes 1572872 | tf_op jit(solution)/shard_map/ppermute | solution.py:129
  108.6 1.9 %collective-permute-done.11.other_ref = f32[16,8,8,128]{3,2,1,0:T(8,128)} collective-permute-done((f32[16,8,8,128]{3,2,1,0:T(8,128)}, f32[16,8,8,128]{3,2,1,0:T(8,128)}, u32[]{:S(2)}, u32[]{:S(2)}) %collective-permute-start.11) | collective-permute-done | bytes 524320 | tf_op jit(solution)/shard_map/ppermute | solution.py:129
  110.5 26.8 %inverse_factor.1 = f32[512,512]{1,0:T(8,128)} custom-call(s32[1]{0:T(128)} %bitcast.16.core_ref, f32[16,8,8,128]{3,2,1,0:T(8,128)} %copy-done.4, f32[16,8,8,128]{3,2,1,0:T(8,128)} %collective-permute-done.11.other_ref), custom_call_target="tpu_custom_call" | custom-call | flops 40000000 | bytes 2097152 | tf_op jit(solution)/shard_map/inverse_factor/pallas_call | solution.py:113
  137.3 0.1 convert_reduce_fusion
  137.4 3.0 %fusion.5 = f32[64,512]{1,0:T(8,128)} fusion(f32[512,512]{1,0:T(8,128)} %inverse_factor.1, f32[64,512]{1,0:T(8,128)S(1)} %copy-done.7, f32[64,512]{1,0:T(8,128)S(1)} %convert_reduce_fusion), kind=kOutput, calls=%fused_computation.17 | convolution fusion | flops 201359360 | bytes 1441792 | tf_op jit(solution)/shard_map/dot_general | solution.py:210
  (27 shorter events, 0.2 us)
Async XLA Ops:
  0.0 43.6 %copy-start = (bf16[4,512,512]{2,1,0:T(8,128)(2,1)S(1)}, bf16[4,512,512]{2,1,0:T(8,128)(2,1)}, u32[]{:S(2)}) copy-start(bf16[4,512,512]{2,1,0:T(8,128)(2,1)} %param.6) | copy-start | bytes 6291460
  1.1 7.5 %collective-permute-start = (bf16[64,2048]{1,0:T(8,128)(2,1)S(1)}, bf16[64,2048]{1,0:T(8,128)(2,1)S(1)}, u32[]{:S(2)}, u32[]{:S(2)}) collective-permute-start(bf16[64,2048]{1,0:T(8,128)(2,1)S(1)} %constant_dynamic-slice_fusion.10), channel_id=1, source_target_pairs={{0,1},{1,0},{2,3},{3,2},{4,5},{5,4},{6,7},{7,6},{8,9},{9,8},{10,11... | collective-permute-start | bytes 786440 | tf_op jit(solution)/shard_map/ppermute | solution.py:129
  30.5 17.4 %copy-start.3 = (bf16[32,64,128]{2,1,0:T(8,128)(2,1)}, bf16[32,64,128]{2,1,0:T(8,128)(2,1)S(1)}, u32[]{:S(2)}) copy-start(bf16[32,64,128]{2,1,0:T(8,128)(2,1)S(1)} %all_to_all.20) | copy-start | bytes 1572868
  30.5 2.6 %collective-permute-start.1 = (bf16[64,128]{1,0:T(8,128)(2,1)S(1)}, bf16[64,128]{1,0:T(8,128)(2,1)S(1)}, u32[]{:S(2)}, u32[]{:S(2)}) collective-permute-start(bf16[64,128]{1,0:T(8,128)(2,1)S(1)} %get-tuple-element.7), channel_id=1, source_target_pairs={{0,1},{1,0},{2,3},{3,2},{4,5},{5,4},{6,7},{7,6},{8,9},{9,8},{10,11... | collective-permute-start | bytes 49160 | tf_op jit(solution)/shard_map/ppermute | solution.py:137
  33.2 14.7 %collective-permute-start.3 = (bf16[2,64,128]{2,1,0:T(8,128)(2,1)S(1)}, bf16[2,64,128]{2,1,0:T(8,128)(2,1)S(1)}, u32[]{:S(2)}, u32[]{:S(2)}) collective-permute-start(bf16[2,64,128]{2,1,0:T(8,128)(2,1)S(1)} %get-tuple-element.18), channel_id=1, source_target_pairs={{0,4},{2,6},{4,0},{6,2},{1,5},{3,7},{5,1},{7,3},{8,12},{10,14},{12... | collective-permute-start | bytes 98312 | tf_op jit(solution)/shard_map/ppermute | solution.py:137
  40.0 7.9 %collective-permute-start.2 = (bf16[2,64,128]{2,1,0:T(8,128)(2,1)S(1)}, bf16[2,64,128]{2,1,0:T(8,128)(2,1)S(1)}, u32[]{:S(2)}, u32[]{:S(2)}) collective-permute-start(bf16[2,64,128]{2,1,0:T(8,128)(2,1)S(1)} %get-tuple-element.18), channel_id=1, source_target_pairs={{0,2},{2,4},{4,6},{6,0},{1,3},{3,5},{5,7},{7,1},{8,10},{10,12},{12... | collective-permute-start | bytes 98312 | tf_op jit(solution)/shard_map/ppermute | solution.py:137
  41.2 6.7 %collective-permute-start.4 = (bf16[2,64,128]{2,1,0:T(8,128)(2,1)S(1)}, bf16[2,64,128]{2,1,0:T(8,128)(2,1)S(1)}, u32[]{:S(2)}, u32[]{:S(2)}) collective-permute-start(bf16[2,64,128]{2,1,0:T(8,128)(2,1)S(1)} %get-tuple-element.18), channel_id=1, source_target_pairs={{0,6},{2,0},{4,2},{6,4},{1,7},{3,1},{5,3},{7,5},{8,14},{10,8},{12,... | collective-permute-start | bytes 98312 | tf_op jit(solution)/shard_map/ppermute | solution.py:137
  47.9 0.7 copy-start.5
  48.0 1.6 %copy-start.2 = (bf16[4,512,512]{1,2,0:T(8,128)(2,1)S(1)}, bf16[4,512,512]{1,2,0:T(8,128)(2,1)}, u32[]{:S(2)}) copy-start(bf16[4,512,512]{1,2,0:T(8,128)(2,1)} %convolution_convert_fusion) | copy-start | bytes 6291460
  56.6 2.6 %copy-start.1 = (f32[32,64,512]{2,1,0:T(8,128)}, f32[32,64,512]{2,1,0:T(8,128)S(1)}, u32[]{:S(2)}) copy-start(f32[32,64,512]{2,1,0:T(8,128)S(1)} %bitcast_subtract_fusion) | copy-start | bytes 12582916
  56.6 5.0 %copy-start.6 = (bf16[4,2,64,128]{3,2,1,0:T(8,128)(2,1)S(1)}, bf16[4,2,64,128]{3,2,1,0:T(8,128)(2,1)}, u32[]{:S(2)}) copy-start(bf16[4,2,64,128]{3,2,1,0:T(8,128)(2,1)} %copy-done.5) | copy-start | bytes 393220
  56.6 5.8 %copy-start.7 = (f32[64,512]{1,0:T(8,128)S(1)}, f32[64,512]{1,0:T(8,128)}, u32[]{:S(2)}) copy-start(f32[64,512]{1,0:T(8,128)} %param.9) | copy-start | bytes 393220
  59.1 30.0 %collective-permute-start.5 = (f32[16,1,64,512]{3,2,1,0:T(8,128)}, f32[16,1,64,512]{3,2,1,0:T(8,128)}, u32[]{:S(2)}, u32[]{:S(2)}) collective-permute-start(f32[16,1,64,512]{3,2,1,0:T(8,128)} %constant_dynamic-slice_fusion.5), channel_id=1, source_target_pairs={{0,8},{8,0},{1,9},{9,1},{2,10},{10,2},{3,11},{11,3},{4,12},{12,4},... | collective-permute-start | bytes 6291464 | tf_op jit(solution)/shard_map/ppermute | solution.py:129
  63.9 1.8 %collective-permute-start.6 = (f32[32,512]{1,0:T(8,128)S(1)}, f32[32,512]{1,0:T(8,128)S(1)}, u32[]{:S(2)}, u32[]{:S(2)}) collective-permute-start(f32[32,512]{1,0:T(8,128)S(1)} %constant_dynamic-slice_fusion.4), channel_id=1, source_target_pairs={{0,8},{8,0},{1,9},{9,1},{2,10},{10,2},{3,11},{11,3},{4,12},{12,4},... | collective-permute-start | bytes 196616 | tf_op jit(solution)/shard_map/ppermute | solution.py:129
  75.1 2.5 %collective-permute-start.7 = (f32[8,128]{1,0:T(8,128)S(1)}, f32[8,128]{1,0:T(8,128)S(1)}, u32[]{:S(2)}, u32[]{:S(2)}) collective-permute-start(f32[8,128]{1,0:T(8,128)S(1)} %reduce_sum.19), channel_id=1, source_target_pairs={{0,1},{1,0},{2,3},{3,2},{4,5},{5,4},{6,7},{7,6},{8,9},{9,8},{10,11... | collective-permute-start | bytes 12296 | tf_op jit(solution)/shard_map/ppermute | solution.py:137
  77.7 6.5 %collective-permute-start.9 = (f32[2,8,128]{2,1,0:T(8,128)S(1)}, f32[2,8,128]{2,1,0:T(8,128)S(1)}, u32[]{:S(2)}, u32[]{:S(2)}) collective-permute-start(f32[2,8,128]{2,1,0:T(8,128)S(1)} %get-tuple-element.22), channel_id=1, source_target_pairs={{0,4},{2,6},{4,0},{6,2},{1,5},{3,7},{5,1},{7,3},{8,12},{10,14},{12... | collective-permute-start | bytes 24584 | tf_op jit(solution)/shard_map/ppermute | solution.py:137
  78.4 5.8 %collective-permute-start.8 = (f32[2,8,128]{2,1,0:T(8,128)S(1)}, f32[2,8,128]{2,1,0:T(8,128)S(1)}, u32[]{:S(2)}, u32[]{:S(2)}) collective-permute-start(f32[2,8,128]{2,1,0:T(8,128)S(1)} %get-tuple-element.22), channel_id=1, source_target_pairs={{0,2},{2,4},{4,6},{6,0},{1,3},{3,5},{5,7},{7,1},{8,10},{10,12},{12... | collective-permute-start | bytes 24584 | tf_op jit(solution)/shard_map/ppermute | solution.py:137
  81.3 3.4 %collective-permute-start.10 = (f32[2,8,128]{2,1,0:T(8,128)S(1)}, f32[2,8,128]{2,1,0:T(8,128)S(1)}, u32[]{:S(2)}, u32[]{:S(2)}) collective-permute-start(f32[2,8,128]{2,1,0:T(8,128)S(1)} %get-tuple-element.22), channel_id=1, source_target_pairs={{0,6},{2,0},{4,2},{6,4},{1,7},{3,1},{5,3},{7,5},{8,14},{10,8},{12,... | collective-permute-start | bytes 24584 | tf_op jit(solution)/shard_map/ppermute | solution.py:137
  85.6 12.5 %all-to-all-start.3 = ((f32[16,8,8,128]{3,2,1,0:T(8,128)}), f32[16,8,8,128]{3,2,1,0:T(8,128)S(1)}, u32[]{:S(2)}, u32[]{:S(2)}) async-start(f32[16,8,8,128]{3,2,1,0:T(8,128)} %broadcast_in_dim.8), calls=%async_computation.3 | async-start | bytes 1048576 | tf_op jit(solution)/shard_map/all_to_all | solution.py:150
  98.1 0.8 copy-start.4
  98.9 38.3 %all-to-all-start.1 = ((bf16[16,64,512]{2,1,0:T(8,128)(2,1)}), bf16[16,64,512]{2,1,0:T(8,128)(2,1)S(1)}, u32[]{:S(2)}, u32[]{:S(2)}) async-start(bf16[16,64,512]{2,1,0:T(8,128)(2,1)} %fusion.3), calls=%async_computation.1 | async-start | bytes 2097152 | tf_op jit(solution)/shard_map/all_to_all | solution.py:150
  102.6 7.9 %collective-permute-start.11 = (f32[16,8,8,128]{3,2,1,0:T(8,128)}, f32[16,8,8,128]{3,2,1,0:T(8,128)}, u32[]{:S(2)}, u32[]{:S(2)}) collective-permute-start(f32[16,8,8,128]{3,2,1,0:T(8,128)} %copy-done.4), channel_id=1, source_target_pairs={{0,8},{8,0},{1,9},{9,1},{2,10},{10,2},{3,11},{11,3},{4,12},{12,4},... | collective-permute-start | bytes 1572872 | tf_op jit(solution)/shard_map/ppermute | solution.py:129

commit v2 on v1

--- a/solution.py
+++ b/solution.py
@@ -1,5 +1,6 @@
 import jax
 import jax.numpy as jnp
+import numpy as np
 from jax import lax
 from jax.experimental import pallas as pl
 from jax.experimental.pallas import tpu as pltpu
@@ -73,20 +74,15 @@
     return lax.dot_general(a, b, (dims, ((), ())), precision=lax.Precision.HIGHEST, preferred_element_type=F32)
 
 
-def inverse_kernel(core_ref, own_ref, other_ref, w_ref, s_ref, d_ref):
+def inverse_kernel(place_ref, own_ref, other_ref, w_ref, s_ref, d_ref):
     n = w_ref.shape[0]
     blocks = n // BLOCK
-    planes = own_ref.shape[1]
-    half = n // planes // 2
-    own = pl.multiple_of(core_ref[0] * half, half)
-    other = pl.multiple_of(half - core_ref[0] * half, half)
-    for piece in range(own_ref.shape[0]):
-        down, across = divmod(piece, n // BLOCK)
-        for plane in range(planes):
-            at = plane * 2 * half + down * 8
-            lanes = slice(across * BLOCK, (across + 1) * BLOCK)
-            s_ref[pl.ds(own + at, 8), lanes] = own_ref[piece, plane]
-            s_ref[pl.ds(other + at, 8), lanes] = other_ref[piece, plane]
+    planes, half = own_ref.shape[0], own_ref.shape[1]
+    for piece in range(planes):
+        own = pl.multiple_of(place_ref[0, piece], half)
+        other = pl.multiple_of(place_ref[1, piece], half)
+        s_ref[pl.ds(own, half), :] = own_ref[piece]
+        s_ref[pl.ds(other, half), :] = other_ref[piece]
     for k in range(blocks):
         lo, hi = k * BLOCK, (k + 1) * BLOCK
         done = factor_block([s_ref[lo + 8 * g : lo + 8 * g + 8, lo:hi] for g in range(BLOCK // 8)])
@@ -109,7 +105,8 @@
                 w_ref[il:ih, lo:hi] = -new[:, lo:hi]
 
 
-def inverse_factor(core, own, other, n):
+def inverse_factor(place, own, other):
+    n = own.shape[-1]
     return pl.pallas_call(
         inverse_kernel,
         out_shape=jax.ShapeDtypeStruct((n, n), F32),
@@ -122,7 +119,7 @@
         scratch_shapes=[pltpu.VMEM((n, n), F32), pltpu.VMEM((BLOCK, BLOCK), F32)],
         cost_estimate=pl.CostEstimate(flops=40_000_000, bytes_accessed=2 * n * n * 4, transcendentals=n),
         name="inverse_factor",
-    )(core, own, other)
+    )(place, own, other)
 
 
 def swapped(value, axis):
@@ -137,7 +134,9 @@
         pieces.append(lax.ppermute(value, axis, [(i, (i + step) % peers) for i in range(peers)]))
     pieces = jnp.stack(pieces)
     return jnp.stack(
-        [lax.dynamic_index_in_dim(pieces, (place - q) % peers, 0, keepdims=False) for q in range(peers)]
+        [lax.dynamic_index_in_dim(
+                pieces, lax.rem(place + (peers - q), peers), 0, keepdims=False
+            ) for q in range(peers)]
     )
 
 
@@ -146,66 +145,108 @@
     return pieces.reshape(-1, *value.shape)
 
 
+def shifts(value, axis):
+    peers = lax.axis_size(axis)
+    return [value] + [
+        lax.ppermute(value, axis, [(i, (i + step) % peers) for i in range(peers)])
+        for step in range(1, peers)
+    ]
+
+
+def plane_pieces(value):
+    pairs = jnp.stack([value, swapped(value, "col")])
+    return jnp.concatenate(shifts(pairs, "row"))
+
+
+def piece_places(core, rows):
+    peers = lax.axis_size("row")
+    piece = np.arange(2 * peers)
+    row = lax.rem(lax.axis_index("row") + (peers - piece // 2), peers)
+    col = lax.rem(lax.axis_index("col") + piece % 2, 2)
+    side = lax.rem(core + np.arange(2), 2)
+    return ((row * 2 + col) * rows)[None, :] + (side * (rows // 2))[:, None]
+
+
 def exchanged(pieces, axis):
     return lax.all_to_all(pieces, axis, 0, 0, tiled=True)
 
 
-def half_of(value, dim, which, parts=2):
-    size = value.shape[dim] // parts
+def half_of(value, dim, which):
+    size = value.shape[dim] // 2
     return lax.dynamic_slice_in_dim(value, which * size, size, dim)
 
 
-def factor_slices(factor):
-    col = lax.axis_index("col")
-    chips = lax.axis_size(SCEN) // 2
-    mine = half_of(factor, 0, col)
-    theirs = swapped(half_of(factor, 0, 1 - col), "col")
-    mine, theirs = (
-        jnp.moveaxis(v.reshape(v.shape[0], chips, -1), 1, 0) for v in (mine, theirs)
-    )
-    first = jnp.where(col == 0, mine, theirs)
-    second = jnp.where(col == 0, theirs, mine)
-    return exchanged(jnp.concatenate([first, second]), SCEN)
+def pack_kernel(row_ref, factor_ref, theirs_ref, out_ref):
+    rows, width = out_ref.shape[2], out_ref.shape[3]
+    start = pl.multiple_of(row_ref[0], rows)
+    for q in range(out_ref.shape[0]):
+        lanes = slice(q * width, (q + 1) * width)
+        out_ref[q, 0] = factor_ref[pl.ds(start, rows), lanes]
+        out_ref[q, 1] = theirs_ref[:, lanes]
+
+
+def packed(row, factor, theirs, parts):
+    rows, columns = theirs.shape
+    vmem = pl.BlockSpec(memory_space=pltpu.VMEM)
+    return pl.pallas_call(
+        pack_kernel,
+        out_shape=jax.ShapeDtypeStruct((parts, 2, rows, columns // parts), factor.dtype),
+        in_specs=[pl.BlockSpec(memory_space=pltpu.SMEM), vmem, vmem],
+        out_specs=vmem,
+        cost_estimate=pl.CostEstimate(flops=1_000_000, bytes_accessed=4 * rows * columns * 2, transcendentals=0),
+        name="packed",
+    )(row, factor, theirs)
+
+
+def ordered(first, second, flip):
+    return jnp.where(flip == 0, first, second), jnp.where(flip == 0, second, first)
 
 
 def per_device(border, panel_border, kinv, factor, root_block):
     core = lax.axis_index(CORE)
     scen = lax.axis_index(SCEN)
+    col = lax.axis_index("col")
     plane = lax.axis_index(("row", "col"))
     chips = lax.axis_size(CHIPS)
     groups, rows, n = border.shape[1], border.shape[2], border.shape[3]
-
-    slices = factor_slices(factor)
-    leading = all_planes(slices[0])
-    leading = leading.reshape(-1, leading.shape[-1])
-
+    width = panel_border.shape[2]
+
+    theirs = swapped(half_of(factor, 0, 1 - col), "col")
     solved = jnp.einsum(
         "snm,smp->snp", kinv, panel_border, preferred_element_type=F32
     ).astype(BF16)
+    theirs, solved = lax.optimization_barrier((theirs, solved))
+    slices = packed((col * rows).astype(jnp.int32).reshape(1), factor, theirs, chips)
+    slices = exchanged(slices, CHIPS)
+    coupling = jnp.einsum("sgrn,snp->grp", border, solved, preferred_element_type=F32)
+    coupling = coupling.reshape(chips, 2, rows, width)
+    slices, coupling = lax.optimization_barrier((slices, coupling))
+    bulk = half_of(coupling, 1, core)[:, 0] + swapped(half_of(coupling, 1, 1 - core)[:, 0], CORE)
+
+    keep, send = ordered(slices[0, 0], slices[0, 1], col)
+    head = jnp.where(core == 0, keep, lax.ppermute(send, CORE, [(0, 1)]))
+    leading = all_planes(head).reshape(-1, head.shape[-1])
 
     own_solved = lax.dynamic_slice_in_dim(solved, plane * rows, rows, 2)
     panel = jnp.einsum("snr,snp->rp", own_solved, panel_border, preferred_element_type=F32)
+    panel = panel + jnp.where(scen == 0, root_block, 0.0)
     panel = panel - lax.dot_general(
-        slices[0], leading, (((1,), (1,)), ((), ())), preferred_element_type=F32
-    )
-    panel = panel + jnp.where(scen == 0, root_block, 0.0)
+        head, leading, (((1,), (1,)), ((), ())), preferred_element_type=F32
+    )
     panel = half_of(panel, 0, core) + swapped(half_of(panel, 0, 1 - core), CORE)
-    width = panel.shape[1]
-    tiles = panel.reshape(panel.shape[0] // 8, 8, width // BLOCK, BLOCK)
-    tiles = tiles.transpose(0, 2, 1, 3).reshape(-1, 8, BLOCK)
-    tile = jnp.sum(exchanged(tiles, CHIPS), axis=0)
-    tile = all_planes(tile)
-    own = exchanged(jnp.broadcast_to(tile, (chips, *tile.shape)), CHIPS)
+    panel = sum(shifts(panel, "scen_1"))
+    panel = sum(shifts(panel, "scen_0"))
+    own = plane_pieces(panel)
     other = swapped(own, CORE)
-    inverse = inverse_factor(core.astype(jnp.int32).reshape(1), own, other, width)
-
-    coupling = jnp.einsum("sgrn,snp->grp", border, solved, preferred_element_type=F32)
-    update = lax.dot_general(
-        slices, leading, (((2,), (1,)), ((), ())), preferred_element_type=F32
-    )
-    partial = (coupling - update).reshape(chips, 2, rows, width)
-    mine = half_of(partial, 1, core)[:, 0] + swapped(half_of(partial, 1, 1 - core), CORE)[:, 0]
-    pieces = exchanged(mine.astype(BF16), CHIPS)
+    inverse = inverse_factor(piece_places(core, rows), own, other)
+
+    leads = ordered(leading, swapped(leading, CORE), core)
+    leads = ordered(*leads, col)
+    for slot in range(2):
+        bulk = bulk - lax.dot_general(
+            slices[:, slot], leads[slot], (((2,), (1,)), ((), ())), preferred_element_type=F32
+        )
+    pieces = exchanged(bulk.astype(BF16), CHIPS)
     schur = root_block + jnp.sum(pieces.astype(F32), axis=0)
     return lax.dot_general(
         schur, inverse, (((1,), (1,)), ((), ())),

time: 141 us -> 129 us (0.915)
  blocking collectives: 30 us -> 0 us
  starting transfers between devices: 35.2 us -> 49.4 us
  matrix products: 17.2 us -> 23.8 us
  waiting for transfers between devices: 19.5 us -> 14.5 us
  local copies, waits for them, and re-layouts: 6.43 us -> 10.4 us
  other arithmetic: 4.94 us -> 1.56 us
  Pallas kernels: 26.8 us -> 28.7 us
    all_to_all x2 -> x0, blocking collectives: 30 us -> none  [exchanged(): return lax.all_to_all(pieces, axis, 0, 0, tiled=True)]
    ppermute x0 -> x10, starting transfers between devices: none -> 14.6 us  [the longest x9 13.3 us: shifts(): lax.ppermute(value, axis, [(i, (i + step) % peers) for i in range(peers)])]
    ppermute x0 -> x10, waiting for transfers between devices: none -> 10.1 us  [the longest x9 7.46 us: shifts(): lax.ppermute(value, axis, [(i, (i + step) % peers) for i in range(peers)])]
    ppermute x8 -> x4, starting transfers between devices: 17 us -> 11.1 us  [gathered(): lax.ppermute(value, axis, [(i, (i + step) % peers) for i in range(peers)])]
    ppermute x8 -> x4, waiting for transfers between devices: 5.6 us -> 0.01 us  [gathered(): lax.ppermute(value, axis, [(i, (i + step) % peers) for i in range(peers)])]
    all_to_all x2, waiting for transfers between devices: 5.41 us -> 0.01 us  [exchanged(): return lax.all_to_all(pieces, axis, 0, 0, tiled=True)]
    all_to_all x2, starting transfers between devices: 7.22 us -> 11.5 us  [exchanged(): return lax.all_to_all(pieces, axis, 0, 0, tiled=True)]
    ppermute x4 -> x6, waiting for transfers between devices: 8.54 us -> 4.46 us  [swapped(): return lax.ppermute(value, axis, [(0, 1), (1, 0)])]
  transfers between devices with their start and end apart: 14 -> 22, of which waited for: 8 -> 10; matrix products, arithmetic and copies ran while one was open for 8% -> 24% of each run, Pallas kernels for 19% -> 21%
where the time goes in v2:
time: 129 us
  starting transfers between devices  49.4 us (38%)
  Pallas kernels  28.7 us (22%)
  matrix products  23.8 us (18%)
  waiting for transfers between devices  14.5 us (11%)
  local copies, waits for them, and re-layouts  10.4 us (8%)
  other arithmetic  1.56 us (1%)
    pallas_call x1, Pallas kernels, inverse_factor(): pl.pallas_call(inverse_kernel, out_shape=jax.ShapeDtypeStruct((n, n), F32...  26.7 us
    ppermute x9, starting transfers between devices, shifts(): lax.ppermute(value, axis, [(i, (i + step) % peers) for i in range(peers)])  13.3 us
    ppermute x6, starting transfers between devices, swapped(): return lax.ppermute(value, axis, [(0, 1), (1, 0)])  12.3 us
    all_to_all x2, starting transfers between devices, exchanged(): return lax.all_to_all(pieces, axis, 0, 0, tiled=True)  11.5 us
    ppermute x4, starting transfers between devices, gathered(): lax.ppermute(value, axis, [(i, (i + step) % peers) for i in range(peers)])  11.1 us
    dot_general x1, matrix products, per_device(): jnp.einsum('sgrn,snp->grp', border, solved, preferred_element_type=F32)  10.5 us
    ppermute x9, waiting for transfers between devices, shifts(): lax.ppermute(value, axis, [(i, (i + step) % peers) for i in range(peers)])  7.46 us
    unnamed x13, local copies, waits for them, and re-layouts  4.49 us
  transfers between devices with their start and end apart: 22, of which 10 were waited for; matrix products, arithmetic and copies ran while one was open for 24% of the time, Pallas kernels for 21%

profile of v2, /device:TPU:1, one launch (start us, length us, event | category | flops | bytes accessed | tf_op | source)
XLA Modules:
  0.0 128.6 jit_solution(4775364099705181638)
XLA Ops:
  0.0 1.1 constant_dynamic-slice_fusion.5
  1.1 2.5 %collective-permute-start = (bf16[64,2048]{1,0:T(8,128)(2,1)S(1)}, bf16[64,2048]{1,0:T(8,128)(2,1)S(1)}, u32[]{:S(2)}, u32[]{:S(2)}) collective-permute-start(bf16[64,2048]{1,0:T(8,128)(2,1)S(1)} %constant_dynamic-slice_fusion.5), channel_id=1, source_target_pairs={{0,1},{1,0},{2,3},{3,2},{4,5},{5,4},{6,7},{7,6},{8,9},{9,8},{10,11... | collective-permute-start | bytes 786440 | tf_op jit(solution)/shard_map/ppermute | solution.py:126
  3.7 4.2 %convolution_convert_fusion = bf16[4,512,512]{2,1,0:T(8,128)(2,1)} fusion(bf16[4,512,512]{2,1,0:T(8,128)(2,1)} %param.10, bf16[4,512,512]{2,1,0:T(8,128)(2,1)S(1)} %copy-done), kind=kOutput, calls=%fused_computation.8 | convolution fusion | flops 1074790400 | bytes 6291456 | tf_op jit(solution)/shard_map/snm,smp->snp/dot_general | solution.py:215
  7.9 0.7 collective-permute-done.theirs_ref
  8.7 0.7 copy-done.2
  9.4 2.0 %packed.1 = bf16[16,2,64,128]{3,2,1,0:T(8,128)(2,1)} custom-call(s32[1]{0:T(128)} %bitcast.row_ref, bf16[128,2048]{1,0:T(8,128)(2,1)} %factor_ref.1, bf16[64,2048]{1,0:T(8,128)(2,1)} %copy-done.2), custom_call_target="tpu_custom_call" | custom-call | flops 1000000 | bytes 1048576 | tf_op jit(solution)/shard_map/packed/pallas_call | solution.py:191
  11.4 7.7 %all-to-all-start = ((bf16[16,2,64,128]{3,2,1,0:T(8,128)(2,1)}), bf16[16,2,64,128]{3,2,1,0:T(8,128)(2,1)S(1)}, u32[]{:S(2)}, u32[]{:S(2)}) async-start(bf16[16,2,64,128]{3,2,1,0:T(8,128)(2,1)} %packed.1), calls=%async_computation | async-start | bytes 1048576 | tf_op jit(solution)/shard_map/all_to_all | solution.py:171
  19.1 10.5 %fusion = f32[512,32,64,1]{0,2,1,3:T(8,128)} fusion(bf16[4,32,64,512]{3,2,1,0:T(8,128)(2,1)} %param.8, bf16[4,512,512]{2,1,0:T(8,128)(2,1)} %convolution_convert_fusion), kind=kOutput, calls=%fused_computation | convolution fusion | flops 4294967296 | bytes 14680064 | tf_op jit(solution)/shard_map/sgrn,snp->grp/dot_general | solution.py:221
  29.6 1.3 %collective-permute-start.2 = (bf16[64,128]{1,0:T(8,128)(2,1)S(1)}, bf16[64,128]{1,0:T(8,128)(2,1)S(1)}, u32[]{:S(2)}, u32[]{:S(2)}) collective-permute-start(bf16[64,128]{1,0:T(8,128)(2,1)S(1)} %select_bitcast_fusion), channel_id=1, source_target_pairs={{0,8},{1,9},{2,10},{3,11},{4,12},{5,13},{6,14},{7,15},{16,24},{17,... | collective-permute-start | bytes 49160 | tf_op jit(solution)/shard_map/ppermute | solution.py:227
  30.9 2.6 %collective-permute-done.2 = bf16[64,128]{1,0:T(8,128)(2,1)S(1)} collective-permute-done((bf16[64,128]{1,0:T(8,128)(2,1)S(1)}, bf16[64,128]{1,0:T(8,128)(2,1)S(1)}, u32[]{:S(2)}, u32[]{:S(2)}) %collective-permute-start.2) | collective-permute-done | bytes 16416 | tf_op jit(solution)/shard_map/ppermute | solution.py:227
  33.5 1.4 %collective-permute-start.3 = (bf16[64,128]{1,0:T(8,128)(2,1)S(1)}, bf16[64,128]{1,0:T(8,128)(2,1)S(1)}, u32[]{:S(2)}, u32[]{:S(2)}) collective-permute-start(bf16[64,128]{1,0:T(8,128)(2,1)S(1)} %bitcast_select_fusion), channel_id=1, source_target_pairs={{0,1},{1,0},{2,3},{3,2},{4,5},{5,4},{6,7},{7,6},{8,9},{9,8},{10,11... | collective-permute-start | bytes 49160 | tf_op jit(solution)/shard_map/ppermute | solution.py:134
  34.9 3.2 %dynamic-slice_bitcast_fusion = f32[16,64,512]{2,1,0:T(8,128)} fusion(f32[16,2,64,512]{3,2,1,0:T(8,128)} %bitcast.65, s32[]{:T(128)S(6)} %select_n.94), kind=kLoop, calls=%fused_computation.7 | loop fusion | bytes 4194308 | tf_op jit(solution)/shard_map/squeeze | solution.py:224
  38.1 0.4 collective-permute-start.1
  38.6 6.1 %collective-permute-start.5 = (bf16[2,64,128]{2,1,0:T(8,128)(2,1)S(1)}, bf16[2,64,128]{2,1,0:T(8,128)(2,1)S(1)}, u32[]{:S(2)}, u32[]{:S(2)}) collective-permute-start(bf16[2,64,128]{2,1,0:T(8,128)(2,1)S(1)} %get-tuple-element.20), channel_id=1, source_target_pairs={{0,4},{2,6},{4,0},{6,2},{1,5},{3,7},{5,1},{7,3},{8,12},{10,14},{12... | collective-permute-start | bytes 98312 | tf_op jit(solution)/shard_map/ppermute | solution.py:134
  44.7 1.2 collective-permute-start.4
  45.9 2.4 %collective-permute-start.6 = (bf16[2,64,128]{2,1,0:T(8,128)(2,1)S(1)}, bf16[2,64,128]{2,1,0:T(8,128)(2,1)S(1)}, u32[]{:S(2)}, u32[]{:S(2)}) collective-permute-start(bf16[2,64,128]{2,1,0:T(8,128)(2,1)S(1)} %get-tuple-element.20), channel_id=1, source_target_pairs={{0,6},{2,0},{4,2},{6,4},{1,7},{3,1},{5,3},{7,5},{8,14},{10,8},{12,... | collective-permute-start | bytes 98312 | tf_op jit(solution)/shard_map/ppermute | solution.py:134
  48.3 1.7 %fusion.5 = f32[64,512]{1,0:T(8,128)S(1)} fusion(bf16[4,512,512]{2,1,0:T(8,128)(2,1)S(1)} %copy-done, bf16[4,512,512]{2,1,0:T(8,128)(2,1)} %convolution_convert_fusion, s32[]{:T(128)S(6)} %select_n.114, f32[64,512]{1,0:T(8,128)S(1)} %copy-done.1, pred[]{:T(512)S(6)} %eq.16), kind=kOutput, calls=%fused_computation.11 | convolution fusion | flops 134283264 | bytes 2883589 | tf_op jit(solution)/shard_map/snr,snp->rp/dot_general | solution.py:231
  50.3 1.4 %collective-permute-start.8 = (f32[32,512]{1,0:T(8,128)S(1)}, f32[32,512]{1,0:T(8,128)S(1)}, u32[]{:S(2)}, u32[]{:S(2)}) collective-permute-start(f32[32,512]{1,0:T(8,128)S(1)} %constant_dynamic-slice_fusion), channel_id=1, source_target_pairs={{0,8},{8,0},{1,9},{9,1},{2,10},{10,2},{3,11},{11,3},{4,12},{12,4},... | collective-permute-start | bytes 196616 | tf_op jit(solution)/shard_map/ppermute | solution.py:126
  51.7 0.9 collective-permute-done.8
  52.6 2.7 %collective-permute-start.11 = (f32[32,512]{1,0:T(8,128)S(1)}, f32[32,512]{1,0:T(8,128)S(1)}, u32[]{:S(2)}, u32[]{:S(2)}) collective-permute-start(f32[32,512]{1,0:T(8,128)S(1)} %dynamic-slice_add_fusion), channel_id=1, source_target_pairs={{0,48},{16,0},{32,16},{48,32},{1,49},{17,1},{33,17},{49,33},{2,50}... | collective-permute-start | bytes 196616 | tf_op jit(solution)/shard_map/ppermute | solution.py:151
  55.3 0.6 collective-permute-start.10
  55.9 0.6 collective-permute-start.9
  56.7 3.3 %collective-permute-done.10 = f32[32,512]{1,0:T(8,128)S(1)} collective-permute-done((f32[32,512]{1,0:T(8,128)S(1)}, f32[32,512]{1,0:T(8,128)S(1)}, u32[]{:S(2)}, u32[]{:S(2)}) %collective-permute-start.10) | collective-permute-done | bytes 65568 | tf_op jit(solution)/shard_map/ppermute | solution.py:151
  60.0 1.7 %collective-permute-done.9 = f32[32,512]{1,0:T(8,128)S(1)} collective-permute-done((f32[32,512]{1,0:T(8,128)S(1)}, f32[32,512]{1,0:T(8,128)S(1)}, u32[]{:S(2)}, u32[]{:S(2)}) %collective-permute-start.9) | collective-permute-done | bytes 65568 | tf_op jit(solution)/shard_map/ppermute | solution.py:151
  61.7 2.5 %collective-permute-start.14 = (f32[32,512]{1,0:T(8,128)S(1)}, f32[32,512]{1,0:T(8,128)S(1)}, u32[]{:S(2)}, u32[]{:S(2)}) collective-permute-start(f32[32,512]{1,0:T(8,128)S(1)} %add_add_fusion.1), channel_id=1, source_target_pairs={{0,192},{64,0},{128,64},{192,128},{1,193},{65,1},{129,65},{193,129... | collective-permute-start | bytes 196616 | tf_op jit(solution)/shard_map/ppermute | solution.py:151
  64.2 0.6 collective-permute-start.13
  64.8 0.6 collective-permute-start.12
  65.3 1.9 %collective-permute-start.7 = (bf16[512,128]{1,0:T(8,128)(2,1)S(1)}, bf16[512,128]{1,0:T(8,128)(2,1)S(1)}, u32[]{:S(2)}, u32[]{:S(2)}) collective-permute-start(bf16[512,128]{1,0:T(8,128)(2,1)S(1)} %bitcast.68), channel_id=1, source_target_pairs={{0,8},{8,0},{1,9},{9,1},{2,10},{10,2},{3,11},{11,3},{4,12},{12,4},... | collective-permute-start | bytes 393224 | tf_op jit(solution)/shard_map/ppermute | solution.py:126
  67.3 1.6 %collective-permute-done.13 = f32[32,512]{1,0:T(8,128)S(1)} collective-permute-done((f32[32,512]{1,0:T(8,128)S(1)}, f32[32,512]{1,0:T(8,128)S(1)}, u32[]{:S(2)}, u32[]{:S(2)}) %collective-permute-start.13) | collective-permute-done | bytes 65568 | tf_op jit(solution)/shard_map/ppermute | solution.py:151
  68.9 0.7 collective-permute-done.12
  69.5 0.6 constant_dynamic-update-slice_fusion.4
  70.2 1.1 collective-permute-start.15
  71.2 0.4 fusion.11
  71.7 1.6 %collective-permute-done.15 = f32[32,512]{1,0:T(8,128)S(1)} collective-permute-done((f32[32,512]{1,0:T(8,128)S(1)}, f32[32,512]{1,0:T(8,128)S(1)}, u32[]{:S(2)}, u32[]{:S(2)}) %collective-permute-start.15) | collective-permute-done | bytes 65568 | tf_op jit(solution)/shard_map/ppermute | solution.py:126
  73.3 3.7 %collective-permute-start.18 = (f32[2,32,512]{2,1,0:T(8,128)S(1)}, f32[2,32,512]{2,1,0:T(8,128)}, u32[]{:S(2)}, u32[]{:S(2)}) collective-permute-start(f32[2,32,512]{2,1,0:T(8,128)S(1)} %pad_maximum_fusion.2), channel_id=1, source_target_pairs={{0,6},{2,0},{4,2},{6,4},{1,7},{3,1},{5,3},{7,5},{8,14},{10,8},{12,... | collective-permute-start | bytes 393224 | tf_op jit(solution)/shard_map/ppermute | solution.py:151
  76.9 0.7 collective-permute-start.17
  77.7 1.4 %collective-permute-start.16 = (f32[2,32,512]{2,1,0:T(8,128)S(1)}, f32[2,32,512]{2,1,0:T(8,128)}, u32[]{:S(2)}, u32[]{:S(2)}) collective-permute-start(f32[2,32,512]{2,1,0:T(8,128)S(1)} %pad_maximum_fusion.2), channel_id=1, source_target_pairs={{0,2},{2,4},{4,6},{6,0},{1,3},{3,5},{5,7},{7,1},{8,10},{10,12},{12... | collective-permute-start | bytes 393224 | tf_op jit(solution)/shard_map/ppermute | solution.py:151
  79.1 3.7 %fusion.4 = bf16[16,64,512]{2,1,0:T(8,128)(2,1)} fusion(f32[16,64,512]{2,1,0:T(8,128)S(1)} %fusion.11, f32[16,64,512]{2,1,0:T(8,128)} %collective-permute-done.1, f32[16,2,64,512]{3,2,1,0:T(8,128)} %bitcast.66, s32[]{:T(128)S(6)} %select_n.93, bf16[16,2,64,128]{3,2,1,0:T(8,128)(2,1)S(1)} %all-to-all-done, pred[]{:T(512)S(6)} %eq.6, ...), kind=kOutput, calls=%fused_computation.5 | convolution fusion | flops 136511488 | bytes 7864326 | tf_op jit(solution)/shard_map/dot_general | solution.py:246
  82.9 3.8 %all-to-all-start.1 = ((bf16[16,64,512]{2,1,0:T(8,128)(2,1)}), bf16[16,64,512]{2,1,0:T(8,128)(2,1)S(1)}, u32[]{:S(2)}, u32[]{:S(2)}) async-start(bf16[16,64,512]{2,1,0:T(8,128)(2,1)} %fusion.4), calls=%async_computation.1 | async-start | bytes 2097152 | tf_op jit(solution)/shard_map/all_to_all | solution.py:171
  86.7 0.6 constant_dynamic-update-slice_fusion.3
  87.3 1.6 %constant_dynamic-update-slice_fusion.2 = f32[8,32,512]{2,1,0:T(8,128)} fusion(f32[8,32,512]{2,1,0:T(8,128)} %constant_dynamic-update-slice_fusion.3, f32[2,32,512]{2,1,0:T(8,128)} %collective-permute-done.16), kind=kLoop, calls=%fused_computation.46 | loop fusion | bytes 262144
  88.9 1.6 %constant_dynamic-update-slice_fusion.1 = f32[8,32,512]{2,1,0:T(8,128)} fusion(f32[8,32,512]{2,1,0:T(8,128)} %constant_dynamic-update-slice_fusion.2, f32[2,32,512]{2,1,0:T(8,128)} %collective-permute-done.17), kind=kLoop, calls=%fused_computation.45 | loop fusion | bytes 262144
  90.4 1.6 %constant_dynamic-update-slice_fusion.own_ref = f32[8,32,512]{2,1,0:T(8,128)} fusion(f32[8,32,512]{2,1,0:T(8,128)} %constant_dynamic-update-slice_fusion.1, f32[2,32,512]{2,1,0:T(8,128)} %collective-permute-done.18), kind=kLoop, calls=%fused_computation.44 | loop fusion | bytes 262144 | tf_op jit(solution)/shard_map/concatenate | solution.py:158
  92.0 4.9 %collective-permute-start.19 = (f32[8,32,512]{2,1,0:T(8,128)}, f32[8,32,512]{2,1,0:T(8,128)}, u32[]{:S(2)}, u32[]{:S(2)}) collective-permute-start(f32[8,32,512]{2,1,0:T(8,128)} %constant_dynamic-update-slice_fusion.own_ref), channel_id=1, source_target_pairs={{0,8},{8,0},{1,9},{9,1},{2,10},{10,2},{3,11},{11,3},{4,12},{12,4},... | collective-permute-start | bytes 1572872 | tf_op jit(solution)/shard_map/ppermute | solution.py:126
  97.0 0.6 broadcast_add_fusion.place_ref
  97.6 1.2 collective-permute-done.19.other_ref
  98.8 26.7 %inverse_factor.1 = f32[512,512]{1,0:T(8,128)} custom-call(s32[2,8]{1,0:T(2,128)} %broadcast_add_fusion.place_ref, f32[8,32,512]{2,1,0:T(8,128)} %constant_dynamic-update-slice_fusion.own_ref, f32[8,32,512]{2,1,0:T(8,128)} %collective-permute-done.19.other_ref), custom_call_target="tpu_custom_call" | custom-call | flops 40000000 | bytes 2097152 | tf_op jit(solution)/shard_map/inverse_factor/pallas_call | solution.py:110
  125.7 3.0 %fusion.17 = f32[64,512]{1,0:T(8,128)} fusion(f32[512,512]{1,0:T(8,128)} %inverse_factor.1, f32[64,512]{1,0:T(8,128)S(1)} %copy-done.1, f32[64,512]{1,0:T(8,128)S(1)} %convert_reduce_fusion), kind=kOutput, calls=%fused_computation.24 | convolution fusion | flops 201359360 | bytes 1441792 | tf_op jit(solution)/shard_map/dot_general | solution.py:251
  (37 shorter events, 0.7 us)
Async XLA Ops:
  0.0 3.7 %copy-start = (bf16[4,512,512]{2,1,0:T(8,128)(2,1)S(1)}, bf16[4,512,512]{2,1,0:T(8,128)(2,1)}, u32[]{:S(2)}) copy-start(bf16[4,512,512]{2,1,0:T(8,128)(2,1)} %param.9) | copy-start | bytes 6291460
  1.1 7.5 %collective-permute-start = (bf16[64,2048]{1,0:T(8,128)(2,1)S(1)}, bf16[64,2048]{1,0:T(8,128)(2,1)S(1)}, u32[]{:S(2)}, u32[]{:S(2)}) collective-permute-start(bf16[64,2048]{1,0:T(8,128)(2,1)S(1)} %constant_dynamic-slice_fusion.5), channel_id=1, source_target_pairs={{0,1},{1,0},{2,3},{3,2},{4,5},{5,4},{6,7},{7,6},{8,9},{9,8},{10,11... | collective-permute-start | bytes 786440 | tf_op jit(solution)/shard_map/ppermute | solution.py:126
  8.7 0.7 copy-start.2
  11.4 18.2 %all-to-all-start = ((bf16[16,2,64,128]{3,2,1,0:T(8,128)(2,1)}), bf16[16,2,64,128]{3,2,1,0:T(8,128)(2,1)S(1)}, u32[]{:S(2)}, u32[]{:S(2)}) async-start(bf16[16,2,64,128]{3,2,1,0:T(8,128)(2,1)} %packed.1), calls=%async_computation | async-start | bytes 1048576 | tf_op jit(solution)/shard_map/all_to_all | solution.py:171
  29.6 4.0 %collective-permute-start.2 = (bf16[64,128]{1,0:T(8,128)(2,1)S(1)}, bf16[64,128]{1,0:T(8,128)(2,1)S(1)}, u32[]{:S(2)}, u32[]{:S(2)}) collective-permute-start(bf16[64,128]{1,0:T(8,128)(2,1)S(1)} %select_bitcast_fusion), channel_id=1, source_target_pairs={{0,8},{1,9},{2,10},{3,11},{4,12},{5,13},{6,14},{7,15},{16,24},{17,... | collective-permute-start | bytes 49160 | tf_op jit(solution)/shard_map/ppermute | solution.py:227
  33.5 14.8 %copy-start.1 = (f32[64,512]{1,0:T(8,128)S(1)}, f32[64,512]{1,0:T(8,128)}, u32[]{:S(2)}) copy-start(f32[64,512]{1,0:T(8,128)} %param.12) | copy-start | bytes 393220
  33.5 5.1 %collective-permute-start.3 = (bf16[64,128]{1,0:T(8,128)(2,1)S(1)}, bf16[64,128]{1,0:T(8,128)(2,1)S(1)}, u32[]{:S(2)}, u32[]{:S(2)}) collective-permute-start(bf16[64,128]{1,0:T(8,128)(2,1)S(1)} %bitcast_select_fusion), channel_id=1, source_target_pairs={{0,1},{1,0},{2,3},{3,2},{4,5},{5,4},{6,7},{7,6},{8,9},{9,8},{10,11... | collective-permute-start | bytes 49160 | tf_op jit(solution)/shard_map/ppermute | solution.py:134
  38.1 41.0 %collective-permute-start.1 = (f32[16,64,512]{2,1,0:T(8,128)}, f32[16,64,512]{2,1,0:T(8,128)}, u32[]{:S(2)}, u32[]{:S(2)}) collective-permute-start(f32[16,64,512]{2,1,0:T(8,128)} %dynamic-slice_bitcast_fusion), channel_id=1, source_target_pairs={{0,8},{8,0},{1,9},{9,1},{2,10},{10,2},{3,11},{11,3},{4,12},{12,4},... | collective-permute-start | bytes 6291464 | tf_op jit(solution)/shard_map/ppermute | solution.py:126
  38.6 11.4 %collective-permute-start.5 = (bf16[2,64,128]{2,1,0:T(8,128)(2,1)S(1)}, bf16[2,64,128]{2,1,0:T(8,128)(2,1)S(1)}, u32[]{:S(2)}, u32[]{:S(2)}) collective-permute-start(bf16[2,64,128]{2,1,0:T(8,128)(2,1)S(1)} %get-tuple-element.20), channel_id=1, source_target_pairs={{0,4},{2,6},{4,0},{6,2},{1,5},{3,7},{5,1},{7,3},{8,12},{10,14},{12... | collective-permute-start | bytes 98312 | tf_op jit(solution)/shard_map/ppermute | solution.py:134
  44.7 5.3 %collective-permute-start.4 = (bf16[2,64,128]{2,1,0:T(8,128)(2,1)S(1)}, bf16[2,64,128]{2,1,0:T(8,128)(2,1)S(1)}, u32[]{:S(2)}, u32[]{:S(2)}) collective-permute-start(bf16[2,64,128]{2,1,0:T(8,128)(2,1)S(1)} %get-tuple-element.20), channel_id=1, source_target_pairs={{0,2},{2,4},{4,6},{6,0},{1,3},{3,5},{5,7},{7,1},{8,10},{10,12},{12... | collective-permute-start | bytes 98312 | tf_op jit(solution)/shard_map/ppermute | solution.py:134
  45.9 4.1 %collective-permute-start.6 = (bf16[2,64,128]{2,1,0:T(8,128)(2,1)S(1)}, bf16[2,64,128]{2,1,0:T(8,128)(2,1)S(1)}, u32[]{:S(2)}, u32[]{:S(2)}) collective-permute-start(bf16[2,64,128]{2,1,0:T(8,128)(2,1)S(1)} %get-tuple-element.20), channel_id=1, source_target_pairs={{0,6},{2,0},{4,2},{6,4},{1,7},{3,1},{5,3},{7,5},{8,14},{10,8},{12,... | collective-permute-start | bytes 98312 | tf_op jit(solution)/shard_map/ppermute | solution.py:134
  50.3 2.3 %collective-permute-start.8 = (f32[32,512]{1,0:T(8,128)S(1)}, f32[32,512]{1,0:T(8,128)S(1)}, u32[]{:S(2)}, u32[]{:S(2)}) collective-permute-start(f32[32,512]{1,0:T(8,128)S(1)} %constant_dynamic-slice_fusion), channel_id=1, source_target_pairs={{0,8},{8,0},{1,9},{9,1},{2,10},{10,2},{3,11},{11,3},{4,12},{12,4},... | collective-permute-start | bytes 196616 | tf_op jit(solution)/shard_map/ppermute | solution.py:126
  52.6 4.0 %collective-permute-start.11 = (f32[32,512]{1,0:T(8,128)S(1)}, f32[32,512]{1,0:T(8,128)S(1)}, u32[]{:S(2)}, u32[]{:S(2)}) collective-permute-start(f32[32,512]{1,0:T(8,128)S(1)} %dynamic-slice_add_fusion), channel_id=1, source_target_pairs={{0,48},{16,0},{32,16},{48,32},{1,49},{17,1},{33,17},{49,33},{2,50}... | collective-permute-start | bytes 196616 | tf_op jit(solution)/shard_map/ppermute | solution.py:151
  55.3 4.7 %collective-permute-start.10 = (f32[32,512]{1,0:T(8,128)S(1)}, f32[32,512]{1,0:T(8,128)S(1)}, u32[]{:S(2)}, u32[]{:S(2)}) collective-permute-start(f32[32,512]{1,0:T(8,128)S(1)} %dynamic-slice_add_fusion), channel_id=1, source_target_pairs={{0,32},{16,48},{32,0},{48,16},{1,33},{17,49},{33,1},{49,17},{2,34}... | collective-permute-start | bytes 196616 | tf_op jit(solution)/shard_map/ppermute | solution.py:151
  55.9 5.8 %collective-permute-start.9 = (f32[32,512]{1,0:T(8,128)S(1)}, f32[32,512]{1,0:T(8,128)S(1)}, u32[]{:S(2)}, u32[]{:S(2)}) collective-permute-start(f32[32,512]{1,0:T(8,128)S(1)} %dynamic-slice_add_fusion), channel_id=1, source_target_pairs={{0,16},{16,32},{32,48},{48,0},{1,17},{17,33},{33,49},{49,1},{2,18}... | collective-permute-start | bytes 196616 | tf_op jit(solution)/shard_map/ppermute | solution.py:151
  61.7 5.5 %collective-permute-start.14 = (f32[32,512]{1,0:T(8,128)S(1)}, f32[32,512]{1,0:T(8,128)S(1)}, u32[]{:S(2)}, u32[]{:S(2)}) collective-permute-start(f32[32,512]{1,0:T(8,128)S(1)} %add_add_fusion.1), channel_id=1, source_target_pairs={{0,192},{64,0},{128,64},{192,128},{1,193},{65,1},{129,65},{193,129... | collective-permute-start | bytes 196616 | tf_op jit(solution)/shard_map/ppermute | solution.py:151
  64.2 4.7 %collective-permute-start.13 = (f32[32,512]{1,0:T(8,128)S(1)}, f32[32,512]{1,0:T(8,128)S(1)}, u32[]{:S(2)}, u32[]{:S(2)}) collective-permute-start(f32[32,512]{1,0:T(8,128)S(1)} %add_add_fusion.1), channel_id=1, source_target_pairs={{0,128},{64,192},{128,0},{192,64},{1,129},{65,193},{129,1},{193,65... | collective-permute-start | bytes 196616 | tf_op jit(solution)/shard_map/ppermute | solution.py:151
  64.8 4.8 %collective-permute-start.12 = (f32[32,512]{1,0:T(8,128)S(1)}, f32[32,512]{1,0:T(8,128)S(1)}, u32[]{:S(2)}, u32[]{:S(2)}) collective-permute-start(f32[32,512]{1,0:T(8,128)S(1)} %add_add_fusion.1), channel_id=1, source_target_pairs={{0,64},{64,128},{128,192},{192,0},{1,65},{65,129},{129,193},{193,1... | collective-permute-start | bytes 196616 | tf_op jit(solution)/shard_map/ppermute | solution.py:151
  65.3 5.9 %collective-permute-start.7 = (bf16[512,128]{1,0:T(8,128)(2,1)S(1)}, bf16[512,128]{1,0:T(8,128)(2,1)S(1)}, u32[]{:S(2)}, u32[]{:S(2)}) collective-permute-start(bf16[512,128]{1,0:T(8,128)(2,1)S(1)} %bitcast.68), channel_id=1, source_target_pairs={{0,8},{8,0},{1,9},{9,1},{2,10},{10,2},{3,11},{11,3},{4,12},{12,4},... | collective-permute-start | bytes 393224 | tf_op jit(solution)/shard_map/ppermute | solution.py:126
  70.2 3.1 %collective-permute-start.15 = (f32[32,512]{1,0:T(8,128)S(1)}, f32[32,512]{1,0:T(8,128)S(1)}, u32[]{:S(2)}, u32[]{:S(2)}) collective-permute-start(f32[32,512]{1,0:T(8,128)S(1)} %get-tuple-element.14), channel_id=1, source_target_pairs={{0,1},{1,0},{2,3},{3,2},{4,5},{5,4},{6,7},{7,6},{8,9},{9,8},{10,11... | collective-permute-start | bytes 196616 | tf_op jit(solution)/shard_map/ppermute | solution.py:126
  73.3 17.1 %collective-permute-start.18 = (f32[2,32,512]{2,1,0:T(8,128)S(1)}, f32[2,32,512]{2,1,0:T(8,128)}, u32[]{:S(2)}, u32[]{:S(2)}) collective-permute-start(f32[2,32,512]{2,1,0:T(8,128)S(1)} %pad_maximum_fusion.2), channel_id=1, source_target_pairs={{0,6},{2,0},{4,2},{6,4},{1,7},{3,1},{5,3},{7,5},{8,14},{10,8},{12,... | collective-permute-start | bytes 393224 | tf_op jit(solution)/shard_map/ppermute | solution.py:151
  76.9 11.9 %collective-permute-start.17 = (f32[2,32,512]{2,1,0:T(8,128)S(1)}, f32[2,32,512]{2,1,0:T(8,128)}, u32[]{:S(2)}, u32[]{:S(2)}) collective-permute-start(f32[2,32,512]{2,1,0:T(8,128)S(1)} %pad_maximum_fusion.2), channel_id=1, source_target_pairs={{0,4},{2,6},{4,0},{6,2},{1,5},{3,7},{5,1},{7,3},{8,12},{10,14},{12... | collective-permute-start | bytes 393224 | tf_op jit(solution)/shard_map/ppermute | solution.py:151
  77.7 9.6 %collective-permute-start.16 = (f32[2,32,512]{2,1,0:T(8,128)S(1)}, f32[2,32,512]{2,1,0:T(8,128)}, u32[]{:S(2)}, u32[]{:S(2)}) collective-permute-start(f32[2,32,512]{2,1,0:T(8,128)S(1)} %pad_maximum_fusion.2), channel_id=1, source_target_pairs={{0,2},{2,4},{4,6},{6,0},{1,3},{3,5},{5,7},{7,1},{8,10},{10,12},{12... | collective-permute-start | bytes 393224 | tf_op jit(solution)/shard_map/ppermute | solution.py:151
  82.9 14.1 %copy-start.3 = (s32[8]{0:T(128)S(1)}, s32[8]{0:T(128)}, u32[]{:S(2)}) copy-start(s32[8]{0:T(128)} %constant.88.clone) | copy-start | bytes 100
  82.9 14.1 %copy-start.4 = (s32[8]{0:T(128)S(1)}, s32[8]{0:T(128)}, u32[]{:S(2)}) copy-start(s32[8]{0:T(128)} %constant.87.clone) | copy-start | bytes 100
  82.9 42.6 %all-to-all-start.1 = ((bf16[16,64,512]{2,1,0:T(8,128)(2,1)}), bf16[16,64,512]{2,1,0:T(8,128)(2,1)S(1)}, u32[]{:S(2)}, u32[]{:S(2)}) async-start(bf16[16,64,512]{2,1,0:T(8,128)(2,1)} %fusion.4), calls=%async_computation.1 | async-start | bytes 2097152 | tf_op jit(solution)/shard_map/all_to_all | solution.py:171
  92.0 6.8 %collective-permute-start.19 = (f32[8,32,512]{2,1,0:T(8,128)}, f32[8,32,512]{2,1,0:T(8,128)}, u32[]{:S(2)}, u32[]{:S(2)}) collective-permute-start(f32[8,32,512]{2,1,0:T(8,128)} %constant_dynamic-update-slice_fusion.own_ref), channel_id=1, source_target_pairs={{0,8},{8,0},{1,9},{9,1},{2,10},{10,2},{3,11},{11,3},{4,12},{12,4},... | collective-permute-start | bytes 1572872 | tf_op jit(solution)/shard_map/ppermute | solution.py:126

commit v3 on v2

v3 whole, which is shorter than its diff:
```python
import jax
import jax.numpy as jnp
import numpy as np
from jax import lax
from jax.experimental import pallas as pl
from jax.experimental.pallas import tpu as pltpu
from jax.sharding import Mesh
from jax.sharding import PartitionSpec as P

CHIPS = ("scen_0", "scen_1")
CORE = "scen_2"
SCEN = ("scen_0", "scen_1", "scen_2")
SCEN_ROW = ("scen_0", "scen_1", "scen_2", "row")
SCEN_ROW_COL = ("scen_0", "scen_1", "scen_2", "row", "col")
BF16 = jnp.bfloat16

BLOCK = 128
F32 = jnp.float32


def spread_row(value, row):
    return jnp.broadcast_to(value[row : row + 1, :], value.shape)


def spread_lane(value, lane):
    return jnp.broadcast_to(value[:, lane : lane + 1], value.shape)


def factor_block(rows):
    groups = len(rows)
    tile = rows[0].shape
    sub = lax.broadcasted_iota(jnp.int32, tile, 0)
    lane = lax.broadcasted_iota(jnp.int32, tile, 1)
    inverse = [jnp.where(lane == sub + 8 * g, 1.0, 0.0).astype(F32) for g in range(groups)]
    rows = list(rows)
    done = []
    for t in range(groups):
        cols = [spread_lane(rows[t], 8 * t + j) for j in range(8)]
        left, right = rows[t], inverse[t]
        ahead = inverse[t]
        scale = jnp.zeros(tile, F32)
        square = jnp.zeros(tile, F32)
        for k in range(8):
            root = lax.rsqrt(spread_row(cols[k], k))
            recip = root * root
            scale = jnp.where(sub == k, root, scale)
            square = jnp.where(sub == k, recip, square)
            full = jnp.where(sub == k, 0.0, cols[k] * recip)
            below = jnp.where(sub > k, full, 0.0)
            for j in range(k + 1, 8):
                cols[j] = cols[j] - full * spread_row(cols[j], k)
            left = left - full * spread_row(left, k)
            right = right - full * spread_row(right, k)
            ahead = ahead - below * spread_row(ahead, k)
        done.append(ahead * scale)
        if t == groups - 1:
            break
        left, right = left * square, right * square
        lefts = [spread_row(left, j) for j in range(8)]
        rights = [spread_row(right, j) for j in range(8)]
        for g in range(t + 1, groups):
            coef = [spread_lane(rows[g], 8 * t + j) for j in range(8)]
            a = [coef[j] * lefts[j] for j in range(8)]
            b = [coef[j] * rights[j] for j in range(8)]
            while len(a) > 1:
                a = [a[i] + a[i + 1] for i in range(0, len(a), 2)]
                b = [b[i] + b[i + 1] for i in range(0, len(b), 2)]
            rows[g] = rows[g] - a[0]
            inverse[g] = inverse[g] - b[0]
    return done


def split(value):
    high = value.astype(BF16)
    return high, (value - high.astype(F32)).astype(BF16)


def dot(a, b, dims=((1,), (0,))):
    (ah, al), (bh, bl) = split(a), split(b)
    terms = [
        lax.dot_general(x, y, (dims, ((), ())), preferred_element_type=F32)
        for x, y in ((al, bh), (ah, bl), (ah, bh))
    ]
    return terms[0] + terms[1] + terms[2]


TILES = tuple((i, j) for i in range(4) for j in range(i, 4))


def tile_rows(i, j):
    at = TILES.index((i, j)) * BLOCK
    return slice(at, at + BLOCK)


def inverse_kernel(place_ref, *refs):
    part_refs, (w_ref, s_ref, d_ref) = refs[:-3], refs[-3:]
    n = w_ref.shape[0]
    blocks = n // BLOCK
    count = place_ref.shape[0] // len(part_refs)
    size = part_refs[0].shape[0] // count
    for p, part in enumerate(part_refs):
        for q in range(count):
            at = pl.multiple_of(place_ref[p * count + q], 8)
            s_ref[pl.ds(at, size), :] = part[q * size : (q + 1) * size, :]

    def finish(k):
        lo, hi = k * BLOCK, (k + 1) * BLOCK
        w = d_ref[...]
        if k > 0:
            w_ref[lo:hi, 0:lo] = dot(w, w_ref[lo:hi, 0:lo])
        w_ref[lo:hi, lo:hi] = w
        if hi == n:
            return
        w_ref[lo:hi, hi:n] = jnp.zeros((BLOCK, n - hi), F32)
        u = dot(w, jnp.concatenate([s_ref[tile_rows(k, j), :] for j in range(k + 1, blocks)], axis=1))
        for i in range(k + 1, blocks):
            il, ih = i * BLOCK, (i + 1) * BLOCK
            ui = u[:, il - hi : ih - hi]
            drop = dot(ui, u[:, il - hi :], ((0,), (0,)))
            for j in range(i, blocks):
                cut = (j - i) * BLOCK
                s_ref[tile_rows(i, j), :] = s_ref[tile_rows(i, j), :] - drop[:, cut : cut + BLOCK]
            new = dot(ui, w_ref[lo:hi, 0:hi], ((0,), (0,)))
            if k > 0:
                w_ref[il:ih, 0:lo] = w_ref[il:ih, 0:lo] - new[:, 0:lo]
            w_ref[il:ih, lo:hi] = -new[:, lo:hi]

    def step(k, carry):
        own = (k * blocks - k * (k - 1) // 2) * BLOCK
        done = factor_block(
            [s_ref[pl.ds(pl.multiple_of(own + 8 * g, 8), 8), :] for g in range(BLOCK // 8)]
        )
        for g in range(BLOCK // 8):
            d_ref[8 * g : 8 * g + 8, :] = done[g]
        for static in range(blocks):
            pl.when(k == static)(lambda static=static: finish(static))
        return carry

    lax.fori_loop(0, blocks, step, 0)


def inverse_factor(place, parts, n):
    vmem = pl.BlockSpec(memory_space=pltpu.VMEM)
    return pl.pallas_call(
        inverse_kernel,
        out_shape=jax.ShapeDtypeStruct((n, n), F32),
        in_specs=[pl.BlockSpec(memory_space=pltpu.SMEM)] + [vmem] * len(parts),
        out_specs=vmem,
        scratch_shapes=[
            pltpu.VMEM((len(TILES) * BLOCK, BLOCK), F32),
            pltpu.VMEM((BLOCK, BLOCK), F32),
        ],
        cost_estimate=pl.CostEstimate(flops=40_000_000, bytes_accessed=2 * n * n * 4, transcendentals=n),
        compiler_params=pltpu.CompilerParams(vmem_limit_bytes=12 * 2**20),
        name="inverse_factor",
    )(place, *parts)


def panel_kernel(place_ref, gram_ref, *refs):
    parts = (len(refs) - 4) // 2
    lead_parts, root_parts = refs[:parts], refs[parts : 2 * parts]
    mine_ref, theirs_ref, lead_ref, root_ref = refs[2 * parts :]
    rows = lead_parts[0].shape[1]
    for p in range(parts):
        for q in range(2):
            at = pl.multiple_of(place_ref[2 * p + q], rows)
            lead_ref[pl.ds(at, rows), :] = lead_parts[p][q]
            root_ref[pl.ds(at, rows), :] = root_parts[p][q]
    core = place_ref[2 * parts]
    half = len(TILES) // 2
    for b, (i, j) in enumerate(TILES):
        top, side = slice(i * BLOCK, (i + 1) * BLOCK), slice(j * BLOCK, (j + 1) * BLOCK)
        square = lax.dot_general(
            lead_ref[top, :], lead_ref[side, :], (((1,), (1,)), ((), ())), preferred_element_type=F32
        )
        value = root_ref[top, side] + gram_ref[top, side] - square
        keep = core == b // half
        at = slice(b % half * BLOCK, (b % half + 1) * BLOCK)

        @pl.when(keep)
        def _():
            mine_ref[at, :] = value

        @pl.when(jnp.logical_not(keep))
        def _():
            theirs_ref[at, :] = value


def panel_halves(place, gram, leads, roots):
    vmem = pl.BlockSpec(memory_space=pltpu.VMEM)
    n = gram.shape[0]
    half = jax.ShapeDtypeStruct((len(TILES) // 2 * BLOCK, BLOCK), F32)
    return pl.pallas_call(
        panel_kernel,
        out_shape=(half, half, jax.ShapeDtypeStruct((n, leads[0].shape[-1]), BF16)),
        in_specs=[pl.BlockSpec(memory_space=pltpu.SMEM)] + [vmem] * (1 + len(leads) + len(roots)),
        out_specs=(vmem, vmem, vmem),
        scratch_shapes=[pltpu.VMEM((n, n), F32)],
        cost_estimate=pl.CostEstimate(flops=2_000_000, bytes_accessed=4 * n * n * 4, transcendentals=0),
        compiler_params=pltpu.CompilerParams(vmem_limit_bytes=12 * 2**20),
        name="panel_halves",
    )(place, gram, *leads, *roots)


def coupling_kernel(core_ref, border_ref, solved_ref, sent_ref, kept_ref):
    scens, step, _, rows, n = border_ref.shape
    left = jnp.concatenate([border_ref[s, :, 0].reshape(step * rows, n) for s in range(scens)], axis=1)
    right = solved_ref[...].reshape(scens * n, solved_ref.shape[-1])
    total = jnp.dot(left, right, preferred_element_type=F32).reshape(sent_ref.shape)
    first = pl.program_id(0) < pl.num_programs(0) // 2

    @pl.when(first)
    def _():
        sent_ref[...] = total

    @pl.when(jnp.logical_not(first))
    def _():
        kept_ref[...] = total


def coupling_halves(core, border, solved, step=8):
    scens, chips, _, rows, n = border.shape
    width = solved.shape[-1]
    steps = chips // step
    half = jax.ShapeDtypeStruct((chips, rows, width), F32)
    grid_spec = pltpu.PrefetchScalarGridSpec(
        num_scalar_prefetch=1,
        grid=(2 * steps,),
        in_specs=[
            pl.BlockSpec(
                (scens, step, 1, rows, n),
                lambda t, c: (0, lax.rem(t, steps), lax.rem(c[0] + 1 + t // steps, 2), 0, 0),
            ),
            pl.BlockSpec((scens, n, width), lambda t, c: (0, 0, 0)),
        ],
        out_specs=[
            pl.BlockSpec((step, rows, width), lambda t, c: (jnp.minimum(t, steps - 1), 0, 0)),
            pl.BlockSpec((step, rows, width), lambda t, c: (jnp.maximum(t - steps, 0), 0, 0)),
        ],
    )
    return pl.pallas_call(
        coupling_kernel,
        out_shape=(half, half),
        grid_spec=grid_spec,
        compiler_params=pltpu.CompilerParams(dimension_semantics=("arbitrary",)),
        cost_estimate=pl.CostEstimate(
            flops=4 * scens * chips * rows * n * width,
            bytes_accessed=2 * scens * chips * rows * n * 2 + 2 * chips * rows * width * 4,
            transcendentals=0,
        ),
        name="coupling_halves",
    )(core, border, solved)


def swapped(value, axis):
    return lax.ppermute(value, axis, [(0, 1), (1, 0)])


def shifts(value, axis):
    peers = lax.axis_size(axis)
    return [value] + [
        lax.ppermute(value, axis, [(i, (i + step) % peers) for i in range(peers)])
        for step in range(1, peers)
    ]


def plane_parts(value):
    return shifts(jnp.stack([value, swapped(value, "col")]), "row")


def plane_parts_of_first(value):
    rows = lax.axis_size("row")
    pairs = jnp.stack([value, lax.ppermute(value, (*SCEN, "col"), [(0, 1), (1, 0)])])
    return [pairs] + [
        lax.ppermute(pairs, (*SCEN, "row"), [(i, (i + step) % rows) for i in range(rows)])
        for step in range(1, rows)
    ]


def part_places(rows):
    peers = lax.axis_size("row")
    part = np.arange(2 * peers)
    row = lax.rem(lax.axis_index("row") + (peers - part // 2), peers)
    col = lax.rem(lax.axis_index("col") + part % 2, 2)
    return (row * 2 + col) * rows


def piece_places(core, size):
    across, down = lax.axis_size("scen_1"), lax.axis_size("scen_0")
    piece = np.arange(2 * across * down)
    side = lax.rem(core + piece // (across * down), 2)
    x = lax.rem(lax.axis_index("scen_1") + (across - piece // down % across), across)
    y = lax.rem(lax.axis_index("scen_0") + (down - piece % down), down)
    return ((side * across + x) * down + y) * size


def scattered_sum(value, axis):
    peers = lax.axis_size(axis)
    place = lax.axis_index(axis)
    size = value.shape[0] // peers
    total = lax.dynamic_slice_in_dim(value, place * size, size, 0)
    for step in range(1, peers):
        piece = lax.dynamic_slice_in_dim(value, lax.rem(place + step, peers) * size, size, 0)
        total = total + lax.ppermute(piece, axis, [(i, (i + step) % peers) for i in range(peers)])
    return total


def exchanged(pieces, axis):
    return lax.all_to_all(pieces, axis, 0, 0, tiled=True)


def half_of(value, dim, which):
    size = value.shape[dim] // 2
    return lax.dynamic_slice_in_dim(value, which * size, size, dim)


def pack_kernel(row_ref, factor_ref, theirs_ref, out_ref):
    rows, width = out_ref.shape[2], out_ref.shape[3]
    start = pl.multiple_of(row_ref[0], rows)
    for q in range(out_ref.shape[0]):
        lanes = slice(q * width, (q + 1) * width)
        out_ref[q, 0] = factor_ref[pl.ds(start, rows), lanes]
        out_ref[q, 1] = theirs_ref[:, lanes]


def packed(row, factor, theirs, parts):
    rows, columns = theirs.shape
    vmem = pl.BlockSpec(memory_space=pltpu.VMEM)
    return pl.pallas_call(
        pack_kernel,
        out_shape=jax.ShapeDtypeStruct((parts, 2, rows, columns // parts), factor.dtype),
        in_specs=[pl.BlockSpec(memory_space=pltpu.SMEM), vmem, vmem],
        out_specs=vmem,
        cost_estimate=pl.CostEstimate(flops=1_000_000, bytes_accessed=4 * rows * columns * 2, transcendentals=0),
        compiler_params=pltpu.CompilerParams(vmem_limit_bytes=12 * 2**20),
        name="packed",
    )(row, factor, theirs)


def ordered(first, second, flip):
    return jnp.where(flip == 0, first, second), jnp.where(flip == 0, second, first)


def per_device(border, panel_border, kinv, factor, root_block):
    core = lax.axis_index(CORE).astype(jnp.int32)
    scen = lax.axis_index(SCEN)
    col = lax.axis_index("col")
    chips = lax.axis_size(CHIPS)
    rows = border.shape[2]
    width = panel_border.shape[2]

    theirs = swapped(half_of(factor, 0, 1 - col), "col")
    roots = plane_parts_of_first(jnp.where(scen == 0, root_block, 0.0))
    solved = jnp.einsum(
        "snm,smp->snp", kinv, panel_border, preferred_element_type=F32
    ).astype(BF16)
    theirs, solved = lax.optimization_barrier((theirs, solved))
    slices = packed((col * rows).astype(jnp.int32).reshape(1), factor, theirs, chips)
    slices = exchanged(slices, CHIPS)
    halves = border.reshape(border.shape[0], chips, 2, rows, border.shape[3])
    sent, kept = coupling_halves(core.reshape(1), halves, solved)
    gram = jnp.einsum("snr,snp->rp", solved, panel_border, preferred_element_type=F32)
    slices, sent, kept, gram, roots = lax.optimization_barrier((slices, sent, kept, gram, roots))
    bulk = kept + swapped(sent, CORE)

    keep, send = ordered(slices[0, 0], slices[0, 1], col)
    head = jnp.where(core == 0, keep, lax.ppermute(send, CORE, [(0, 1)]))
    place = jnp.concatenate([part_places(rows).astype(jnp.int32), core.reshape(1)])
    mine, theirs, leading = panel_halves(place, gram, plane_parts(head), roots)
    piece = mine + swapped(theirs, CORE)
    piece = scattered_sum(piece, "scen_1")
    piece = scattered_sum(piece, "scen_0")
    place = piece_places(core, piece.shape[0]).astype(jnp.int32)
    own = shifts(jnp.concatenate(shifts(piece, "scen_0")), "scen_1")
    inverse = inverse_factor(place, own + [swapped(part, CORE) for part in own], width)

    leads = ordered(leading, swapped(leading, CORE), core)
    leads = ordered(*leads, col)
    for slot in range(2):
        bulk = bulk - lax.dot_general(
            slices[:, slot], leads[slot], (((2,), (1,)), ((), ())), preferred_element_type=F32
        )
    pieces = exchanged(bulk.astype(BF16), CHIPS)
    schur = root_block + jnp.sum(pieces.astype(F32), axis=0)
    return lax.dot_general(
        schur, inverse, (((1,), (1,)), ((), ())),
        precision=lax.Precision.HIGH, preferred_element_type=F32,
    )


def solution(mesh):
    split = Mesh(
        mesh.devices.reshape(4, 4, 2, mesh.shape["row"], mesh.shape["col"]),
        ("scen_0", "scen_1", "scen_2", "row", "col"),
    )
    in_specs = (
        P(SCEN, None, ("row", "col"), None),
        P(SCEN, None, None),
        P(SCEN, None, None),
        P(SCEN_ROW, "col"),
        P(SCEN_ROW_COL, None),
    )
    out_specs = P(SCEN_ROW_COL, None)
    return jax.shard_map(
        per_device, mesh=split, in_specs=in_specs, out_specs=out_specs, check_vma=False
    )
```

time: 129 us -> 146 us (1.13)
  starting transfers between devices: 49.4 us -> 74.4 us
  matrix products: 23.8 us -> 13.1 us
  Pallas kernels: 28.7 us -> 38.2 us
  local copies, waits for them, and re-layouts: 10.4 us -> 1.79 us
  other arithmetic: 1.56 us -> 3.09 us
    ppermute x6 -> x9, starting transfers between devices: 12.3 us -> 26.2 us  [swapped(): return lax.ppermute(value, axis, [(0, 1), (1, 0)])]
    pallas_call x0 -> x2, Pallas kernels: none -> 13.1 us  [the longest x1 9.61 us: coupling_halves(): pl.pallas_call(coupling_kernel, out_shape=(half, half), grid_spec=grid_sp...]
    dot_general x3 -> x1, matrix products: 12.4 us -> 2.86 us  [per_device(): jnp.einsum('snr,snp->rp', solved, panel_border, preferred_element_type=F32)]
    ppermute x9, starting transfers between devices: 13.3 us -> 20.5 us  [shifts(): lax.ppermute(value, axis, [(i, (i + step) % peers) for i in range(peers)])]
    ppermute x4 -> x10, starting transfers between devices: 11.1 us -> 14.9 us  [the longest x6 10 us: scattered_sum(): lax.ppermute(piece, axis, [(i, (i + step) % peers) for i in range(peers)])]
    unnamed x13 -> x24, local copies, waits for them, and re-layouts: 4.49 us -> 0.77 us
    squeeze x1 -> x0, local copies, waits for them, and re-layouts: 3.2 us -> none  [per_device(): half_of(coupling, 1, 1 - core)[:, 0]]
    pallas_call x1, Pallas kernels: 26.7 us -> 24.2 us  [inverse_factor(): pl.pallas_call(inverse_kernel, out_shape=jax.ShapeDtypeStruct((n, n), F32...]
  transfers between devices with their start and end apart: 22 -> 31, of which waited for: 10 -> 10; matrix products, arithmetic and copies ran while one was open for 24% -> 10% of each run, Pallas kernels for 21% -> 26%
where the time goes in v3:
time: 146 us
  starting transfers between devices  74.4 us (51%)
  Pallas kernels  38.2 us (26%)
  waiting for transfers between devices  14.8 us (10%)
  matrix products  13.1 us (9%)
  other arithmetic  3.09 us (2%)
  local copies, waits for them, and re-layouts  1.79 us (1%)
    ppermute x9, starting transfers between devices, swapped(): return lax.ppermute(value, axis, [(0, 1), (1, 0)])  26.2 us
    pallas_call x1, Pallas kernels, inverse_factor(): pl.pallas_call(inverse_kernel, out_shape=jax.ShapeDtypeStruct((n, n), F32...  24.2 us
    ppermute x9, starting transfers between devices, shifts(): lax.ppermute(value, axis, [(i, (i + step) % peers) for i in range(peers)])  20.5 us
    all_to_all x2, starting transfers between devices, exchanged(): return lax.all_to_all(pieces, axis, 0, 0, tiled=True)  11.5 us
    ppermute x6, starting transfers between devices, scattered_sum(): lax.ppermute(piece, axis, [(i, (i + step) % peers) for i in range(peers)])  10 us
    pallas_call x1, Pallas kernels, coupling_halves(): pl.pallas_call(coupling_kernel, out_shape=(half, half), grid_spec=grid_sp...  9.61 us
    ppermute x9, waiting for transfers between devices, shifts(): lax.ppermute(value, axis, [(i, (i + step) % peers) for i in range(peers)])  6.76 us
    dot_general x2, matrix products, per_device(): lax.dot_general(slices[:, slot], leads[slot], (((2,), (1,)), ((), ())), p...  4.67 us
  transfers between devices with their start and end apart: 31, of which 10 were waited for; matrix products, arithmetic and copies ran while one was open for 10% of the time, Pallas kernels for 26%

profile of v3, /device:TPU:1, one launch (start us, length us, event | category | flops | bytes accessed | tf_op | source)
XLA Modules:
  0.0 145.6 jit_solution(1717538058084966580)
XLA Ops:
  0.0 0.8 collective-permute-start.1
  0.8 1.0 constant_dynamic-slice_fusion.6
  1.8 2.5 %collective-permute-start = (bf16[64,2048]{1,0:T(8,128)(2,1)S(1)}, bf16[64,2048]{1,0:T(8,128)(2,1)S(1)}, u32[]{:S(2)}, u32[]{:S(2)}) collective-permute-start(bf16[64,2048]{1,0:T(8,128)(2,1)S(1)} %constant_dynamic-slice_fusion.6), channel_id=1, source_target_pairs={{0,1},{1,0},{2,3},{3,2},{4,5},{5,4},{6,7},{7,6},{8,9},{9,8},{10,11... | collective-permute-start | bytes 786440 | tf_op jit(solution)/shard_map/ppermute | solution.py:256
  4.4 4.3 %convolution_convert_fusion.solved_ref = bf16[4,512,512]{2,1,0:T(8,128)(2,1)} fusion(bf16[4,512,512]{2,1,0:T(8,128)(2,1)} %param.12, bf16[4,512,512]{2,1,0:T(8,128)(2,1)S(1)} %copy-done), kind=kOutput, calls=%fused_computation.2 | convolution fusion | flops 1074790400 | bytes 6291456 | tf_op jit(solution)/shard_map/snm,smp->snp/dot_general | solution.py:354
  8.7 1.4 collective-permute-start.2
  10.1 1.4 collective-permute-start.3
  11.5 1.4 collective-permute-start.4
  12.9 0.9 packed.1
  13.7 6.8 %all-to-all-start = ((bf16[16,2,64,128]{3,2,1,0:T(8,128)(2,1)}), bf16[16,2,64,128]{3,2,1,0:T(8,128)(2,1)}, u32[]{:S(2)}, u32[]{:S(2)}) async-start(bf16[16,2,64,128]{3,2,1,0:T(8,128)(2,1)} %packed.1), calls=%async_computation | async-start | bytes 1048576 | tf_op jit(solution)/shard_map/all_to_all | solution.py:309
  20.6 2.9 %convolution_bitcast_fusion.gram_ref = f32[512,512]{1,0:T(8,128)S(1)} fusion(bf16[4,512,512]{2,1,0:T(8,128)(2,1)} %convolution_convert_fusion.solved_ref, bf16[4,512,512]{2,1,0:T(8,128)(2,1)S(1)} %copy-done), kind=kOutput, calls=%fused_computation.3 | convolution fusion | flops 1073741824 | bytes 5242880 | tf_op jit(solution)/shard_map/snr,snp->rp/dot_general | solution.py:362
  23.5 9.6 %coupling_halves.1 = (f32[16,64,512]{2,1,0:T(8,128)}, f32[16,64,512]{2,1,0:T(8,128)}) custom-call(s32[1]{0:T(128)} %bitcast.1.core_ref, bf16[4,16,2,64,512]{4,3,2,1,0:T(8,128)(2,1)} %bitcast.36, bf16[4,512,512]{2,1,0:T(8,128)(2,1)} %convolution_convert_fusion.solved_ref), custom_call_target="tpu_custom_call" | custom-call | flops 4294967296 | bytes 12582912 | tf_op jit(solution)/shard_map/coupling_halves/pallas_call | solution.py:241
  33.1 13.7 %collective-permute-start.5 = (f32[16,64,512]{2,1,0:T(8,128)}, f32[16,64,512]{2,1,0:T(8,128)}, u32[]{:S(2)}, u32[]{:S(2)}) collective-permute-start(f32[16,64,512]{2,1,0:T(8,128)} %get-tuple-element.25), channel_id=1, source_target_pairs={{0,8},{8,0},{1,9},{9,1},{2,10},{10,2},{3,11},{11,3},{4,12},{12,4},... | collective-permute-start | bytes 6291464 | tf_op jit(solution)/shard_map/ppermute | solution.py:256
  47.5 1.3 collective-permute-start.6
  48.8 2.0 %collective-permute-done.6 = bf16[64,128]{1,0:T(8,128)(2,1)S(1)} collective-permute-done((bf16[64,128]{1,0:T(8,128)(2,1)S(1)}, bf16[64,128]{1,0:T(8,128)(2,1)S(1)}, u32[]{:S(2)}, u32[]{:S(2)}) %collective-permute-start.6) | collective-permute-done | bytes 16416 | tf_op jit(solution)/shard_map/ppermute | solution.py:367
  50.8 0.7 bitcast_select_fusion
  52.3 1.8 %collective-permute-done.7 = bf16[64,128]{1,0:T(8,128)(2,1)S(1)} collective-permute-done((bf16[64,128]{1,0:T(8,128)(2,1)S(1)}, bf16[64,128]{1,0:T(8,128)(2,1)S(1)}, u32[]{:S(2)}, u32[]{:S(2)}) %collective-permute-start.7) | collective-permute-done | bytes 16416 | tf_op jit(solution)/shard_map/ppermute | solution.py:256
  54.1 2.4 %collective-permute-start.8 = (bf16[2,64,128]{2,1,0:T(8,128)(2,1)S(1)}, bf16[2,64,128]{2,1,0:T(8,128)(2,1)S(1)}, u32[]{:S(2)}, u32[]{:S(2)}) collective-permute-start(bf16[2,64,128]{2,1,0:T(8,128)(2,1)S(1)} %pad_maximum_fusion.2.refs_0_), channel_id=1, source_target_pairs={{0,2},{2,4},{4,6},{6,0},{1,3},{3,5},{5,7},{7,1},{8,10},{10,12},{12... | collective-permute-start | bytes 98312 | tf_op jit(solution)/shard_map/ppermute | solution.py:262
  56.5 0.9 collective-permute-start.9
  57.9 1.2 collective-permute-done.8.refs_1_
  59.1 4.1 %collective-permute-done.9.refs_2_ = bf16[2,64,128]{2,1,0:T(8,128)(2,1)S(1)} collective-permute-done((bf16[2,64,128]{2,1,0:T(8,128)(2,1)S(1)}, bf16[2,64,128]{2,1,0:T(8,128)(2,1)S(1)}, u32[]{:S(2)}, u32[]{:S(2)}) %collective-permute-start.9) | collective-permute-done | bytes 32800 | tf_op jit(solution)/shard_map/ppermute | solution.py:262
  63.2 3.5 %panel_halves.1 = (f32[640,128]{1,0:T(8,128)S(1)}, f32[640,128]{1,0:T(8,128)}, bf16[512,128]{1,0:T(8,128)(2,1)S(1)}) custom-call(s32[9]{0:T(128)S(1)} %pad_add_fusion.place_ref, f32[512,512]{1,0:T(8,128)S(1)} %convolution_bitcast_fusion.gram_ref, bf16[2,64,128]{2,1,0:T(8,128)(2,1)S(1)} %pad_maximum_fusion.2.refs_0_, ...), custom_call_target="tpu_custom_call" | custom-call | flops 2000000 | bytes 4194304 | tf_op jit(solution)/shard_map/panel_halves/pallas_call | solution.py:193
  67.4 3.0 %collective-permute-start.11 = (bf16[512,128]{1,0:T(8,128)(2,1)S(1)}, bf16[512,128]{1,0:T(8,128)(2,1)S(1)}, u32[]{:S(2)}, u32[]{:S(2)}) collective-permute-start(bf16[512,128]{1,0:T(8,128)(2,1)S(1)} %get-tuple-element.32), channel_id=1, source_target_pairs={{0,8},{8,0},{1,9},{9,1},{2,10},{10,2},{3,11},{11,3},{4,12},{12,4},... | collective-permute-start | bytes 393224 | tf_op jit(solution)/shard_map/ppermute | solution.py:256
  70.4 1.0 collective-permute-done.11
  71.4 1.4 fusion.4
  72.9 1.5 %collective-permute-start.13 = (f32[160,128]{1,0:T(8,128)S(1)}, f32[160,128]{1,0:T(8,128)S(1)}, u32[]{:S(2)}, u32[]{:S(2)}) collective-permute-start(f32[160,128]{1,0:T(8,128)S(1)} %get-tuple-element.35), channel_id=1, source_target_pairs={{0,16},{16,32},{32,48},{48,0},{1,17},{17,33},{33,49},{49,1},{2,18}... | collective-permute-start | bytes 245768 | tf_op jit(solution)/shard_map/ppermute | solution.py:304
  74.4 2.4 %collective-permute-start.14 = (f32[160,128]{1,0:T(8,128)S(1)}, f32[160,128]{1,0:T(8,128)S(1)}, u32[]{:S(2)}, u32[]{:S(2)}) collective-permute-start(f32[160,128]{1,0:T(8,128)S(1)} %get-tuple-element.37), channel_id=1, source_target_pairs={{0,32},{16,48},{32,0},{48,16},{1,33},{17,49},{33,1},{49,17},{2,34}... | collective-permute-start | bytes 245768 | tf_op jit(solution)/shard_map/ppermute | solution.py:304
  76.8 1.2 collective-permute-start.15
  78.0 3.3 %subtract_convert_fusion = bf16[16,64,512]{2,1,0:T(8,128)(2,1)} fusion(f32[16,64,512]{2,1,0:T(8,128)S(1)} %fusion.4, f32[16,64,512]{2,1,0:T(8,128)S(1)} %copy-done.4, f32[16,64,512]{2,1,0:T(8,128)} %collective-permute-done.5, bf16[16,2,64,128]{3,2,1,0:T(8,128)(2,1)} %all-to-all-done, pred[]{:T(512)S(6)} %eq.7, bf16[512,128]{1,0:T(8,128)(2,1)S(1)} %get-tuple-element.32, ...), kind=kOutput, calls=%fused_computation.1 | convolution fusion | flops 136511488 | bytes 7864322 | tf_op jit(solution)/shard_map/dot_general | solution.py:380
  81.3 4.7 %all-to-all-start.1 = ((bf16[16,64,512]{2,1,0:T(8,128)(2,1)}), bf16[16,64,512]{2,1,0:T(8,128)(2,1)}, u32[]{:S(2)}, u32[]{:S(2)}) async-start(bf16[16,64,512]{2,1,0:T(8,128)(2,1)} %subtract_convert_fusion), calls=%async_computation.1 | async-start | bytes 2097152 | tf_op jit(solution)/shard_map/all_to_all | solution.py:309
  86.1 1.3 collective-permute-start.16
  87.3 2.4 %collective-permute-start.17 = (f32[40,128]{1,0:T(8,128)S(1)}, f32[40,128]{1,0:T(8,128)S(1)}, u32[]{:S(2)}, u32[]{:S(2)}) collective-permute-start(f32[40,128]{1,0:T(8,128)S(1)} %get-tuple-element.40), channel_id=1, source_target_pairs={{0,128},{64,192},{128,0},{192,64},{1,129},{65,193},{129,1},{193,65... | collective-permute-start | bytes 61448 | tf_op jit(solution)/shard_map/ppermute | solution.py:304
  89.8 1.2 collective-permute-start.18
  91.0 1.0 collective-permute-done.17
  91.9 1.3 collective-permute-done.18
  93.3 2.0 %collective-permute-start.19 = (f32[40,128]{1,0:T(8,128)S(1)}, f32[40,128]{1,0:T(8,128)S(1)}, u32[]{:S(2)}, u32[]{:S(2)}) collective-permute-start(f32[40,128]{1,0:T(8,128)S(1)} %add_add_fusion.1), channel_id=1, source_target_pairs={{0,64},{64,128},{128,192},{192,0},{1,65},{65,129},{129,193},{193,1... | collective-permute-start | bytes 61448 | tf_op jit(solution)/shard_map/ppermute | solution.py:262
  95.3 5.3 %collective-permute-start.20 = (f32[40,128]{1,0:T(8,128)S(1)}, f32[40,128]{1,0:T(8,128)S(1)}, u32[]{:S(2)}, u32[]{:S(2)}) collective-permute-start(f32[40,128]{1,0:T(8,128)S(1)} %add_add_fusion.1), channel_id=1, source_target_pairs={{0,128},{64,192},{128,0},{192,64},{1,129},{65,193},{129,1},{193,65... | collective-permute-start | bytes 61448 | tf_op jit(solution)/shard_map/ppermute | solution.py:262
  100.7 2.0 %collective-permute-start.21 = (f32[40,128]{1,0:T(8,128)S(1)}, f32[40,128]{1,0:T(8,128)S(1)}, u32[]{:S(2)}, u32[]{:S(2)}) collective-permute-start(f32[40,128]{1,0:T(8,128)S(1)} %add_add_fusion.1), channel_id=1, source_target_pairs={{0,192},{64,0},{128,64},{192,128},{1,193},{65,1},{129,65},{193,129... | collective-permute-start | bytes 61448 | tf_op jit(solution)/shard_map/ppermute | solution.py:262
  102.6 1.1 collective-permute-done.21
  103.7 4.0 %collective-permute-start.22 = (f32[160,128]{1,0:T(8,128)S(1)}, f32[160,128]{1,0:T(8,128)S(1)}, u32[]{:S(2)}, u32[]{:S(2)}) collective-permute-start(f32[160,128]{1,0:T(8,128)S(1)} %pad_maximum_fusion.1.refs_0_), channel_id=1, source_target_pairs={{0,16},{16,32},{32,48},{48,0},{1,17},{17,33},{33,49},{49,1},{2,18}... | collective-permute-start | bytes 245768 | tf_op jit(solution)/shard_map/ppermute | solution.py:262
  107.7 2.2 %collective-permute-start.23 = (f32[160,128]{1,0:T(8,128)S(1)}, f32[160,128]{1,0:T(8,128)S(1)}, u32[]{:S(2)}, u32[]{:S(2)}) collective-permute-start(f32[160,128]{1,0:T(8,128)S(1)} %pad_maximum_fusion.1.refs_0_), channel_id=1, source_target_pairs={{0,32},{16,48},{32,0},{48,16},{1,33},{17,49},{33,1},{49,17},{2,34}... | collective-permute-start | bytes 245768 | tf_op jit(solution)/shard_map/ppermute | solution.py:262
  109.9 1.6 %collective-permute-start.24 = (f32[160,128]{1,0:T(8,128)S(1)}, f32[160,128]{1,0:T(8,128)S(1)}, u32[]{:S(2)}, u32[]{:S(2)}) collective-permute-start(f32[160,128]{1,0:T(8,128)S(1)} %pad_maximum_fusion.1.refs_0_), channel_id=1, source_target_pairs={{0,48},{16,0},{32,16},{48,32},{1,49},{17,1},{33,17},{49,33},{2,50}... | collective-permute-start | bytes 245768 | tf_op jit(solution)/shard_map/ppermute | solution.py:262
  111.6 3.0 %collective-permute-start.25 = (f32[160,128]{1,0:T(8,128)S(1)}, f32[160,128]{1,0:T(8,128)S(1)}, u32[]{:S(2)}, u32[]{:S(2)}) collective-permute-start(f32[160,128]{1,0:T(8,128)S(1)} %pad_maximum_fusion.1.refs_0_), channel_id=1, source_target_pairs={{0,8},{8,0},{1,9},{9,1},{2,10},{10,2},{3,11},{11,3},{4,12},{12,4},... | collective-permute-start | bytes 245768 | tf_op jit(solution)/shard_map/ppermute | solution.py:256
  114.9 1.8 %collective-permute-start.27 = (f32[160,128]{1,0:T(8,128)S(1)}, f32[160,128]{1,0:T(8,128)S(1)}, u32[]{:S(2)}, u32[]{:S(2)}) collective-permute-start(f32[160,128]{1,0:T(8,128)S(1)} %collective-permute-done.23.refs_2_), channel_id=1, source_target_pairs={{0,8},{8,0},{1,9},{9,1},{2,10},{10,2},{3,11},{11,3},{4,12},{12,4},... | collective-permute-start | bytes 245768 | tf_op jit(solution)/shard_map/ppermute | solution.py:256
  116.7 1.1 collective-permute-start.28
  117.9 0.9 collective-permute-done.28.refs_7_
  118.7 24.2 %inverse_factor.1 = f32[512,512]{1,0:T(8,128)S(1)} custom-call(s32[32]{0:T(128)S(1)} %fusion.28.place_ref, f32[160,128]{1,0:T(8,128)S(1)} %pad_maximum_fusion.1.refs_0_, f32[160,128]{1,0:T(8,128)S(1)} %collective-permute-done.22.refs_1_, f32[160,128]{1,0:T(8,128)S(1)} %collective-permute-done.23.refs_2_, f32[160,128]{1,0:T(8,128)S(1)} %collective-permute-done.24.refs_3_, ...), custom_call_target="tpu_custom_call" | custom-call | flops 40000000 | bytes 2097152 | tf_op jit(solution)/shard_map/inverse_factor/pallas_call | solution.py:144
  142.9 1.4 convert_reduce_fusion
  144.3 1.3 fusion.10
  (64 shorter events, 3.3 us)
Async XLA Ops:
  0.0 4.4 %copy-start = (bf16[4,512,512]{2,1,0:T(8,128)(2,1)S(1)}, bf16[4,512,512]{2,1,0:T(8,128)(2,1)}, u32[]{:S(2)}) copy-start(bf16[4,512,512]{2,1,0:T(8,128)(2,1)} %param.11) | copy-start | bytes 6291460
  0.0 8.6 %collective-permute-start.1 = (f32[64,512]{1,0:T(8,128)S(1)}, f32[64,512]{1,0:T(8,128)S(1)}, u32[]{:S(2)}, u32[]{:S(2)}) collective-permute-start(f32[64,512]{1,0:T(8,128)S(1)} %broadcast_select_fusion.2), channel_id=1, source_target_pairs={{0,1},{1,0},{2,3},{3,2},{4,5},{5,4},{6,7},{7,6}} | collective-permute-start | bytes 393224 | tf_op jit(solution)/shard_map/ppermute | solution.py:273
  1.8 11.0 %collective-permute-start = (bf16[64,2048]{1,0:T(8,128)(2,1)S(1)}, bf16[64,2048]{1,0:T(8,128)(2,1)S(1)}, u32[]{:S(2)}, u32[]{:S(2)}) collective-permute-start(bf16[64,2048]{1,0:T(8,128)(2,1)S(1)} %constant_dynamic-slice_fusion.6), channel_id=1, source_target_pairs={{0,1},{1,0},{2,3},{3,2},{4,5},{5,4},{6,7},{7,6},{8,9},{9,8},{10,11... | collective-permute-start | bytes 786440 | tf_op jit(solution)/shard_map/ppermute | solution.py:256
  4.4 4.3 %copy-start.5 = (f32[64,512]{1,0:T(8,128)S(1)}, f32[64,512]{1,0:T(8,128)}, u32[]{:S(2)}) copy-start(f32[64,512]{1,0:T(8,128)} %param.14) | copy-start | bytes 393220
  4.4 8.5 %copy-start.1 = (bf16[128,2048]{1,0:T(8,128)(2,1)S(1)}, bf16[128,2048]{1,0:T(8,128)(2,1)}, u32[]{:S(2)}) copy-start(bf16[128,2048]{1,0:T(8,128)(2,1)} %factor_ref.1) | copy-start | bytes 1572868
  8.7 24.4 %collective-permute-start.2 = (f32[2,64,512]{2,1,0:T(8,128)S(1)}, f32[2,64,512]{2,1,0:T(8,128)}, u32[]{:S(2)}, u32[]{:S(2)}) collective-permute-start(f32[2,64,512]{2,1,0:T(8,128)S(1)} %pad_maximum_fusion.refs_4_), channel_id=1, source_target_pairs={{0,2},{2,4},{4,6},{6,0},{1,3},{3,5},{5,7},{7,1}} | collective-permute-start | bytes 786440 | tf_op jit(solution)/shard_map/ppermute | solution.py:275
  10.1 23.0 %collective-permute-start.3 = (f32[2,64,512]{2,1,0:T(8,128)S(1)}, f32[2,64,512]{2,1,0:T(8,128)}, u32[]{:S(2)}, u32[]{:S(2)}) collective-permute-start(f32[2,64,512]{2,1,0:T(8,128)S(1)} %pad_maximum_fusion.refs_4_), channel_id=1, source_target_pairs={{0,4},{2,6},{4,0},{6,2},{1,5},{3,7},{5,1},{7,3}} | collective-permute-start | bytes 786440 | tf_op jit(solution)/shard_map/ppermute | solution.py:275
  11.5 21.6 %collective-permute-start.4 = (f32[2,64,512]{2,1,0:T(8,128)S(1)}, f32[2,64,512]{2,1,0:T(8,128)}, u32[]{:S(2)}, u32[]{:S(2)}) collective-permute-start(f32[2,64,512]{2,1,0:T(8,128)S(1)} %pad_maximum_fusion.refs_4_), channel_id=1, source_target_pairs={{0,6},{2,0},{4,2},{6,4},{1,7},{3,1},{5,3},{7,5}} | collective-permute-start | bytes 786440 | tf_op jit(solution)/shard_map/ppermute | solution.py:275
  13.7 19.3 %all-to-all-start = ((bf16[16,2,64,128]{3,2,1,0:T(8,128)(2,1)}), bf16[16,2,64,128]{3,2,1,0:T(8,128)(2,1)}, u32[]{:S(2)}, u32[]{:S(2)}) async-start(bf16[16,2,64,128]{3,2,1,0:T(8,128)(2,1)} %packed.1), calls=%async_computation | async-start | bytes 1048576 | tf_op jit(solution)/shard_map/all_to_all | solution.py:309
  23.4 28.8 %copy-start.10 = (s32[8]{0:T(128)S(1)}, s32[8]{0:T(128)}, u32[]{:S(2)}) copy-start(s32[8]{0:T(128)} %constant.81.clone) | copy-start | bytes 100
  23.4 28.8 %copy-start.11 = (s32[8]{0:T(128)S(1)}, s32[8]{0:T(128)}, u32[]{:S(2)}) copy-start(s32[8]{0:T(128)} %constant.82.clone) | copy-start | bytes 100
  33.1 44.9 %collective-permute-start.5 = (f32[16,64,512]{2,1,0:T(8,128)}, f32[16,64,512]{2,1,0:T(8,128)}, u32[]{:S(2)}, u32[]{:S(2)}) collective-permute-start(f32[16,64,512]{2,1,0:T(8,128)} %get-tuple-element.25), channel_id=1, source_target_pairs={{0,8},{8,0},{1,9},{9,1},{2,10},{10,2},{3,11},{11,3},{4,12},{12,4},... | collective-permute-start | bytes 6291464 | tf_op jit(solution)/shard_map/ppermute | solution.py:256
  47.5 3.3 %collective-permute-start.6 = (bf16[64,128]{1,0:T(8,128)(2,1)S(1)}, bf16[64,128]{1,0:T(8,128)(2,1)S(1)}, u32[]{:S(2)}, u32[]{:S(2)}) collective-permute-start(bf16[64,128]{1,0:T(8,128)(2,1)S(1)} %select_bitcast_fusion), channel_id=1, source_target_pairs={{0,8},{1,9},{2,10},{3,11},{4,12},{5,13},{6,14},{7,15},{16,24},{17,... | collective-permute-start | bytes 49160 | tf_op jit(solution)/shard_map/ppermute | solution.py:367
  51.5 2.6 %collective-permute-start.7 = (bf16[64,128]{1,0:T(8,128)(2,1)S(1)}, bf16[64,128]{1,0:T(8,128)(2,1)S(1)}, u32[]{:S(2)}, u32[]{:S(2)}) collective-permute-start(bf16[64,128]{1,0:T(8,128)(2,1)S(1)} %bitcast_select_fusion), channel_id=1, source_target_pairs={{0,1},{1,0},{2,3},{3,2},{4,5},{5,4},{6,7},{7,6},{8,9},{9,8},{10,11... | collective-permute-start | bytes 49160 | tf_op jit(solution)/shard_map/ppermute | solution.py:256
  54.1 3.8 %collective-permute-start.10 = (bf16[2,64,128]{2,1,0:T(8,128)(2,1)S(1)}, bf16[2,64,128]{2,1,0:T(8,128)(2,1)S(1)}, u32[]{:S(2)}, u32[]{:S(2)}) collective-permute-start(bf16[2,64,128]{2,1,0:T(8,128)(2,1)S(1)} %pad_maximum_fusion.2.refs_0_), channel_id=1, source_target_pairs={{0,6},{2,0},{4,2},{6,4},{1,7},{3,1},{5,3},{7,5},{8,14},{10,8},{12,... | collective-permute-start | bytes 98312 | tf_op jit(solution)/shard_map/ppermute | solution.py:262
  54.1 5.0 %collective-permute-start.8 = (bf16[2,64,128]{2,1,0:T(8,128)(2,1)S(1)}, bf16[2,64,128]{2,1,0:T(8,128)(2,1)S(1)}, u32[]{:S(2)}, u32[]{:S(2)}) collective-permute-start(bf16[2,64,128]{2,1,0:T(8,128)(2,1)S(1)} %pad_maximum_fusion.2.refs_0_), channel_id=1, source_target_pairs={{0,2},{2,4},{4,6},{6,0},{1,3},{3,5},{5,7},{7,1},{8,10},{10,12},{12... | collective-permute-start | bytes 98312 | tf_op jit(solution)/shard_map/ppermute | solution.py:262
  56.5 6.7 %collective-permute-start.9 = (bf16[2,64,128]{2,1,0:T(8,128)(2,1)S(1)}, bf16[2,64,128]{2,1,0:T(8,128)(2,1)S(1)}, u32[]{:S(2)}, u32[]{:S(2)}) collective-permute-start(bf16[2,64,128]{2,1,0:T(8,128)(2,1)S(1)} %pad_maximum_fusion.2.refs_0_), channel_id=1, source_target_pairs={{0,4},{2,6},{4,0},{6,2},{1,5},{3,7},{5,1},{7,3},{8,12},{10,14},{12... | collective-permute-start | bytes 98312 | tf_op jit(solution)/shard_map/ppermute | solution.py:262
  66.7 0.7 copy-start.2
  67.4 5.4 %copy-start.3 = (f32[640,128]{1,0:T(8,128)S(1)}, f32[640,128]{1,0:T(8,128)}, u32[]{:S(2)}) copy-start(f32[640,128]{1,0:T(8,128)} %copy-done.2) | copy-start | bytes 983044
  67.4 4.0 %collective-permute-start.11 = (bf16[512,128]{1,0:T(8,128)(2,1)S(1)}, bf16[512,128]{1,0:T(8,128)(2,1)S(1)}, u32[]{:S(2)}, u32[]{:S(2)}) collective-permute-start(bf16[512,128]{1,0:T(8,128)(2,1)S(1)} %get-tuple-element.32), channel_id=1, source_target_pairs={{0,8},{8,0},{1,9},{9,1},{2,10},{10,2},{3,11},{11,3},{4,12},{12,4},... | collective-permute-start | bytes 393224 | tf_op jit(solution)/shard_map/ppermute | solution.py:256
  70.4 2.4 %collective-permute-start.12 = (f32[640,128]{1,0:T(8,128)}, f32[640,128]{1,0:T(8,128)S(1)}, u32[]{:S(2)}, u32[]{:S(2)}) collective-permute-start(f32[640,128]{1,0:T(8,128)} %get-tuple-element.34), channel_id=1, source_target_pairs={{0,8},{8,0},{1,9},{9,1},{2,10},{10,2},{3,11},{11,3},{4,12},{12,4},... | collective-permute-start | bytes 983048 | tf_op jit(solution)/shard_map/ppermute | solution.py:256
  70.4 7.6 %copy-start.4 = (f32[16,64,512]{2,1,0:T(8,128)S(1)}, f32[16,64,512]{2,1,0:T(8,128)}, u32[]{:S(2)}) copy-start(f32[16,64,512]{2,1,0:T(8,128)} %get-tuple-element.24) | copy-start | bytes 6291460
  72.9 13.1 %collective-permute-start.13 = (f32[160,128]{1,0:T(8,128)S(1)}, f32[160,128]{1,0:T(8,128)S(1)}, u32[]{:S(2)}, u32[]{:S(2)}) collective-permute-start(f32[160,128]{1,0:T(8,128)S(1)} %get-tuple-element.35), channel_id=1, source_target_pairs={{0,16},{16,32},{32,48},{48,0},{1,17},{17,33},{33,49},{49,1},{2,18}... | collective-permute-start | bytes 245768 | tf_op jit(solution)/shard_map/ppermute | solution.py:304
  74.4 11.6 %collective-permute-start.14 = (f32[160,128]{1,0:T(8,128)S(1)}, f32[160,128]{1,0:T(8,128)S(1)}, u32[]{:S(2)}, u32[]{:S(2)}) collective-permute-start(f32[160,128]{1,0:T(8,128)S(1)} %get-tuple-element.37), channel_id=1, source_target_pairs={{0,32},{16,48},{32,0},{48,16},{1,33},{17,49},{33,1},{49,17},{2,34}... | collective-permute-start | bytes 245768 | tf_op jit(solution)/shard_map/ppermute | solution.py:304
  76.8 9.2 %collective-permute-start.15 = (f32[160,128]{1,0:T(8,128)S(1)}, f32[160,128]{1,0:T(8,128)S(1)}, u32[]{:S(2)}, u32[]{:S(2)}) collective-permute-start(f32[160,128]{1,0:T(8,128)S(1)} %get-tuple-element.36), channel_id=1, source_target_pairs={{0,48},{16,0},{32,16},{48,32},{1,49},{17,1},{33,17},{49,33},{2,50}... | collective-permute-start | bytes 245768 | tf_op jit(solution)/shard_map/ppermute | solution.py:304
  81.3 36.5 %copy-start.7 = (s32[32]{0:T(128)S(1)}, s32[32]{0:T(128)}, u32[]{:S(2)}) copy-start(s32[32]{0:T(128)} %constant.83.clone) | copy-start | bytes 388
  81.3 36.5 %copy-start.8 = (s32[32]{0:T(128)S(1)}, s32[32]{0:T(128)}, u32[]{:S(2)}) copy-start(s32[32]{0:T(128)} %constant.84.clone) | copy-start | bytes 388
  81.3 36.5 %copy-start.9 = (s32[32]{0:T(128)S(1)}, s32[32]{0:T(128)}, u32[]{:S(2)}) copy-start(s32[32]{0:T(128)} %constant.85.clone) | copy-start | bytes 388
  81.3 61.6 %all-to-all-start.1 = ((bf16[16,64,512]{2,1,0:T(8,128)(2,1)}), bf16[16,64,512]{2,1,0:T(8,128)(2,1)}, u32[]{:S(2)}, u32[]{:S(2)}) async-start(bf16[16,64,512]{2,1,0:T(8,128)(2,1)} %subtract_convert_fusion), calls=%async_computation.1 | async-start | bytes 2097152 | tf_op jit(solution)/shard_map/all_to_all | solution.py:309
  86.0 58.4 %copy-start.6 = (f32[64,512]{1,0:T(8,128)S(1)}, f32[64,512]{1,0:T(8,128)}, u32[]{:S(2)}) copy-start(f32[64,512]{1,0:T(8,128)} %param.14) | copy-start | bytes 393220
  86.1 4.9 %collective-permute-start.16 = (f32[40,128]{1,0:T(8,128)S(1)}, f32[40,128]{1,0:T(8,128)S(1)}, u32[]{:S(2)}, u32[]{:S(2)}) collective-permute-start(f32[40,128]{1,0:T(8,128)S(1)} %get-tuple-element.38), channel_id=1, source_target_pairs={{0,64},{64,128},{128,192},{192,0},{1,65},{65,129},{129,193},{193,1... | collective-permute-start | bytes 61448 | tf_op jit(solution)/shard_map/ppermute | solution.py:304
  87.3 4.6 %collective-permute-start.17 = (f32[40,128]{1,0:T(8,128)S(1)}, f32[40,128]{1,0:T(8,128)S(1)}, u32[]{:S(2)}, u32[]{:S(2)}) collective-permute-start(f32[40,128]{1,0:T(8,128)S(1)} %get-tuple-element.40), channel_id=1, source_target_pairs={{0,128},{64,192},{128,0},{192,64},{1,129},{65,193},{129,1},{193,65... | collective-permute-start | bytes 61448 | tf_op jit(solution)/shard_map/ppermute | solution.py:304
  89.8 3.5 %collective-permute-start.18 = (f32[40,128]{1,0:T(8,128)S(1)}, f32[40,128]{1,0:T(8,128)S(1)}, u32[]{:S(2)}, u32[]{:S(2)}) collective-permute-start(f32[40,128]{1,0:T(8,128)S(1)} %get-tuple-element.39), channel_id=1, source_target_pairs={{0,192},{64,0},{128,64},{192,128},{1,193},{65,1},{129,65},{193,129... | collective-permute-start | bytes 61448 | tf_op jit(solution)/shard_map/ppermute | solution.py:304
  93.3 9.3 %collective-permute-start.19 = (f32[40,128]{1,0:T(8,128)S(1)}, f32[40,128]{1,0:T(8,128)S(1)}, u32[]{:S(2)}, u32[]{:S(2)}) collective-permute-start(f32[40,128]{1,0:T(8,128)S(1)} %add_add_fusion.1), channel_id=1, source_target_pairs={{0,64},{64,128},{128,192},{192,0},{1,65},{65,129},{129,193},{193,1... | collective-permute-start | bytes 61448 | tf_op jit(solution)/shard_map/ppermute | solution.py:262
  95.3 7.3 %collective-permute-start.20 = (f32[40,128]{1,0:T(8,128)S(1)}, f32[40,128]{1,0:T(8,128)S(1)}, u32[]{:S(2)}, u32[]{:S(2)}) collective-permute-start(f32[40,128]{1,0:T(8,128)S(1)} %add_add_fusion.1), channel_id=1, source_target_pairs={{0,128},{64,192},{128,0},{192,64},{1,129},{65,193},{129,1},{193,65... | collective-permute-start | bytes 61448 | tf_op jit(solution)/shard_map/ppermute | solution.py:262
  100.7 3.0 %collective-permute-start.21 = (f32[40,128]{1,0:T(8,128)S(1)}, f32[40,128]{1,0:T(8,128)S(1)}, u32[]{:S(2)}, u32[]{:S(2)}) collective-permute-start(f32[40,128]{1,0:T(8,128)S(1)} %add_add_fusion.1), channel_id=1, source_target_pairs={{0,192},{64,0},{128,64},{192,128},{1,193},{65,1},{129,65},{193,129... | collective-permute-start | bytes 61448 | tf_op jit(solution)/shard_map/ppermute | solution.py:262
  103.7 10.8 %collective-permute-start.22 = (f32[160,128]{1,0:T(8,128)S(1)}, f32[160,128]{1,0:T(8,128)S(1)}, u32[]{:S(2)}, u32[]{:S(2)}) collective-permute-start(f32[160,128]{1,0:T(8,128)S(1)} %pad_maximum_fusion.1.refs_0_), channel_id=1, source_target_pairs={{0,16},{16,32},{32,48},{48,0},{1,17},{17,33},{33,49},{49,1},{2,18}... | collective-permute-start | bytes 245768 | tf_op jit(solution)/shard_map/ppermute | solution.py:262
  107.7 7.2 %collective-permute-start.23 = (f32[160,128]{1,0:T(8,128)S(1)}, f32[160,128]{1,0:T(8,128)S(1)}, u32[]{:S(2)}, u32[]{:S(2)}) collective-permute-start(f32[160,128]{1,0:T(8,128)S(1)} %pad_maximum_fusion.1.refs_0_), channel_id=1, source_target_pairs={{0,32},{16,48},{32,0},{48,16},{1,33},{17,49},{33,1},{49,17},{2,34}... | collective-permute-start | bytes 245768 | tf_op jit(solution)/shard_map/ppermute | solution.py:262
  109.9 6.7 %collective-permute-start.24 = (f32[160,128]{1,0:T(8,128)S(1)}, f32[160,128]{1,0:T(8,128)S(1)}, u32[]{:S(2)}, u32[]{:S(2)}) collective-permute-start(f32[160,128]{1,0:T(8,128)S(1)} %pad_maximum_fusion.1.refs_0_), channel_id=1, source_target_pairs={{0,48},{16,0},{32,16},{48,32},{1,49},{17,1},{33,17},{49,33},{2,50}... | collective-permute-start | bytes 245768 | tf_op jit(solution)/shard_map/ppermute | solution.py:262
  111.6 6.3 %collective-permute-start.25 = (f32[160,128]{1,0:T(8,128)S(1)}, f32[160,128]{1,0:T(8,128)S(1)}, u32[]{:S(2)}, u32[]{:S(2)}) collective-permute-start(f32[160,128]{1,0:T(8,128)S(1)} %pad_maximum_fusion.1.refs_0_), channel_id=1, source_target_pairs={{0,8},{8,0},{1,9},{9,1},{2,10},{10,2},{3,11},{11,3},{4,12},{12,4},... | collective-permute-start | bytes 245768 | tf_op jit(solution)/shard_map/ppermute | solution.py:256
  114.5 3.3 %collective-permute-start.26 = (f32[160,128]{1,0:T(8,128)S(1)}, f32[160,128]{1,0:T(8,128)S(1)}, u32[]{:S(2)}, u32[]{:S(2)}) collective-permute-start(f32[160,128]{1,0:T(8,128)S(1)} %collective-permute-done.22.refs_1_), channel_id=1, source_target_pairs={{0,8},{8,0},{1,9},{9,1},{2,10},{10,2},{3,11},{11,3},{4,12},{12,4},... | collective-permute-start | bytes 245768 | tf_op jit(solution)/shard_map/ppermute | solution.py:256
  114.9 3.0 %collective-permute-start.27 = (f32[160,128]{1,0:T(8,128)S(1)}, f32[160,128]{1,0:T(8,128)S(1)}, u32[]{:S(2)}, u32[]{:S(2)}) collective-permute-start(f32[160,128]{1,0:T(8,128)S(1)} %collective-permute-done.23.refs_2_), channel_id=1, source_target_pairs={{0,8},{8,0},{1,9},{9,1},{2,10},{10,2},{3,11},{11,3},{4,12},{12,4},... | collective-permute-start | bytes 245768 | tf_op jit(solution)/shard_map/ppermute | solution.py:256
  116.7 2.1 %collective-permute-start.28 = (f32[160,128]{1,0:T(8,128)S(1)}, f32[160,128]{1,0:T(8,128)S(1)}, u32[]{:S(2)}, u32[]{:S(2)}) collective-permute-start(f32[160,128]{1,0:T(8,128)S(1)} %collective-permute-done.24.refs_3_), channel_id=1, source_target_pairs={{0,8},{8,0},{1,9},{9,1},{2,10},{10,2},{3,11},{11,3},{4,12},{12,4},... | collective-permute-start | bytes 245768 | tf_op jit(solution)/shard_map/ppermute | solution.py:256

commit v4 on v3

--- a/solution.py
+++ b/solution.py
@@ -84,24 +84,15 @@
     return terms[0] + terms[1] + terms[2]
 
 
-TILES = tuple((i, j) for i in range(4) for j in range(i, 4))
-
-
-def tile_rows(i, j):
-    at = TILES.index((i, j)) * BLOCK
-    return slice(at, at + BLOCK)
-
-
 def inverse_kernel(place_ref, *refs):
     part_refs, (w_ref, s_ref, d_ref) = refs[:-3], refs[-3:]
     n = w_ref.shape[0]
     blocks = n // BLOCK
-    count = place_ref.shape[0] // len(part_refs)
-    size = part_refs[0].shape[0] // count
+    count, size, _ = part_refs[0].shape
     for p, part in enumerate(part_refs):
         for q in range(count):
-            at = pl.multiple_of(place_ref[p * count + q], 8)
-            s_ref[pl.ds(at, size), :] = part[q * size : (q + 1) * size, :]
+            at = pl.multiple_of(place_ref[p * count + q], size)
+            s_ref[pl.ds(at, size), :] = part[q]
 
     def finish(k):
         lo, hi = k * BLOCK, (k + 1) * BLOCK
@@ -112,23 +103,20 @@
         if hi == n:
             return
         w_ref[lo:hi, hi:n] = jnp.zeros((BLOCK, n - hi), F32)
-        u = dot(w, jnp.concatenate([s_ref[tile_rows(k, j), :] for j in range(k + 1, blocks)], axis=1))
+        u = dot(w, s_ref[lo:hi, hi:n])
         for i in range(k + 1, blocks):
             il, ih = i * BLOCK, (i + 1) * BLOCK
             ui = u[:, il - hi : ih - hi]
-            drop = dot(ui, u[:, il - hi :], ((0,), (0,)))
-            for j in range(i, blocks):
-                cut = (j - i) * BLOCK
-                s_ref[tile_rows(i, j), :] = s_ref[tile_rows(i, j), :] - drop[:, cut : cut + BLOCK]
+            s_ref[il:ih, il:n] = s_ref[il:ih, il:n] - dot(ui, u[:, il - hi :], ((0,), (0,)))
             new = dot(ui, w_ref[lo:hi, 0:hi], ((0,), (0,)))
             if k > 0:
                 w_ref[il:ih, 0:lo] = w_ref[il:ih, 0:lo] - new[:, 0:lo]
             w_ref[il:ih, lo:hi] = -new[:, lo:hi]
 
     def step(k, carry):
-        own = (k * blocks - k * (k - 1) // 2) * BLOCK
+        lanes = pl.ds(pl.multiple_of(k * BLOCK, BLOCK), BLOCK)
         done = factor_block(
-            [s_ref[pl.ds(pl.multiple_of(own + 8 * g, 8), 8), :] for g in range(BLOCK // 8)]
+            [s_ref[pl.ds(pl.multiple_of(k * BLOCK + 8 * g, 8), 8), lanes] for g in range(BLOCK // 8)]
         )
         for g in range(BLOCK // 8):
             d_ref[8 * g : 8 * g + 8, :] = done[g]
@@ -139,67 +127,51 @@
     lax.fori_loop(0, blocks, step, 0)
 
 
-def inverse_factor(place, parts, n):
+def inverse_factor(place, parts):
     vmem = pl.BlockSpec(memory_space=pltpu.VMEM)
+    n = parts[0].shape[-1]
     return pl.pallas_call(
         inverse_kernel,
         out_shape=jax.ShapeDtypeStruct((n, n), F32),
         in_specs=[pl.BlockSpec(memory_space=pltpu.SMEM)] + [vmem] * len(parts),
         out_specs=vmem,
-        scratch_shapes=[
-            pltpu.VMEM((len(TILES) * BLOCK, BLOCK), F32),
-            pltpu.VMEM((BLOCK, BLOCK), F32),
-        ],
+        scratch_shapes=[pltpu.VMEM((n, n), F32), pltpu.VMEM((BLOCK, BLOCK), F32)],
         cost_estimate=pl.CostEstimate(flops=40_000_000, bytes_accessed=2 * n * n * 4, transcendentals=n),
         compiler_params=pltpu.CompilerParams(vmem_limit_bytes=12 * 2**20),
         name="inverse_factor",
     )(place, *parts)
 
 
-def panel_kernel(place_ref, gram_ref, *refs):
-    parts = (len(refs) - 4) // 2
-    lead_parts, root_parts = refs[:parts], refs[parts : 2 * parts]
-    mine_ref, theirs_ref, lead_ref, root_ref = refs[2 * parts :]
-    rows = lead_parts[0].shape[1]
-    for p in range(parts):
+def panel_kernel(place_ref, head_ref, base_ref, *refs):
+    lead_parts, (mine_ref, theirs_ref, lead_ref, rows_ref) = refs[:-4], refs[-4:]
+    rows = head_ref.shape[0]
+    for p, part in enumerate(lead_parts):
         for q in range(2):
             at = pl.multiple_of(place_ref[2 * p + q], rows)
-            lead_ref[pl.ds(at, rows), :] = lead_parts[p][q]
-            root_ref[pl.ds(at, rows), :] = root_parts[p][q]
-    core = place_ref[2 * parts]
-    half = len(TILES) // 2
-    for b, (i, j) in enumerate(TILES):
-        top, side = slice(i * BLOCK, (i + 1) * BLOCK), slice(j * BLOCK, (j + 1) * BLOCK)
-        square = lax.dot_general(
-            lead_ref[top, :], lead_ref[side, :], (((1,), (1,)), ((), ())), preferred_element_type=F32
-        )
-        value = root_ref[top, side] + gram_ref[top, side] - square
-        keep = core == b // half
-        at = slice(b % half * BLOCK, (b % half + 1) * BLOCK)
-
-        @pl.when(keep)
-        def _():
-            mine_ref[at, :] = value
-
-        @pl.when(jnp.logical_not(keep))
-        def _():
-            theirs_ref[at, :] = value
-
-
-def panel_halves(place, gram, leads, roots):
+            lead_ref[pl.ds(at, rows), :] = part[q]
+    rows_ref[...] = base_ref[...] - lax.dot_general(
+        head_ref[...], lead_ref[...], (((1,), (1,)), ((), ())), preferred_element_type=F32
+    )
+    half = rows // 2
+    own = pl.multiple_of(place_ref[2 * len(lead_parts)], half)
+    mine_ref[...] = rows_ref[pl.ds(own, half), :]
+    theirs_ref[...] = rows_ref[pl.ds(pl.multiple_of(half - own, half), half), :]
+
+
+def panel_rows(place, head, base, leads):
     vmem = pl.BlockSpec(memory_space=pltpu.VMEM)
-    n = gram.shape[0]
-    half = jax.ShapeDtypeStruct((len(TILES) // 2 * BLOCK, BLOCK), F32)
+    rows, n = base.shape
+    half = jax.ShapeDtypeStruct((rows // 2, n), F32)
     return pl.pallas_call(
         panel_kernel,
-        out_shape=(half, half, jax.ShapeDtypeStruct((n, leads[0].shape[-1]), BF16)),
-        in_specs=[pl.BlockSpec(memory_space=pltpu.SMEM)] + [vmem] * (1 + len(leads) + len(roots)),
+        out_shape=(half, half, jax.ShapeDtypeStruct((n, head.shape[-1]), BF16)),
+        in_specs=[pl.BlockSpec(memory_space=pltpu.SMEM)] + [vmem] * (2 + len(leads)),
         out_specs=(vmem, vmem, vmem),
-        scratch_shapes=[pltpu.VMEM((n, n), F32)],
-        cost_estimate=pl.CostEstimate(flops=2_000_000, bytes_accessed=4 * n * n * 4, transcendentals=0),
+        scratch_shapes=[pltpu.VMEM((rows, n), F32)],
+        cost_estimate=pl.CostEstimate(flops=1_000_000, bytes_accessed=4 * rows * n * 4, transcendentals=0),
         compiler_params=pltpu.CompilerParams(vmem_limit_bytes=12 * 2**20),
-        name="panel_halves",
-    )(place, gram, *leads, *roots)
+        name="panel_rows",
+    )(place, head, base, *leads)
 
 
 def coupling_kernel(core_ref, border_ref, solved_ref, sent_ref, kept_ref):
@@ -265,16 +237,8 @@
 
 
 def plane_parts(value):
-    return shifts(jnp.stack([value, swapped(value, "col")]), "row")
-
-
-def plane_parts_of_first(value):
-    rows = lax.axis_size("row")
-    pairs = jnp.stack([value, lax.ppermute(value, (*SCEN, "col"), [(0, 1), (1, 0)])])
-    return [pairs] + [
-        lax.ppermute(pairs, (*SCEN, "row"), [(i, (i + step) % rows) for i in range(rows)])
-        for step in range(1, rows)
-    ]
+    pairs = jnp.stack([value, swapped(value, "col")])
+    return shifts(pairs, "row")
 
 
 def part_places(rows):
@@ -283,26 +247,6 @@
     row = lax.rem(lax.axis_index("row") + (peers - part // 2), peers)
     col = lax.rem(lax.axis_index("col") + part % 2, 2)
     return (row * 2 + col) * rows
-
-
-def piece_places(core, size):
-    across, down = lax.axis_size("scen_1"), lax.axis_size("scen_0")
-    piece = np.arange(2 * across * down)
-    side = lax.rem(core + piece // (across * down), 2)
-    x = lax.rem(lax.axis_index("scen_1") + (across - piece // down % across), across)
-    y = lax.rem(lax.axis_index("scen_0") + (down - piece % down), down)
-    return ((side * across + x) * down + y) * size
-
-
-def scattered_sum(value, axis):
-    peers = lax.axis_size(axis)
-    place = lax.axis_index(axis)
-    size = value.shape[0] // peers
-    total = lax.dynamic_slice_in_dim(value, place * size, size, 0)
-    for step in range(1, peers):
-        piece = lax.dynamic_slice_in_dim(value, lax.rem(place + step, peers) * size, size, 0)
-        total = total + lax.ppermute(piece, axis, [(i, (i + step) % peers) for i in range(peers)])
-    return total
 
 
 def exchanged(pieces, axis):
@@ -347,10 +291,9 @@
     col = lax.axis_index("col")
     chips = lax.axis_size(CHIPS)
     rows = border.shape[2]
-    width = panel_border.shape[2]
+    plane = lax.axis_index(("row", "col"))
 
     theirs = swapped(half_of(factor, 0, 1 - col), "col")
-    roots = plane_parts_of_first(jnp.where(scen == 0, root_block, 0.0))
     solved = jnp.einsum(
         "snm,smp->snp", kinv, panel_border, preferred_element_type=F32
     ).astype(BF16)
@@ -359,20 +302,25 @@
     slices = exchanged(slices, CHIPS)
     halves = border.reshape(border.shape[0], chips, 2, rows, border.shape[3])
     sent, kept = coupling_halves(core.reshape(1), halves, solved)
-    gram = jnp.einsum("snr,snp->rp", solved, panel_border, preferred_element_type=F32)
-    slices, sent, kept, gram, roots = lax.optimization_barrier((slices, sent, kept, gram, roots))
+    slices, sent, kept = lax.optimization_barrier((slices, sent, kept))
     bulk = kept + swapped(sent, CORE)
 
     keep, send = ordered(slices[0, 0], slices[0, 1], col)
     head = jnp.where(core == 0, keep, lax.ppermute(send, CORE, [(0, 1)]))
-    place = jnp.concatenate([part_places(rows).astype(jnp.int32), core.reshape(1)])
-    mine, theirs, leading = panel_halves(place, gram, plane_parts(head), roots)
-    piece = mine + swapped(theirs, CORE)
-    piece = scattered_sum(piece, "scen_1")
-    piece = scattered_sum(piece, "scen_0")
-    place = piece_places(core, piece.shape[0]).astype(jnp.int32)
-    own = shifts(jnp.concatenate(shifts(piece, "scen_0")), "scen_1")
-    inverse = inverse_factor(place, own + [swapped(part, CORE) for part in own], width)
+    own_solved = lax.dynamic_slice_in_dim(solved, plane * rows, rows, 2)
+    base = jnp.einsum("snr,snp->rp", own_solved, panel_border, preferred_element_type=F32)
+    base = base + jnp.where(scen == 0, root_block, 0.0)
+    places = part_places(rows).astype(jnp.int32)
+    offset = core.reshape(1) * (rows // 2)
+    mine, theirs, leading = panel_rows(
+        jnp.concatenate([places, offset]), head, base, plane_parts(head)
+    )
+    panel = mine + swapped(theirs, CORE)
+    panel = sum(shifts(panel, "scen_1"))
+    panel = sum(shifts(panel, "scen_0"))
+    own = plane_parts(panel)
+    places = jnp.concatenate([places + offset, places + (rows // 2 - offset)])
+    inverse = inverse_factor(places, own + [swapped(part, CORE) for part in own])
 
     leads = ordered(leading, swapped(leading, CORE), core)
     leads = ordered(*leads, col)

time: 146 us -> 134 us (0.918); the launches traced: 146 us -> 132 us
  starting transfers between devices: 74.4 us -> 61.1 us
  waiting for transfers between devices: 14.8 us -> 21.8 us
  Pallas kernels: 38.2 us -> 35.4 us
  matrix products: 13.1 us -> 10.7 us
  other arithmetic: 3.09 us -> 1.63 us
    ppermute x10 -> x0, starting transfers between devices: 14.9 us -> none  [the longest x6 10 us: scattered_sum(): lax.ppermute(piece, axis, [(i, (i + step) % peers) for i in range(peers)])]
    ppermute x9 -> x10, starting transfers between devices: 26.2 us -> 20.8 us  [swapped(): return lax.ppermute(value, axis, [(0, 1), (1, 0)])]
    ppermute x9 -> x12, waiting for transfers between devices: 6.76 us -> 12 us  [shifts(): lax.ppermute(value, axis, [(i, (i + step) % peers) for i in range(peers)])]
    ppermute x9 -> x12, starting transfers between devices: 20.5 us -> 25.3 us  [shifts(): lax.ppermute(value, axis, [(i, (i + step) % peers) for i in range(peers)])]
    ppermute x9 -> x10, waiting for transfers between devices: 3.7 us -> 6.61 us  [swapped(): return lax.ppermute(value, axis, [(0, 1), (1, 0)])]
    pallas_call x1, Pallas kernels: 3.51 us -> 0.74 us  [panel_rows(): pl.pallas_call(panel_kernel, out_shape=(half, half, jax.ShapeDtypeStruct(...]
    ppermute x10 -> x0, waiting for transfers between devices: 2.34 us -> none  [the longest x6 2.33 us: scattered_sum(): lax.ppermute(piece, axis, [(i, (i + step) % peers) for i in range(peers)])]
    all_to_all x2, starting transfers between devices: 11.5 us -> 13.6 us  [exchanged(): return lax.all_to_all(pieces, axis, 0, 0, tiled=True)]
  transfers between devices with their start and end apart: 31 -> 25, of which waited for: 10 -> 13; matrix products, arithmetic and copies ran while one was open for 10% -> 7% of each run, Pallas kernels for 26% -> 26%
where the time goes in v4:
time: 134 us; the launch traced here: 132 us
  starting transfers between devices  61.1 us (46%)
  Pallas kernels  35.4 us (26%)
  waiting for transfers between devices  21.8 us (16%)
  matrix products  10.7 us (8%)
  other arithmetic  1.63 us (1%)
    ppermute x12, starting transfers between devices, shifts(): lax.ppermute(value, axis, [(i, (i + step) % peers) for i in range(peers)])  25.3 us
    pallas_call x1, Pallas kernels, inverse_factor(): pl.pallas_call(inverse_kernel, out_shape=jax.ShapeDtypeStruct((n, n), F32...  24.2 us
    ppermute x10, starting transfers between devices, swapped(): return lax.ppermute(value, axis, [(0, 1), (1, 0)])  20.8 us
    all_to_all x2, starting transfers between devices, exchanged(): return lax.all_to_all(pieces, axis, 0, 0, tiled=True)  13.6 us
    ppermute x12, waiting for transfers between devices, shifts(): lax.ppermute(value, axis, [(i, (i + step) % peers) for i in range(peers)])  12 us
    pallas_call x1, Pallas kernels, coupling_halves(): pl.pallas_call(coupling_kernel, out_shape=(half, half), grid_spec=grid_sp...  9.61 us
    ppermute x10, waiting for transfers between devices, swapped(): return lax.ppermute(value, axis, [(0, 1), (1, 0)])  6.61 us
    dot_general x1, matrix products, per_device(): jnp.einsum('snm,smp->snp', kinv, panel_border, preferred_element_type=F32)  4.26 us
  transfers between devices with their start and end apart: 25, of which 13 were waited for; matrix products, arithmetic and copies ran while one was open for 7% of the time, Pallas kernels for 26%

profile of v4, /device:TPU:1, one launch (start us, length us, event | category | flops | bytes accessed | tf_op | source)
XLA Modules:
  0.0 132.0 jit_solution(1620002290907829454)
XLA Ops:
  0.0 1.1 constant_dynamic-slice_fusion
  1.1 2.5 %collective-permute-start = (bf16[64,2048]{1,0:T(8,128)(2,1)S(1)}, bf16[64,2048]{1,0:T(8,128)(2,1)S(1)}, u32[]{:S(2)}, u32[]{:S(2)}) collective-permute-start(bf16[64,2048]{1,0:T(8,128)(2,1)S(1)} %constant_dynamic-slice_fusion), channel_id=1, source_target_pairs={{0,1},{1,0},{2,3},{3,2},{4,5},{5,4},{6,7},{7,6},{8,9},{9,8},{10,11... | collective-permute-start | bytes 786440 | tf_op jit(solution)/shard_map/ppermute | solution.py:228
  3.7 4.3 %convolution_convert_fusion.solved_ref = bf16[4,512,512]{2,1,0:T(8,128)(2,1)} fusion(bf16[4,512,512]{2,1,0:T(8,128)(2,1)} %param.9, bf16[4,512,512]{2,1,0:T(8,128)(2,1)S(1)} %copy-done), kind=kOutput, calls=%fused_computation.2 | convolution fusion | flops 1074790400 | bytes 6291456 | tf_op jit(solution)/shard_map/snm,smp->snp/dot_general | solution.py:297
  7.9 0.7 collective-permute-done.theirs_ref
  8.7 0.9 packed.1
  9.6 7.7 %all-to-all-start = ((bf16[16,2,64,128]{3,2,1,0:T(8,128)(2,1)}), bf16[16,2,64,128]{3,2,1,0:T(8,128)(2,1)S(1)}, u32[]{:S(2)}, u32[]{:S(2)}) async-start(bf16[16,2,64,128]{3,2,1,0:T(8,128)(2,1)} %packed.1), calls=%async_computation | async-start | bytes 1048576 | tf_op jit(solution)/shard_map/all_to_all | solution.py:253
  17.3 9.6 %coupling_halves.1 = (f32[16,64,512]{2,1,0:T(8,128)}, f32[16,64,512]{2,1,0:T(8,128)}) custom-call(s32[1]{0:T(128)} %bitcast.1.core_ref, bf16[4,16,2,64,512]{4,3,2,1,0:T(8,128)(2,1)} %bitcast.39, bf16[4,512,512]{2,1,0:T(8,128)(2,1)} %convolution_convert_fusion.solved_ref), custom_call_target="tpu_custom_call" | custom-call | flops 4294967296 | bytes 12582912 | tf_op jit(solution)/shard_map/coupling_halves/pallas_call | solution.py:213
  26.9 0.5 all-to-all-done
  27.4 2.3 %collective-permute-start.1 = (f32[16,64,512]{2,1,0:T(8,128)}, f32[16,64,512]{2,1,0:T(8,128)}, u32[]{:S(2)}, u32[]{:S(2)}) collective-permute-start(f32[16,64,512]{2,1,0:T(8,128)} %get-tuple-element.20), channel_id=1, source_target_pairs={{0,8},{8,0},{1,9},{9,1},{2,10},{10,2},{3,11},{11,3},{4,12},{12,4},... | collective-permute-start | bytes 6291464 | tf_op jit(solution)/shard_map/ppermute | solution.py:228
  29.7 1.3 collective-permute-start.2
  31.1 2.7 %collective-permute-done.2 = bf16[64,128]{1,0:T(8,128)(2,1)S(1)} collective-permute-done((bf16[64,128]{1,0:T(8,128)(2,1)S(1)}, bf16[64,128]{1,0:T(8,128)(2,1)S(1)}, u32[]{:S(2)}, u32[]{:S(2)}) %collective-permute-start.2) | collective-permute-done | bytes 16416 | tf_op jit(solution)/shard_map/ppermute | solution.py:309
  33.7 1.3 %collective-permute-start.3 = (bf16[64,128]{1,0:T(8,128)(2,1)S(1)}, bf16[64,128]{1,0:T(8,128)(2,1)S(1)}, u32[]{:S(2)}, u32[]{:S(2)}) collective-permute-start(bf16[64,128]{1,0:T(8,128)(2,1)S(1)} %bitcast_select_fusion.head_ref), channel_id=1, source_target_pairs={{0,1},{1,0},{2,3},{3,2},{4,5},{5,4},{6,7},{7,6},{8,9},{9,8},{10,11... | collective-permute-start | bytes 49160 | tf_op jit(solution)/shard_map/ppermute | solution.py:228
  35.1 1.2 collective-permute-done.3
  36.3 3.0 %collective-permute-start.4 = (bf16[2,64,128]{2,1,0:T(8,128)(2,1)S(1)}, bf16[2,64,128]{2,1,0:T(8,128)(2,1)S(1)}, u32[]{:S(2)}, u32[]{:S(2)}) collective-permute-start(bf16[2,64,128]{2,1,0:T(8,128)(2,1)S(1)} %pad_maximum_fusion.1.refs_0_), channel_id=1, source_target_pairs={{0,2},{2,4},{4,6},{6,0},{1,3},{3,5},{5,7},{7,1},{8,10},{10,12},{12... | collective-permute-start | bytes 98312 | tf_op jit(solution)/shard_map/ppermute | solution.py:234
  39.3 4.8 %collective-permute-start.5 = (bf16[2,64,128]{2,1,0:T(8,128)(2,1)S(1)}, bf16[2,64,128]{2,1,0:T(8,128)(2,1)S(1)}, u32[]{:S(2)}, u32[]{:S(2)}) collective-permute-start(bf16[2,64,128]{2,1,0:T(8,128)(2,1)S(1)} %pad_maximum_fusion.1.refs_0_), channel_id=1, source_target_pairs={{0,4},{2,6},{4,0},{6,2},{1,5},{3,7},{5,1},{7,3},{8,12},{10,14},{12... | collective-permute-start | bytes 98312 | tf_op jit(solution)/shard_map/ppermute | solution.py:234
  44.1 2.4 %collective-permute-start.6 = (bf16[2,64,128]{2,1,0:T(8,128)(2,1)S(1)}, bf16[2,64,128]{2,1,0:T(8,128)(2,1)S(1)}, u32[]{:S(2)}, u32[]{:S(2)}) collective-permute-start(bf16[2,64,128]{2,1,0:T(8,128)(2,1)S(1)} %pad_maximum_fusion.1.refs_0_), channel_id=1, source_target_pairs={{0,6},{2,0},{4,2},{6,4},{1,7},{3,1},{5,3},{7,5},{8,14},{10,8},{12,... | collective-permute-start | bytes 98312 | tf_op jit(solution)/shard_map/ppermute | solution.py:234
  46.5 1.7 %fusion.base_ref = f32[64,512]{1,0:T(8,128)S(1)} fusion(bf16[4,512,512]{2,1,0:T(8,128)(2,1)S(1)} %copy-done, bf16[4,512,512]{2,1,0:T(8,128)(2,1)} %convolution_convert_fusion.solved_ref, s32[]{:T(128)S(6)} %select_n.70, f32[64,512]{1,0:T(8,128)S(1)} %copy-done.3, pred[]{:T(512)S(6)} %eq.16), kind=kOutput, calls=%fused_computation.4 | convolution fusion | flops 134283264 | bytes 2883589 | tf_op jit(solution)/shard_map/snr,snp->rp/dot_general | solution.py:311
  48.3 0.1 collective-permute-done.6.refs_3_
  48.4 0.7 panel_rows.1
  49.2 2.5 %collective-permute-start.7 = (bf16[512,128]{1,0:T(8,128)(2,1)S(1)}, bf16[512,128]{1,0:T(8,128)(2,1)S(1)}, u32[]{:S(2)}, u32[]{:S(2)}) collective-permute-start(bf16[512,128]{1,0:T(8,128)(2,1)S(1)} %get-tuple-element.22), channel_id=1, source_target_pairs={{0,8},{8,0},{1,9},{9,1},{2,10},{10,2},{3,11},{11,3},{4,12},{12,4},... | collective-permute-start | bytes 393224 | tf_op jit(solution)/shard_map/ppermute | solution.py:228
  51.6 0.1 collective-permute-start.8
  51.7 1.2 collective-permute-done.8
  52.9 2.2 %collective-permute-start.10 = (f32[32,512]{1,0:T(8,128)S(1)}, f32[32,512]{1,0:T(8,128)S(1)}, u32[]{:S(2)}, u32[]{:S(2)}) collective-permute-start(f32[32,512]{1,0:T(8,128)S(1)} %add.99), channel_id=1, source_target_pairs={{0,32},{16,48},{32,0},{48,16},{1,33},{17,49},{33,1},{49,17},{2,34}... | collective-permute-start | bytes 196616 | tf_op jit(solution)/shard_map/ppermute | solution.py:234
  55.0 0.9 collective-permute-start.11
  55.9 0.6 collective-permute-start.9
  56.5 0.4 fusion.6
  57.0 3.0 %subtract_convert_fusion = bf16[16,64,512]{2,1,0:T(8,128)(2,1)} fusion(f32[16,64,512]{2,1,0:T(8,128)S(1)} %fusion.6, f32[16,64,512]{2,1,0:T(8,128)S(1)} %copy-done.2, f32[16,64,512]{2,1,0:T(8,128)} %collective-permute-done.1, bf16[16,2,64,128]{3,2,1,0:T(8,128)(2,1)S(1)} %all-to-all-done, pred[]{:T(512)S(6)} %eq.6, ...), kind=kOutput, calls=%fused_computation.1 | convolution fusion | flops 136511488 | bytes 7864322 | tf_op jit(solution)/shard_map/dot_general | solution.py:328
  60.0 5.9 %all-to-all-start.1 = ((bf16[16,64,512]{2,1,0:T(8,128)(2,1)}), bf16[16,64,512]{2,1,0:T(8,128)(2,1)}, u32[]{:S(2)}, u32[]{:S(2)}) async-start(bf16[16,64,512]{2,1,0:T(8,128)(2,1)} %subtract_convert_fusion), calls=%async_computation.1 | async-start | bytes 2097152 | tf_op jit(solution)/shard_map/all_to_all | solution.py:253
  66.0 1.4 %collective-permute-start.12 = (f32[32,512]{1,0:T(8,128)S(1)}, f32[32,512]{1,0:T(8,128)S(1)}, u32[]{:S(2)}, u32[]{:S(2)}) collective-permute-start(f32[32,512]{1,0:T(8,128)S(1)} %add_add_fusion.1), channel_id=1, source_target_pairs={{0,64},{64,128},{128,192},{192,0},{1,65},{65,129},{129,193},{193,1... | collective-permute-start | bytes 196616 | tf_op jit(solution)/shard_map/ppermute | solution.py:234
  67.4 2.4 %collective-permute-start.13 = (f32[32,512]{1,0:T(8,128)S(1)}, f32[32,512]{1,0:T(8,128)S(1)}, u32[]{:S(2)}, u32[]{:S(2)}) collective-permute-start(f32[32,512]{1,0:T(8,128)S(1)} %add_add_fusion.1), channel_id=1, source_target_pairs={{0,128},{64,192},{128,0},{192,64},{1,129},{65,193},{129,1},{193,65... | collective-permute-start | bytes 196616 | tf_op jit(solution)/shard_map/ppermute | solution.py:234
  69.8 1.2 collective-permute-start.14
  71.0 1.9 %collective-permute-done.12 = f32[32,512]{1,0:T(8,128)S(1)} collective-permute-done((f32[32,512]{1,0:T(8,128)S(1)}, f32[32,512]{1,0:T(8,128)S(1)}, u32[]{:S(2)}, u32[]{:S(2)}) %collective-permute-start.12) | collective-permute-done | bytes 65568 | tf_op jit(solution)/shard_map/ppermute | solution.py:234
  72.8 8.7 %collective-permute-done.13 = f32[32,512]{1,0:T(8,128)S(1)} collective-permute-done((f32[32,512]{1,0:T(8,128)S(1)}, f32[32,512]{1,0:T(8,128)S(1)}, u32[]{:S(2)}, u32[]{:S(2)}) %collective-permute-start.13) | collective-permute-done | bytes 65568 | tf_op jit(solution)/shard_map/ppermute | solution.py:234
  81.5 0.4 collective-permute-done.14
  81.9 0.8 collective-permute-start.15
  82.8 2.4 %collective-permute-done.15 = f32[32,512]{1,0:T(8,128)S(1)} collective-permute-done((f32[32,512]{1,0:T(8,128)S(1)}, f32[32,512]{1,0:T(8,128)S(1)}, u32[]{:S(2)}, u32[]{:S(2)}) %collective-permute-start.15) | collective-permute-done | bytes 65568 | tf_op jit(solution)/shard_map/ppermute | solution.py:228
  85.1 1.9 %collective-permute-start.16 = (f32[2,32,512]{2,1,0:T(8,128)S(1)}, f32[2,32,512]{2,1,0:T(8,128)S(1)}, u32[]{:S(2)}, u32[]{:S(2)}) collective-permute-start(f32[2,32,512]{2,1,0:T(8,128)S(1)} %pad_maximum_fusion.refs_0_), channel_id=1, source_target_pairs={{0,2},{2,4},{4,6},{6,0},{1,3},{3,5},{5,7},{7,1},{8,10},{10,12},{12... | collective-permute-start | bytes 393224 | tf_op jit(solution)/shard_map/ppermute | solution.py:234
  87.0 3.8 %collective-permute-start.17 = (f32[2,32,512]{2,1,0:T(8,128)S(1)}, f32[2,32,512]{2,1,0:T(8,128)S(1)}, u32[]{:S(2)}, u32[]{:S(2)}) collective-permute-start(f32[2,32,512]{2,1,0:T(8,128)S(1)} %pad_maximum_fusion.refs_0_), channel_id=1, source_target_pairs={{0,4},{2,6},{4,0},{6,2},{1,5},{3,7},{5,1},{7,3},{8,12},{10,14},{12... | collective-permute-start | bytes 393224 | tf_op jit(solution)/shard_map/ppermute | solution.py:234
  90.9 0.8 collective-permute-start.18
  91.7 4.8 %collective-permute-start.19 = (f32[2,32,512]{2,1,0:T(8,128)S(1)}, f32[2,32,512]{2,1,0:T(8,128)S(1)}, u32[]{:S(2)}, u32[]{:S(2)}) collective-permute-start(f32[2,32,512]{2,1,0:T(8,128)S(1)} %pad_maximum_fusion.refs_0_), channel_id=1, source_target_pairs={{0,8},{8,0},{1,9},{9,1},{2,10},{10,2},{3,11},{11,3},{4,12},{12,4},... | collective-permute-start | bytes 393224 | tf_op jit(solution)/shard_map/ppermute | solution.py:228
  96.6 0.9 collective-permute-start.20
  97.5 0.9 collective-permute-done.17.refs_2_
  98.4 5.4 %collective-permute-start.21 = (f32[2,32,512]{2,1,0:T(8,128)S(1)}, f32[2,32,512]{2,1,0:T(8,128)S(1)}, u32[]{:S(2)}, u32[]{:S(2)}) collective-permute-start(f32[2,32,512]{2,1,0:T(8,128)S(1)} %collective-permute-done.17.refs_2_), channel_id=1, source_target_pairs={{0,8},{8,0},{1,9},{9,1},{2,10},{10,2},{3,11},{11,3},{4,12},{12,4},... | collective-permute-start | bytes 393224 | tf_op jit(solution)/shard_map/ppermute | solution.py:228
  104.0 0.8 collective-permute-done.21.refs_6_
  104.8 0.4 collective-permute-done.22.refs_7_
  105.1 24.2 %inverse_factor.1 = f32[512,512]{1,0:T(8,128)S(1)} custom-call(s32[16]{0:T(128)S(1)} %pad_add_fusion.1.place_ref, f32[2,32,512]{2,1,0:T(8,128)S(1)} %pad_maximum_fusion.refs_0_, f32[2,32,512]{2,1,0:T(8,128)S(1)} %collective-permute-done.16.refs_1_, f32[2,32,512]{2,1,0:T(8,128)S(1)} %collective-permute-done.17.refs_2_, ...), custom_call_target="tpu_custom_call" | custom-call | flops 40000000 | bytes 2097152 | tf_op jit(solution)/shard_map/inverse_factor/pallas_call | solution.py:133
  129.3 1.4 %convert_reduce_fusion = f32[64,512]{1,0:T(8,128)S(1)} fusion(bf16[16,64,512]{2,1,0:T(8,128)(2,1)} %all-to-all-done.1), kind=kLoop, calls=%fused_computation | loop fusion | flops 1015808 | bytes 1179648 | tf_op jit(solution)/shard_map/reduce_sum | solution.py:332
  130.7 1.3 fusion.12
  (36 shorter events, 0.4 us)
Async XLA Ops:
  0.0 3.7 %copy-start = (bf16[4,512,512]{2,1,0:T(8,128)(2,1)S(1)}, bf16[4,512,512]{2,1,0:T(8,128)(2,1)}, u32[]{:S(2)}) copy-start(bf16[4,512,512]{2,1,0:T(8,128)(2,1)} %param.8) | copy-start | bytes 6291460
  1.1 7.5 %collective-permute-start = (bf16[64,2048]{1,0:T(8,128)(2,1)S(1)}, bf16[64,2048]{1,0:T(8,128)(2,1)S(1)}, u32[]{:S(2)}, u32[]{:S(2)}) collective-permute-start(bf16[64,2048]{1,0:T(8,128)(2,1)S(1)} %constant_dynamic-slice_fusion), channel_id=1, source_target_pairs={{0,1},{1,0},{2,3},{3,2},{4,5},{5,4},{6,7},{7,6},{8,9},{9,8},{10,11... | collective-permute-start | bytes 786440 | tf_op jit(solution)/shard_map/ppermute | solution.py:228
  3.7 5.0 %copy-start.1 = (bf16[128,2048]{1,0:T(8,128)(2,1)S(1)}, bf16[128,2048]{1,0:T(8,128)(2,1)}, u32[]{:S(2)}) copy-start(bf16[128,2048]{1,0:T(8,128)(2,1)} %factor_ref.1) | copy-start | bytes 1572868
  9.6 17.8 %all-to-all-start = ((bf16[16,2,64,128]{3,2,1,0:T(8,128)(2,1)}), bf16[16,2,64,128]{3,2,1,0:T(8,128)(2,1)S(1)}, u32[]{:S(2)}, u32[]{:S(2)}) async-start(bf16[16,2,64,128]{3,2,1,0:T(8,128)(2,1)} %packed.1), calls=%async_computation | async-start | bytes 1048576 | tf_op jit(solution)/shard_map/all_to_all | solution.py:253
  17.2 13.8 %copy-start.4 = (s32[8]{0:T(128)S(1)}, s32[8]{0:T(128)}, u32[]{:S(2)}) copy-start(s32[8]{0:T(128)} %constant.49.clone) | copy-start | bytes 100
  17.3 13.8 %copy-start.5 = (s32[8]{0:T(128)S(1)}, s32[8]{0:T(128)}, u32[]{:S(2)}) copy-start(s32[8]{0:T(128)} %constant.50.clone) | copy-start | bytes 100
  17.3 29.2 %copy-start.3 = (f32[64,512]{1,0:T(8,128)S(1)}, f32[64,512]{1,0:T(8,128)}, u32[]{:S(2)}) copy-start(f32[64,512]{1,0:T(8,128)} %param.11) | copy-start | bytes 393220
  27.4 29.6 %collective-permute-start.1 = (f32[16,64,512]{2,1,0:T(8,128)}, f32[16,64,512]{2,1,0:T(8,128)}, u32[]{:S(2)}, u32[]{:S(2)}) collective-permute-start(f32[16,64,512]{2,1,0:T(8,128)} %get-tuple-element.20), channel_id=1, source_target_pairs={{0,8},{8,0},{1,9},{9,1},{2,10},{10,2},{3,11},{11,3},{4,12},{12,4},... | collective-permute-start | bytes 6291464 | tf_op jit(solution)/shard_map/ppermute | solution.py:228
  29.7 4.0 %collective-permute-start.2 = (bf16[64,128]{1,0:T(8,128)(2,1)S(1)}, bf16[64,128]{1,0:T(8,128)(2,1)S(1)}, u32[]{:S(2)}, u32[]{:S(2)}) collective-permute-start(bf16[64,128]{1,0:T(8,128)(2,1)S(1)} %select_bitcast_fusion), channel_id=1, source_target_pairs={{0,8},{1,9},{2,10},{3,11},{4,12},{5,13},{6,14},{7,15},{16,24},{17,... | collective-permute-start | bytes 49160 | tf_op jit(solution)/shard_map/ppermute | solution.py:309
  33.7 2.6 %collective-permute-start.3 = (bf16[64,128]{1,0:T(8,128)(2,1)S(1)}, bf16[64,128]{1,0:T(8,128)(2,1)S(1)}, u32[]{:S(2)}, u32[]{:S(2)}) collective-permute-start(bf16[64,128]{1,0:T(8,128)(2,1)S(1)} %bitcast_select_fusion.head_ref), channel_id=1, source_target_pairs={{0,1},{1,0},{2,3},{3,2},{4,5},{5,4},{6,7},{7,6},{8,9},{9,8},{10,11... | collective-permute-start | bytes 49160 | tf_op jit(solution)/shard_map/ppermute | solution.py:228
  36.3 11.9 %collective-permute-start.4 = (bf16[2,64,128]{2,1,0:T(8,128)(2,1)S(1)}, bf16[2,64,128]{2,1,0:T(8,128)(2,1)S(1)}, u32[]{:S(2)}, u32[]{:S(2)}) collective-permute-start(bf16[2,64,128]{2,1,0:T(8,128)(2,1)S(1)} %pad_maximum_fusion.1.refs_0_), channel_id=1, source_target_pairs={{0,2},{2,4},{4,6},{6,0},{1,3},{3,5},{5,7},{7,1},{8,10},{10,12},{12... | collective-permute-start | bytes 98312 | tf_op jit(solution)/shard_map/ppermute | solution.py:234
  39.3 8.9 %collective-permute-start.5 = (bf16[2,64,128]{2,1,0:T(8,128)(2,1)S(1)}, bf16[2,64,128]{2,1,0:T(8,128)(2,1)S(1)}, u32[]{:S(2)}, u32[]{:S(2)}) collective-permute-start(bf16[2,64,128]{2,1,0:T(8,128)(2,1)S(1)} %pad_maximum_fusion.1.refs_0_), channel_id=1, source_target_pairs={{0,4},{2,6},{4,0},{6,2},{1,5},{3,7},{5,1},{7,3},{8,12},{10,14},{12... | collective-permute-start | bytes 98312 | tf_op jit(solution)/shard_map/ppermute | solution.py:234
  44.1 4.3 %collective-permute-start.6 = (bf16[2,64,128]{2,1,0:T(8,128)(2,1)S(1)}, bf16[2,64,128]{2,1,0:T(8,128)(2,1)S(1)}, u32[]{:S(2)}, u32[]{:S(2)}) collective-permute-start(bf16[2,64,128]{2,1,0:T(8,128)(2,1)S(1)} %pad_maximum_fusion.1.refs_0_), channel_id=1, source_target_pairs={{0,6},{2,0},{4,2},{6,4},{1,7},{3,1},{5,3},{7,5},{8,14},{10,8},{12,... | collective-permute-start | bytes 98312 | tf_op jit(solution)/shard_map/ppermute | solution.py:234
  48.2 8.7 %copy-start.2 = (f32[16,64,512]{2,1,0:T(8,128)S(1)}, f32[16,64,512]{2,1,0:T(8,128)}, u32[]{:S(2)}) copy-start(f32[16,64,512]{2,1,0:T(8,128)} %get-tuple-element.19) | copy-start | bytes 6291460
  49.2 7.4 %collective-permute-start.7 = (bf16[512,128]{1,0:T(8,128)(2,1)S(1)}, bf16[512,128]{1,0:T(8,128)(2,1)S(1)}, u32[]{:S(2)}, u32[]{:S(2)}) collective-permute-start(bf16[512,128]{1,0:T(8,128)(2,1)S(1)} %get-tuple-element.22), channel_id=1, source_target_pairs={{0,8},{8,0},{1,9},{9,1},{2,10},{10,2},{3,11},{11,3},{4,12},{12,4},... | collective-permute-start | bytes 393224 | tf_op jit(solution)/shard_map/ppermute | solution.py:228
  51.6 1.3 collective-permute-start.8
  52.9 13.1 %collective-permute-start.10 = (f32[32,512]{1,0:T(8,128)S(1)}, f32[32,512]{1,0:T(8,128)S(1)}, u32[]{:S(2)}, u32[]{:S(2)}) collective-permute-start(f32[32,512]{1,0:T(8,128)S(1)} %add.99), channel_id=1, source_target_pairs={{0,32},{16,48},{32,0},{48,16},{1,33},{17,49},{33,1},{49,17},{2,34}... | collective-permute-start | bytes 196616 | tf_op jit(solution)/shard_map/ppermute | solution.py:234
  55.0 10.9 %collective-permute-start.11 = (f32[32,512]{1,0:T(8,128)S(1)}, f32[32,512]{1,0:T(8,128)S(1)}, u32[]{:S(2)}, u32[]{:S(2)}) collective-permute-start(f32[32,512]{1,0:T(8,128)S(1)} %add.99), channel_id=1, source_target_pairs={{0,48},{16,0},{32,16},{48,32},{1,49},{17,1},{33,17},{49,33},{2,50}... | collective-permute-start | bytes 196616 | tf_op jit(solution)/shard_map/ppermute | solution.py:234
  55.9 10.0 %collective-permute-start.9 = (f32[32,512]{1,0:T(8,128)S(1)}, f32[32,512]{1,0:T(8,128)S(1)}, u32[]{:S(2)}, u32[]{:S(2)}) collective-permute-start(f32[32,512]{1,0:T(8,128)S(1)} %add.99), channel_id=1, source_target_pairs={{0,16},{16,32},{32,48},{48,0},{1,17},{17,33},{33,49},{49,1},{2,18}... | collective-permute-start | bytes 196616 | tf_op jit(solution)/shard_map/ppermute | solution.py:234
  60.0 69.3 %all-to-all-start.1 = ((bf16[16,64,512]{2,1,0:T(8,128)(2,1)}), bf16[16,64,512]{2,1,0:T(8,128)(2,1)}, u32[]{:S(2)}, u32[]{:S(2)}) async-start(bf16[16,64,512]{2,1,0:T(8,128)(2,1)} %subtract_convert_fusion), calls=%async_computation.1 | async-start | bytes 2097152 | tf_op jit(solution)/shard_map/all_to_all | solution.py:253
  66.0 6.8 %collective-permute-start.12 = (f32[32,512]{1,0:T(8,128)S(1)}, f32[32,512]{1,0:T(8,128)S(1)}, u32[]{:S(2)}, u32[]{:S(2)}) collective-permute-start(f32[32,512]{1,0:T(8,128)S(1)} %add_add_fusion.1), channel_id=1, source_target_pairs={{0,64},{64,128},{128,192},{192,0},{1,65},{65,129},{129,193},{193,1... | collective-permute-start | bytes 196616 | tf_op jit(solution)/shard_map/ppermute | solution.py:234
  67.4 14.1 %collective-permute-start.13 = (f32[32,512]{1,0:T(8,128)S(1)}, f32[32,512]{1,0:T(8,128)S(1)}, u32[]{:S(2)}, u32[]{:S(2)}) collective-permute-start(f32[32,512]{1,0:T(8,128)S(1)} %add_add_fusion.1), channel_id=1, source_target_pairs={{0,128},{64,192},{128,0},{192,64},{1,129},{65,193},{129,1},{193,65... | collective-permute-start | bytes 196616 | tf_op jit(solution)/shard_map/ppermute | solution.py:234
  69.8 12.1 %collective-permute-start.14 = (f32[32,512]{1,0:T(8,128)S(1)}, f32[32,512]{1,0:T(8,128)S(1)}, u32[]{:S(2)}, u32[]{:S(2)}) collective-permute-start(f32[32,512]{1,0:T(8,128)S(1)} %add_add_fusion.1), channel_id=1, source_target_pairs={{0,192},{64,0},{128,64},{192,128},{1,193},{65,1},{129,65},{193,129... | collective-permute-start | bytes 196616 | tf_op jit(solution)/shard_map/ppermute | solution.py:234
  81.9 3.2 %collective-permute-start.15 = (f32[32,512]{1,0:T(8,128)S(1)}, f32[32,512]{1,0:T(8,128)S(1)}, u32[]{:S(2)}, u32[]{:S(2)}) collective-permute-start(f32[32,512]{1,0:T(8,128)S(1)} %add_add_fusion), channel_id=1, source_target_pairs={{0,1},{1,0},{2,3},{3,2},{4,5},{5,4},{6,7},{7,6},{8,9},{9,8},{10,11... | collective-permute-start | bytes 196616 | tf_op jit(solution)/shard_map/ppermute | solution.py:228
  85.1 11.4 %collective-permute-start.16 = (f32[2,32,512]{2,1,0:T(8,128)S(1)}, f32[2,32,512]{2,1,0:T(8,128)S(1)}, u32[]{:S(2)}, u32[]{:S(2)}) collective-permute-start(f32[2,32,512]{2,1,0:T(8,128)S(1)} %pad_maximum_fusion.refs_0_), channel_id=1, source_target_pairs={{0,2},{2,4},{4,6},{6,0},{1,3},{3,5},{5,7},{7,1},{8,10},{10,12},{12... | collective-permute-start | bytes 393224 | tf_op jit(solution)/shard_map/ppermute | solution.py:234
  87.0 11.3 %collective-permute-start.17 = (f32[2,32,512]{2,1,0:T(8,128)S(1)}, f32[2,32,512]{2,1,0:T(8,128)S(1)}, u32[]{:S(2)}, u32[]{:S(2)}) collective-permute-start(f32[2,32,512]{2,1,0:T(8,128)S(1)} %pad_maximum_fusion.refs_0_), channel_id=1, source_target_pairs={{0,4},{2,6},{4,0},{6,2},{1,5},{3,7},{5,1},{7,3},{8,12},{10,14},{12... | collective-permute-start | bytes 393224 | tf_op jit(solution)/shard_map/ppermute | solution.py:234
  90.9 12.9 %collective-permute-start.18 = (f32[2,32,512]{2,1,0:T(8,128)S(1)}, f32[2,32,512]{2,1,0:T(8,128)S(1)}, u32[]{:S(2)}, u32[]{:S(2)}) collective-permute-start(f32[2,32,512]{2,1,0:T(8,128)S(1)} %pad_maximum_fusion.refs_0_), channel_id=1, source_target_pairs={{0,6},{2,0},{4,2},{6,4},{1,7},{3,1},{5,3},{7,5},{8,14},{10,8},{12,... | collective-permute-start | bytes 393224 | tf_op jit(solution)/shard_map/ppermute | solution.py:234
  91.7 12.2 %collective-permute-start.19 = (f32[2,32,512]{2,1,0:T(8,128)S(1)}, f32[2,32,512]{2,1,0:T(8,128)S(1)}, u32[]{:S(2)}, u32[]{:S(2)}) collective-permute-start(f32[2,32,512]{2,1,0:T(8,128)S(1)} %pad_maximum_fusion.refs_0_), channel_id=1, source_target_pairs={{0,8},{8,0},{1,9},{9,1},{2,10},{10,2},{3,11},{11,3},{4,12},{12,4},... | collective-permute-start | bytes 393224 | tf_op jit(solution)/shard_map/ppermute | solution.py:228
  96.6 7.4 %collective-permute-start.20 = (f32[2,32,512]{2,1,0:T(8,128)S(1)}, f32[2,32,512]{2,1,0:T(8,128)S(1)}, u32[]{:S(2)}, u32[]{:S(2)}) collective-permute-start(f32[2,32,512]{2,1,0:T(8,128)S(1)} %collective-permute-done.16.refs_1_), channel_id=1, source_target_pairs={{0,8},{8,0},{1,9},{9,1},{2,10},{10,2},{3,11},{11,3},{4,12},{12,4},... | collective-permute-start | bytes 393224 | tf_op jit(solution)/shard_map/ppermute | solution.py:228
  98.4 6.4 %collective-permute-start.21 = (f32[2,32,512]{2,1,0:T(8,128)S(1)}, f32[2,32,512]{2,1,0:T(8,128)S(1)}, u32[]{:S(2)}, u32[]{:S(2)}) collective-permute-start(f32[2,32,512]{2,1,0:T(8,128)S(1)} %collective-permute-done.17.refs_2_), channel_id=1, source_target_pairs={{0,8},{8,0},{1,9},{9,1},{2,10},{10,2},{3,11},{11,3},{4,12},{12,4},... | collective-permute-start | bytes 393224 | tf_op jit(solution)/shard_map/ppermute | solution.py:228
  103.8 1.3 %collective-permute-start.22 = (f32[2,32,512]{2,1,0:T(8,128)S(1)}, f32[2,32,512]{2,1,0:T(8,128)S(1)}, u32[]{:S(2)}, u32[]{:S(2)}) collective-permute-start(f32[2,32,512]{2,1,0:T(8,128)S(1)} %collective-permute-done.18.refs_3_), channel_id=1, source_target_pairs={{0,8},{8,0},{1,9},{9,1},{2,10},{10,2},{3,11},{11,3},{4,12},{12,4},... | collective-permute-start | bytes 393224 | tf_op jit(solution)/shard_map/ppermute | solution.py:228

commit v5 on v4

--- a/solution.py
+++ b/solution.py
@@ -34,8 +34,12 @@
     inverse = [jnp.where(lane == sub + 8 * g, 1.0, 0.0).astype(F32) for g in range(groups)]
     rows = list(rows)
     done = []
+    cols = [spread_lane(rows[0], j) for j in range(8)]
     for t in range(groups):
-        cols = [spread_lane(rows[t], 8 * t + j) for j in range(8)]
+        more = t + 1 < groups
+        if more:
+            extra = [spread_lane(rows[t], 8 * (t + 1) + j) for j in range(8)]
+            following = [spread_lane(rows[t + 1], 8 * (t + 1) + j) for j in range(8)]
         left, right = rows[t], inverse[t]
         ahead = inverse[t]
         scale = jnp.zeros(tile, F32)
@@ -49,6 +53,8 @@
             below = jnp.where(sub > k, full, 0.0)
             for j in range(k + 1, 8):
                 cols[j] = cols[j] - full * spread_row(cols[j], k)
+            if more:
+                extra = [e - full * spread_row(e, k) for e in extra]
             left = left - full * spread_row(left, k)
             right = right - full * spread_row(right, k)
             ahead = ahead - below * spread_row(ahead, k)
@@ -60,6 +66,14 @@
         rights = [spread_row(right, j) for j in range(8)]
         for g in range(t + 1, groups):
             coef = [spread_lane(rows[g], 8 * t + j) for j in range(8)]
+            if g == t + 1:
+                cols = []
+                for j in range(8):
+                    scaled = extra[j] * square
+                    terms = [coef[m] * spread_row(scaled, m) for m in range(8)]
+                    while len(terms) > 1:
+                        terms = [terms[i] + terms[i + 1] for i in range(0, len(terms), 2)]
+                    cols.append(following[j] - terms[0])
             a = [coef[j] * lefts[j] for j in range(8)]
             b = [coef[j] * rights[j] for j in range(8)]
             while len(a) > 1:

time: 134 us -> 126 us (0.940)
  Pallas kernels: 35.4 us -> 27.5 us
    pallas_call x1, Pallas kernels: 24.2 us -> 16.2 us  [inverse_factor(): pl.pallas_call(inverse_kernel, out_shape=jax.ShapeDtypeStruct((n, n), F32...]
  transfers between devices with their start and end apart: 25 -> 25, of which waited for: 13 -> 13; matrix products, arithmetic and copies ran while one was open for 7% -> 8% of each run, Pallas kernels for 26% -> 21%
where the time goes in v5:
time: 126 us; the launch traced here: 124 us
  starting transfers between devices  61.1 us (48%)
  Pallas kernels  27.5 us (22%)
  waiting for transfers between devices  21.8 us (17%)
  matrix products  10.7 us (8%)
  other arithmetic  1.63 us (1%)
    ppermute x12, starting transfers between devices, shifts(): lax.ppermute(value, axis, [(i, (i + step) % peers) for i in range(peers)])  25.3 us
    ppermute x10, starting transfers between devices, swapped(): return lax.ppermute(value, axis, [(0, 1), (1, 0)])  20.8 us
    pallas_call x1, Pallas kernels, inverse_factor(): pl.pallas_call(inverse_kernel, out_shape=jax.ShapeDtypeStruct((n, n), F32...  16.2 us
    all_to_all x2, starting transfers between devices, exchanged(): return lax.all_to_all(pieces, axis, 0, 0, tiled=True)  13.6 us
    ppermute x12, waiting for transfers between devices, shifts(): lax.ppermute(value, axis, [(i, (i + step) % peers) for i in range(peers)])  12 us
    pallas_call x1, Pallas kernels, coupling_halves(): pl.pallas_call(coupling_kernel, out_shape=(half, half), grid_spec=grid_sp...  9.61 us
    ppermute x10, waiting for transfers between devices, swapped(): return lax.ppermute(value, axis, [(0, 1), (1, 0)])  6.61 us
    dot_general x1, matrix products, per_device(): jnp.einsum('snm,smp->snp', kinv, panel_border, preferred_element_type=F32)  4.26 us
  transfers between devices with their start and end apart: 25, of which 13 were waited for; matrix products, arithmetic and copies ran while one was open for 8% of the time, Pallas kernels for 21%

profile of v5, /device:TPU:1, one launch (start us, length us, event | category | flops | bytes accessed | tf_op | source)
XLA Modules:
  0.0 124.0 jit_solution(15075452781406975954)
XLA Ops:
  0.0 1.1 constant_dynamic-slice_fusion
  1.1 2.5 %collective-permute-start = (bf16[64,2048]{1,0:T(8,128)(2,1)S(1)}, bf16[64,2048]{1,0:T(8,128)(2,1)S(1)}, u32[]{:S(2)}, u32[]{:S(2)}) collective-permute-start(bf16[64,2048]{1,0:T(8,128)(2,1)S(1)} %constant_dynamic-slice_fusion), channel_id=1, source_target_pairs={{0,1},{1,0},{2,3},{3,2},{4,5},{5,4},{6,7},{7,6},{8,9},{9,8},{10,11... | collective-permute-start | bytes 786440 | tf_op jit(solution)/shard_map/ppermute | solution.py:242
  3.7 4.3 %convolution_convert_fusion.solved_ref = bf16[4,512,512]{2,1,0:T(8,128)(2,1)} fusion(bf16[4,512,512]{2,1,0:T(8,128)(2,1)} %param.9, bf16[4,512,512]{2,1,0:T(8,128)(2,1)S(1)} %copy-done), kind=kOutput, calls=%fused_computation.2 | convolution fusion | flops 1074790400 | bytes 6291456 | tf_op jit(solution)/shard_map/snm,smp->snp/dot_general | solution.py:311
  7.9 0.7 collective-permute-done.theirs_ref
  8.7 0.9 packed.1
  9.6 7.7 %all-to-all-start = ((bf16[16,2,64,128]{3,2,1,0:T(8,128)(2,1)}), bf16[16,2,64,128]{3,2,1,0:T(8,128)(2,1)S(1)}, u32[]{:S(2)}, u32[]{:S(2)}) async-start(bf16[16,2,64,128]{3,2,1,0:T(8,128)(2,1)} %packed.1), calls=%async_computation | async-start | bytes 1048576 | tf_op jit(solution)/shard_map/all_to_all | solution.py:267
  17.3 9.6 %coupling_halves.1 = (f32[16,64,512]{2,1,0:T(8,128)}, f32[16,64,512]{2,1,0:T(8,128)}) custom-call(s32[1]{0:T(128)} %bitcast.1.core_ref, bf16[4,16,2,64,512]{4,3,2,1,0:T(8,128)(2,1)} %bitcast.39, bf16[4,512,512]{2,1,0:T(8,128)(2,1)} %convolution_convert_fusion.solved_ref), custom_call_target="tpu_custom_call" | custom-call | flops 4294967296 | bytes 12582912 | tf_op jit(solution)/shard_map/coupling_halves/pallas_call | solution.py:227
  26.9 0.5 all-to-all-done
  27.4 2.3 %collective-permute-start.1 = (f32[16,64,512]{2,1,0:T(8,128)}, f32[16,64,512]{2,1,0:T(8,128)}, u32[]{:S(2)}, u32[]{:S(2)}) collective-permute-start(f32[16,64,512]{2,1,0:T(8,128)} %get-tuple-element.20), channel_id=1, source_target_pairs={{0,8},{8,0},{1,9},{9,1},{2,10},{10,2},{3,11},{11,3},{4,12},{12,4},... | collective-permute-start | bytes 6291464 | tf_op jit(solution)/shard_map/ppermute | solution.py:242
  29.7 1.3 %collective-permute-start.2 = (bf16[64,128]{1,0:T(8,128)(2,1)S(1)}, bf16[64,128]{1,0:T(8,128)(2,1)S(1)}, u32[]{:S(2)}, u32[]{:S(2)}) collective-permute-start(bf16[64,128]{1,0:T(8,128)(2,1)S(1)} %select_bitcast_fusion), channel_id=1, source_target_pairs={{0,8},{1,9},{2,10},{3,11},{4,12},{5,13},{6,14},{7,15},{16,24},{17,... | collective-permute-start | bytes 49160 | tf_op jit(solution)/shard_map/ppermute | solution.py:323
  31.1 2.7 %collective-permute-done.2 = bf16[64,128]{1,0:T(8,128)(2,1)S(1)} collective-permute-done((bf16[64,128]{1,0:T(8,128)(2,1)S(1)}, bf16[64,128]{1,0:T(8,128)(2,1)S(1)}, u32[]{:S(2)}, u32[]{:S(2)}) %collective-permute-start.2) | collective-permute-done | bytes 16416 | tf_op jit(solution)/shard_map/ppermute | solution.py:323
  33.7 1.3 %collective-permute-start.3 = (bf16[64,128]{1,0:T(8,128)(2,1)S(1)}, bf16[64,128]{1,0:T(8,128)(2,1)S(1)}, u32[]{:S(2)}, u32[]{:S(2)}) collective-permute-start(bf16[64,128]{1,0:T(8,128)(2,1)S(1)} %bitcast_select_fusion.head_ref), channel_id=1, source_target_pairs={{0,1},{1,0},{2,3},{3,2},{4,5},{5,4},{6,7},{7,6},{8,9},{9,8},{10,11... | collective-permute-start | bytes 49160 | tf_op jit(solution)/shard_map/ppermute | solution.py:242
  35.1 1.2 collective-permute-done.3
  36.3 3.0 %collective-permute-start.4 = (bf16[2,64,128]{2,1,0:T(8,128)(2,1)S(1)}, bf16[2,64,128]{2,1,0:T(8,128)(2,1)S(1)}, u32[]{:S(2)}, u32[]{:S(2)}) collective-permute-start(bf16[2,64,128]{2,1,0:T(8,128)(2,1)S(1)} %pad_maximum_fusion.1.refs_0_), channel_id=1, source_target_pairs={{0,2},{2,4},{4,6},{6,0},{1,3},{3,5},{5,7},{7,1},{8,10},{10,12},{12... | collective-permute-start | bytes 98312 | tf_op jit(solution)/shard_map/ppermute | solution.py:248
  39.3 4.8 %collective-permute-start.5 = (bf16[2,64,128]{2,1,0:T(8,128)(2,1)S(1)}, bf16[2,64,128]{2,1,0:T(8,128)(2,1)S(1)}, u32[]{:S(2)}, u32[]{:S(2)}) collective-permute-start(bf16[2,64,128]{2,1,0:T(8,128)(2,1)S(1)} %pad_maximum_fusion.1.refs_0_), channel_id=1, source_target_pairs={{0,4},{2,6},{4,0},{6,2},{1,5},{3,7},{5,1},{7,3},{8,12},{10,14},{12... | collective-permute-start | bytes 98312 | tf_op jit(solution)/shard_map/ppermute | solution.py:248
  44.1 2.4 %collective-permute-start.6 = (bf16[2,64,128]{2,1,0:T(8,128)(2,1)S(1)}, bf16[2,64,128]{2,1,0:T(8,128)(2,1)S(1)}, u32[]{:S(2)}, u32[]{:S(2)}) collective-permute-start(bf16[2,64,128]{2,1,0:T(8,128)(2,1)S(1)} %pad_maximum_fusion.1.refs_0_), channel_id=1, source_target_pairs={{0,6},{2,0},{4,2},{6,4},{1,7},{3,1},{5,3},{7,5},{8,14},{10,8},{12,... | collective-permute-start | bytes 98312 | tf_op jit(solution)/shard_map/ppermute | solution.py:248
  46.5 1.7 %fusion.base_ref = f32[64,512]{1,0:T(8,128)S(1)} fusion(bf16[4,512,512]{2,1,0:T(8,128)(2,1)S(1)} %copy-done, bf16[4,512,512]{2,1,0:T(8,128)(2,1)} %convolution_convert_fusion.solved_ref, s32[]{:T(128)S(6)} %select_n.70, f32[64,512]{1,0:T(8,128)S(1)} %copy-done.3, pred[]{:T(512)S(6)} %eq.16), kind=kOutput, calls=%fused_computation.4 | convolution fusion | flops 134283264 | bytes 2883589 | tf_op jit(solution)/shard_map/snr,snp->rp/dot_general | solution.py:325
  48.3 0.1 collective-permute-done.6.refs_3_
  48.4 0.7 panel_rows.1
  49.2 2.5 %collective-permute-start.7 = (bf16[512,128]{1,0:T(8,128)(2,1)S(1)}, bf16[512,128]{1,0:T(8,128)(2,1)S(1)}, u32[]{:S(2)}, u32[]{:S(2)}) collective-permute-start(bf16[512,128]{1,0:T(8,128)(2,1)S(1)} %get-tuple-element.22), channel_id=1, source_target_pairs={{0,8},{8,0},{1,9},{9,1},{2,10},{10,2},{3,11},{11,3},{4,12},{12,4},... | collective-permute-start | bytes 393224 | tf_op jit(solution)/shard_map/ppermute | solution.py:242
  51.6 0.1 collective-permute-start.8
  51.7 1.2 collective-permute-done.8
  52.9 2.2 %collective-permute-start.10 = (f32[32,512]{1,0:T(8,128)S(1)}, f32[32,512]{1,0:T(8,128)S(1)}, u32[]{:S(2)}, u32[]{:S(2)}) collective-permute-start(f32[32,512]{1,0:T(8,128)S(1)} %add.99), channel_id=1, source_target_pairs={{0,32},{16,48},{32,0},{48,16},{1,33},{17,49},{33,1},{49,17},{2,34}... | collective-permute-start | bytes 196616 | tf_op jit(solution)/shard_map/ppermute | solution.py:248
  55.0 0.9 collective-permute-start.11
  55.9 0.6 collective-permute-start.9
  56.5 0.4 fusion.6
  57.0 3.0 %subtract_convert_fusion = bf16[16,64,512]{2,1,0:T(8,128)(2,1)} fusion(f32[16,64,512]{2,1,0:T(8,128)S(1)} %fusion.6, f32[16,64,512]{2,1,0:T(8,128)S(1)} %copy-done.2, f32[16,64,512]{2,1,0:T(8,128)} %collective-permute-done.1, bf16[16,2,64,128]{3,2,1,0:T(8,128)(2,1)S(1)} %all-to-all-done, pred[]{:T(512)S(6)} %eq.6, ...), kind=kOutput, calls=%fused_computation.1 | convolution fusion | flops 136511488 | bytes 7864322 | tf_op jit(solution)/shard_map/dot_general | solution.py:342
  60.0 5.9 %all-to-all-start.1 = ((bf16[16,64,512]{2,1,0:T(8,128)(2,1)}), bf16[16,64,512]{2,1,0:T(8,128)(2,1)}, u32[]{:S(2)}, u32[]{:S(2)}) async-start(bf16[16,64,512]{2,1,0:T(8,128)(2,1)} %subtract_convert_fusion), calls=%async_computation.1 | async-start | bytes 2097152 | tf_op jit(solution)/shard_map/all_to_all | solution.py:267
  66.0 1.4 %collective-permute-start.12 = (f32[32,512]{1,0:T(8,128)S(1)}, f32[32,512]{1,0:T(8,128)S(1)}, u32[]{:S(2)}, u32[]{:S(2)}) collective-permute-start(f32[32,512]{1,0:T(8,128)S(1)} %add_add_fusion.1), channel_id=1, source_target_pairs={{0,64},{64,128},{128,192},{192,0},{1,65},{65,129},{129,193},{193,1... | collective-permute-start | bytes 196616 | tf_op jit(solution)/shard_map/ppermute | solution.py:248
  67.4 2.4 %collective-permute-start.13 = (f32[32,512]{1,0:T(8,128)S(1)}, f32[32,512]{1,0:T(8,128)S(1)}, u32[]{:S(2)}, u32[]{:S(2)}) collective-permute-start(f32[32,512]{1,0:T(8,128)S(1)} %add_add_fusion.1), channel_id=1, source_target_pairs={{0,128},{64,192},{128,0},{192,64},{1,129},{65,193},{129,1},{193,65... | collective-permute-start | bytes 196616 | tf_op jit(solution)/shard_map/ppermute | solution.py:248
  69.8 1.2 collective-permute-start.14
  71.0 1.9 %collective-permute-done.12 = f32[32,512]{1,0:T(8,128)S(1)} collective-permute-done((f32[32,512]{1,0:T(8,128)S(1)}, f32[32,512]{1,0:T(8,128)S(1)}, u32[]{:S(2)}, u32[]{:S(2)}) %collective-permute-start.12) | collective-permute-done | bytes 65568 | tf_op jit(solution)/shard_map/ppermute | solution.py:248
  72.8 8.7 %collective-permute-done.13 = f32[32,512]{1,0:T(8,128)S(1)} collective-permute-done((f32[32,512]{1,0:T(8,128)S(1)}, f32[32,512]{1,0:T(8,128)S(1)}, u32[]{:S(2)}, u32[]{:S(2)}) %collective-permute-start.13) | collective-permute-done | bytes 65568 | tf_op jit(solution)/shard_map/ppermute | solution.py:248
  81.5 0.4 collective-permute-done.14
  81.9 0.8 collective-permute-start.15
  82.8 2.4 %collective-permute-done.15 = f32[32,512]{1,0:T(8,128)S(1)} collective-permute-done((f32[32,512]{1,0:T(8,128)S(1)}, f32[32,512]{1,0:T(8,128)S(1)}, u32[]{:S(2)}, u32[]{:S(2)}) %collective-permute-start.15) | collective-permute-done | bytes 65568 | tf_op jit(solution)/shard_map/ppermute | solution.py:242
  85.1 1.9 %collective-permute-start.16 = (f32[2,32,512]{2,1,0:T(8,128)S(1)}, f32[2,32,512]{2,1,0:T(8,128)S(1)}, u32[]{:S(2)}, u32[]{:S(2)}) collective-permute-start(f32[2,32,512]{2,1,0:T(8,128)S(1)} %pad_maximum_fusion.refs_0_), channel_id=1, source_target_pairs={{0,2},{2,4},{4,6},{6,0},{1,3},{3,5},{5,7},{7,1},{8,10},{10,12},{12... | collective-permute-start | bytes 393224 | tf_op jit(solution)/shard_map/ppermute | solution.py:248
  87.0 3.8 %collective-permute-start.17 = (f32[2,32,512]{2,1,0:T(8,128)S(1)}, f32[2,32,512]{2,1,0:T(8,128)S(1)}, u32[]{:S(2)}, u32[]{:S(2)}) collective-permute-start(f32[2,32,512]{2,1,0:T(8,128)S(1)} %pad_maximum_fusion.refs_0_), channel_id=1, source_target_pairs={{0,4},{2,6},{4,0},{6,2},{1,5},{3,7},{5,1},{7,3},{8,12},{10,14},{12... | collective-permute-start | bytes 393224 | tf_op jit(solution)/shard_map/ppermute | solution.py:248
  90.9 0.8 collective-permute-start.18
  91.7 4.8 %collective-permute-start.19 = (f32[2,32,512]{2,1,0:T(8,128)S(1)}, f32[2,32,512]{2,1,0:T(8,128)S(1)}, u32[]{:S(2)}, u32[]{:S(2)}) collective-permute-start(f32[2,32,512]{2,1,0:T(8,128)S(1)} %pad_maximum_fusion.refs_0_), channel_id=1, source_target_pairs={{0,8},{8,0},{1,9},{9,1},{2,10},{10,2},{3,11},{11,3},{4,12},{12,4},... | collective-permute-start | bytes 393224 | tf_op jit(solution)/shard_map/ppermute | solution.py:242
  96.6 0.9 collective-permute-start.20
  97.5 0.9 collective-permute-done.17.refs_2_
  98.4 5.4 %collective-permute-start.21 = (f32[2,32,512]{2,1,0:T(8,128)S(1)}, f32[2,32,512]{2,1,0:T(8,128)S(1)}, u32[]{:S(2)}, u32[]{:S(2)}) collective-permute-start(f32[2,32,512]{2,1,0:T(8,128)S(1)} %collective-permute-done.17.refs_2_), channel_id=1, source_target_pairs={{0,8},{8,0},{1,9},{9,1},{2,10},{10,2},{3,11},{11,3},{4,12},{12,4},... | collective-permute-start | bytes 393224 | tf_op jit(solution)/shard_map/ppermute | solution.py:242
  104.0 0.8 collective-permute-done.21.refs_6_
  104.8 0.4 collective-permute-done.22.refs_7_
  105.1 16.2 %inverse_factor.1 = f32[512,512]{1,0:T(8,128)S(1)} custom-call(s32[16]{0:T(128)S(1)} %pad_add_fusion.1.place_ref, f32[2,32,512]{2,1,0:T(8,128)S(1)} %pad_maximum_fusion.refs_0_, f32[2,32,512]{2,1,0:T(8,128)S(1)} %collective-permute-done.16.refs_1_, f32[2,32,512]{2,1,0:T(8,128)S(1)} %collective-permute-done.17.refs_2_, ...), custom_call_target="tpu_custom_call" | custom-call | flops 40000000 | bytes 2097152 | tf_op jit(solution)/shard_map/inverse_factor/pallas_call | solution.py:147
  121.4 1.4 %convert_reduce_fusion = f32[64,512]{1,0:T(8,128)S(1)} fusion(bf16[16,64,512]{2,1,0:T(8,128)(2,1)} %all-to-all-done.1), kind=kLoop, calls=%fused_computation | loop fusion | flops 1015808 | bytes 1179648 | tf_op jit(solution)/shard_map/reduce_sum | solution.py:346
  122.7 1.3 %fusion.12 = f32[64,512]{1,0:T(8,128)} fusion(f32[512,512]{1,0:T(8,128)S(1)} %inverse_factor.1, f32[64,512]{1,0:T(8,128)S(1)} %copy-done.3, f32[64,512]{1,0:T(8,128)S(1)} %convert_reduce_fusion), kind=kOutput, calls=%fused_computation.15 | convolution fusion | flops 100696064 | bytes 1441792 | tf_op jit(solution)/shard_map/dot_general | solution.py:347
  (36 shorter events, 0.4 us)
Async XLA Ops:
  0.0 3.7 %copy-start = (bf16[4,512,512]{2,1,0:T(8,128)(2,1)S(1)}, bf16[4,512,512]{2,1,0:T(8,128)(2,1)}, u32[]{:S(2)}) copy-start(bf16[4,512,512]{2,1,0:T(8,128)(2,1)} %param.8) | copy-start | bytes 6291460
  1.1 7.5 %collective-permute-start = (bf16[64,2048]{1,0:T(8,128)(2,1)S(1)}, bf16[64,2048]{1,0:T(8,128)(2,1)S(1)}, u32[]{:S(2)}, u32[]{:S(2)}) collective-permute-start(bf16[64,2048]{1,0:T(8,128)(2,1)S(1)} %constant_dynamic-slice_fusion), channel_id=1, source_target_pairs={{0,1},{1,0},{2,3},{3,2},{4,5},{5,4},{6,7},{7,6},{8,9},{9,8},{10,11... | collective-permute-start | bytes 786440 | tf_op jit(solution)/shard_map/ppermute | solution.py:242
  3.7 5.0 %copy-start.1 = (bf16[128,2048]{1,0:T(8,128)(2,1)S(1)}, bf16[128,2048]{1,0:T(8,128)(2,1)}, u32[]{:S(2)}) copy-start(bf16[128,2048]{1,0:T(8,128)(2,1)} %factor_ref.1) | copy-start | bytes 1572868
  9.6 17.8 %all-to-all-start = ((bf16[16,2,64,128]{3,2,1,0:T(8,128)(2,1)}), bf16[16,2,64,128]{3,2,1,0:T(8,128)(2,1)S(1)}, u32[]{:S(2)}, u32[]{:S(2)}) async-start(bf16[16,2,64,128]{3,2,1,0:T(8,128)(2,1)} %packed.1), calls=%async_computation | async-start | bytes 1048576 | tf_op jit(solution)/shard_map/all_to_all | solution.py:267
  17.2 13.8 %copy-start.4 = (s32[8]{0:T(128)S(1)}, s32[8]{0:T(128)}, u32[]{:S(2)}) copy-start(s32[8]{0:T(128)} %constant.49.clone) | copy-start | bytes 100
  17.3 13.8 %copy-start.5 = (s32[8]{0:T(128)S(1)}, s32[8]{0:T(128)}, u32[]{:S(2)}) copy-start(s32[8]{0:T(128)} %constant.50.clone) | copy-start | bytes 100
  17.3 29.2 %copy-start.3 = (f32[64,512]{1,0:T(8,128)S(1)}, f32[64,512]{1,0:T(8,128)}, u32[]{:S(2)}) copy-start(f32[64,512]{1,0:T(8,128)} %param.11) | copy-start | bytes 393220
  27.4 29.6 %collective-permute-start.1 = (f32[16,64,512]{2,1,0:T(8,128)}, f32[16,64,512]{2,1,0:T(8,128)}, u32[]{:S(2)}, u32[]{:S(2)}) collective-permute-start(f32[16,64,512]{2,1,0:T(8,128)} %get-tuple-element.20), channel_id=1, source_target_pairs={{0,8},{8,0},{1,9},{9,1},{2,10},{10,2},{3,11},{11,3},{4,12},{12,4},... | collective-permute-start | bytes 6291464 | tf_op jit(solution)/shard_map/ppermute | solution.py:242
  29.7 4.0 %collective-permute-start.2 = (bf16[64,128]{1,0:T(8,128)(2,1)S(1)}, bf16[64,128]{1,0:T(8,128)(2,1)S(1)}, u32[]{:S(2)}, u32[]{:S(2)}) collective-permute-start(bf16[64,128]{1,0:T(8,128)(2,1)S(1)} %select_bitcast_fusion), channel_id=1, source_target_pairs={{0,8},{1,9},{2,10},{3,11},{4,12},{5,13},{6,14},{7,15},{16,24},{17,... | collective-permute-start | bytes 49160 | tf_op jit(solution)/shard_map/ppermute | solution.py:323
  33.7 2.6 %collective-permute-start.3 = (bf16[64,128]{1,0:T(8,128)(2,1)S(1)}, bf16[64,128]{1,0:T(8,128)(2,1)S(1)}, u32[]{:S(2)}, u32[]{:S(2)}) collective-permute-start(bf16[64,128]{1,0:T(8,128)(2,1)S(1)} %bitcast_select_fusion.head_ref), channel_id=1, source_target_pairs={{0,1},{1,0},{2,3},{3,2},{4,5},{5,4},{6,7},{7,6},{8,9},{9,8},{10,11... | collective-permute-start | bytes 49160 | tf_op jit(solution)/shard_map/ppermute | solution.py:242
  36.3 11.9 %collective-permute-start.4 = (bf16[2,64,128]{2,1,0:T(8,128)(2,1)S(1)}, bf16[2,64,128]{2,1,0:T(8,128)(2,1)S(1)}, u32[]{:S(2)}, u32[]{:S(2)}) collective-permute-start(bf16[2,64,128]{2,1,0:T(8,128)(2,1)S(1)} %pad_maximum_fusion.1.refs_0_), channel_id=1, source_target_pairs={{0,2},{2,4},{4,6},{6,0},{1,3},{3,5},{5,7},{7,1},{8,10},{10,12},{12... | collective-permute-start | bytes 98312 | tf_op jit(solution)/shard_map/ppermute | solution.py:248
  39.3 8.9 %collective-permute-start.5 = (bf16[2,64,128]{2,1,0:T(8,128)(2,1)S(1)}, bf16[2,64,128]{2,1,0:T(8,128)(2,1)S(1)}, u32[]{:S(2)}, u32[]{:S(2)}) collective-permute-start(bf16[2,64,128]{2,1,0:T(8,128)(2,1)S(1)} %pad_maximum_fusion.1.refs_0_), channel_id=1, source_target_pairs={{0,4},{2,6},{4,0},{6,2},{1,5},{3,7},{5,1},{7,3},{8,12},{10,14},{12... | collective-permute-start | bytes 98312 | tf_op jit(solution)/shard_map/ppermute | solution.py:248
  44.1 4.3 %collective-permute-start.6 = (bf16[2,64,128]{2,1,0:T(8,128)(2,1)S(1)}, bf16[2,64,128]{2,1,0:T(8,128)(2,1)S(1)}, u32[]{:S(2)}, u32[]{:S(2)}) collective-permute-start(bf16[2,64,128]{2,1,0:T(8,128)(2,1)S(1)} %pad_maximum_fusion.1.refs_0_), channel_id=1, source_target_pairs={{0,6},{2,0},{4,2},{6,4},{1,7},{3,1},{5,3},{7,5},{8,14},{10,8},{12,... | collective-permute-start | bytes 98312 | tf_op jit(solution)/shard_map/ppermute | solution.py:248
  48.2 8.7 %copy-start.2 = (f32[16,64,512]{2,1,0:T(8,128)S(1)}, f32[16,64,512]{2,1,0:T(8,128)}, u32[]{:S(2)}) copy-start(f32[16,64,512]{2,1,0:T(8,128)} %get-tuple-element.19) | copy-start | bytes 6291460
  49.2 7.4 %collective-permute-start.7 = (bf16[512,128]{1,0:T(8,128)(2,1)S(1)}, bf16[512,128]{1,0:T(8,128)(2,1)S(1)}, u32[]{:S(2)}, u32[]{:S(2)}) collective-permute-start(bf16[512,128]{1,0:T(8,128)(2,1)S(1)} %get-tuple-element.22), channel_id=1, source_target_pairs={{0,8},{8,0},{1,9},{9,1},{2,10},{10,2},{3,11},{11,3},{4,12},{12,4},... | collective-permute-start | bytes 393224 | tf_op jit(solution)/shard_map/ppermute | solution.py:242
  51.6 1.3 %collective-permute-start.8 = (f32[32,512]{1,0:T(8,128)S(1)}, f32[32,512]{1,0:T(8,128)S(1)}, u32[]{:S(2)}, u32[]{:S(2)}) collective-permute-start(f32[32,512]{1,0:T(8,128)S(1)} %get-tuple-element.24), channel_id=1, source_target_pairs={{0,8},{8,0},{1,9},{9,1},{2,10},{10,2},{3,11},{11,3},{4,12},{12,4},... | collective-permute-start | bytes 196616 | tf_op jit(solution)/shard_map/ppermute | solution.py:242
  52.9 13.1 %collective-permute-start.10 = (f32[32,512]{1,0:T(8,128)S(1)}, f32[32,512]{1,0:T(8,128)S(1)}, u32[]{:S(2)}, u32[]{:S(2)}) collective-permute-start(f32[32,512]{1,0:T(8,128)S(1)} %add.99), channel_id=1, source_target_pairs={{0,32},{16,48},{32,0},{48,16},{1,33},{17,49},{33,1},{49,17},{2,34}... | collective-permute-start | bytes 196616 | tf_op jit(solution)/shard_map/ppermute | solution.py:248
  55.0 10.9 %collective-permute-start.11 = (f32[32,512]{1,0:T(8,128)S(1)}, f32[32,512]{1,0:T(8,128)S(1)}, u32[]{:S(2)}, u32[]{:S(2)}) collective-permute-start(f32[32,512]{1,0:T(8,128)S(1)} %add.99), channel_id=1, source_target_pairs={{0,48},{16,0},{32,16},{48,32},{1,49},{17,1},{33,17},{49,33},{2,50}... | collective-permute-start | bytes 196616 | tf_op jit(solution)/shard_map/ppermute | solution.py:248
  55.9 10.0 %collective-permute-start.9 = (f32[32,512]{1,0:T(8,128)S(1)}, f32[32,512]{1,0:T(8,128)S(1)}, u32[]{:S(2)}, u32[]{:S(2)}) collective-permute-start(f32[32,512]{1,0:T(8,128)S(1)} %add.99), channel_id=1, source_target_pairs={{0,16},{16,32},{32,48},{48,0},{1,17},{17,33},{33,49},{49,1},{2,18}... | collective-permute-start | bytes 196616 | tf_op jit(solution)/shard_map/ppermute | solution.py:248
  60.0 61.4 %all-to-all-start.1 = ((bf16[16,64,512]{2,1,0:T(8,128)(2,1)}), bf16[16,64,512]{2,1,0:T(8,128)(2,1)}, u32[]{:S(2)}, u32[]{:S(2)}) async-start(bf16[16,64,512]{2,1,0:T(8,128)(2,1)} %subtract_convert_fusion), calls=%async_computation.1 | async-start | bytes 2097152 | tf_op jit(solution)/shard_map/all_to_all | solution.py:267
  66.0 6.8 %collective-permute-start.12 = (f32[32,512]{1,0:T(8,128)S(1)}, f32[32,512]{1,0:T(8,128)S(1)}, u32[]{:S(2)}, u32[]{:S(2)}) collective-permute-start(f32[32,512]{1,0:T(8,128)S(1)} %add_add_fusion.1), channel_id=1, source_target_pairs={{0,64},{64,128},{128,192},{192,0},{1,65},{65,129},{129,193},{193,1... | collective-permute-start | bytes 196616 | tf_op jit(solution)/shard_map/ppermute | solution.py:248
  67.4 14.1 %collective-permute-start.13 = (f32[32,512]{1,0:T(8,128)S(1)}, f32[32,512]{1,0:T(8,128)S(1)}, u32[]{:S(2)}, u32[]{:S(2)}) collective-permute-start(f32[32,512]{1,0:T(8,128)S(1)} %add_add_fusion.1), channel_id=1, source_target_pairs={{0,128},{64,192},{128,0},{192,64},{1,129},{65,193},{129,1},{193,65... | collective-permute-start | bytes 196616 | tf_op jit(solution)/shard_map/ppermute | solution.py:248
  69.8 12.1 %collective-permute-start.14 = (f32[32,512]{1,0:T(8,128)S(1)}, f32[32,512]{1,0:T(8,128)S(1)}, u32[]{:S(2)}, u32[]{:S(2)}) collective-permute-start(f32[32,512]{1,0:T(8,128)S(1)} %add_add_fusion.1), channel_id=1, source_target_pairs={{0,192},{64,0},{128,64},{192,128},{1,193},{65,1},{129,65},{193,129... | collective-permute-start | bytes 196616 | tf_op jit(solution)/shard_map/ppermute | solution.py:248
  81.9 3.2 %collective-permute-start.15 = (f32[32,512]{1,0:T(8,128)S(1)}, f32[32,512]{1,0:T(8,128)S(1)}, u32[]{:S(2)}, u32[]{:S(2)}) collective-permute-start(f32[32,512]{1,0:T(8,128)S(1)} %add_add_fusion), channel_id=1, source_target_pairs={{0,1},{1,0},{2,3},{3,2},{4,5},{5,4},{6,7},{7,6},{8,9},{9,8},{10,11... | collective-permute-start | bytes 196616 | tf_op jit(solution)/shard_map/ppermute | solution.py:242
  85.1 11.4 %collective-permute-start.16 = (f32[2,32,512]{2,1,0:T(8,128)S(1)}, f32[2,32,512]{2,1,0:T(8,128)S(1)}, u32[]{:S(2)}, u32[]{:S(2)}) collective-permute-start(f32[2,32,512]{2,1,0:T(8,128)S(1)} %pad_maximum_fusion.refs_0_), channel_id=1, source_target_pairs={{0,2},{2,4},{4,6},{6,0},{1,3},{3,5},{5,7},{7,1},{8,10},{10,12},{12... | collective-permute-start | bytes 393224 | tf_op jit(solution)/shard_map/ppermute | solution.py:248
  87.0 11.3 %collective-permute-start.17 = (f32[2,32,512]{2,1,0:T(8,128)S(1)}, f32[2,32,512]{2,1,0:T(8,128)S(1)}, u32[]{:S(2)}, u32[]{:S(2)}) collective-permute-start(f32[2,32,512]{2,1,0:T(8,128)S(1)} %pad_maximum_fusion.refs_0_), channel_id=1, source_target_pairs={{0,4},{2,6},{4,0},{6,2},{1,5},{3,7},{5,1},{7,3},{8,12},{10,14},{12... | collective-permute-start | bytes 393224 | tf_op jit(solution)/shard_map/ppermute | solution.py:248
  90.9 12.9 %collective-permute-start.18 = (f32[2,32,512]{2,1,0:T(8,128)S(1)}, f32[2,32,512]{2,1,0:T(8,128)S(1)}, u32[]{:S(2)}, u32[]{:S(2)}) collective-permute-start(f32[2,32,512]{2,1,0:T(8,128)S(1)} %pad_maximum_fusion.refs_0_), channel_id=1, source_target_pairs={{0,6},{2,0},{4,2},{6,4},{1,7},{3,1},{5,3},{7,5},{8,14},{10,8},{12,... | collective-permute-start | bytes 393224 | tf_op jit(solution)/shard_map/ppermute | solution.py:248
  91.7 12.2 %collective-permute-start.19 = (f32[2,32,512]{2,1,0:T(8,128)S(1)}, f32[2,32,512]{2,1,0:T(8,128)S(1)}, u32[]{:S(2)}, u32[]{:S(2)}) collective-permute-start(f32[2,32,512]{2,1,0:T(8,128)S(1)} %pad_maximum_fusion.refs_0_), channel_id=1, source_target_pairs={{0,8},{8,0},{1,9},{9,1},{2,10},{10,2},{3,11},{11,3},{4,12},{12,4},... | collective-permute-start | bytes 393224 | tf_op jit(solution)/shard_map/ppermute | solution.py:242
  96.6 7.4 %collective-permute-start.20 = (f32[2,32,512]{2,1,0:T(8,128)S(1)}, f32[2,32,512]{2,1,0:T(8,128)S(1)}, u32[]{:S(2)}, u32[]{:S(2)}) collective-permute-start(f32[2,32,512]{2,1,0:T(8,128)S(1)} %collective-permute-done.16.refs_1_), channel_id=1, source_target_pairs={{0,8},{8,0},{1,9},{9,1},{2,10},{10,2},{3,11},{11,3},{4,12},{12,4},... | collective-permute-start | bytes 393224 | tf_op jit(solution)/shard_map/ppermute | solution.py:242
  98.4 6.4 %collective-permute-start.21 = (f32[2,32,512]{2,1,0:T(8,128)S(1)}, f32[2,32,512]{2,1,0:T(8,128)S(1)}, u32[]{:S(2)}, u32[]{:S(2)}) collective-permute-start(f32[2,32,512]{2,1,0:T(8,128)S(1)} %collective-permute-done.17.refs_2_), channel_id=1, source_target_pairs={{0,8},{8,0},{1,9},{9,1},{2,10},{10,2},{3,11},{11,3},{4,12},{12,4},... | collective-permute-start | bytes 393224 | tf_op jit(solution)/shard_map/ppermute | solution.py:242
  103.8 1.3 %collective-permute-start.22 = (f32[2,32,512]{2,1,0:T(8,128)S(1)}, f32[2,32,512]{2,1,0:T(8,128)S(1)}, u32[]{:S(2)}, u32[]{:S(2)}) collective-permute-start(f32[2,32,512]{2,1,0:T(8,128)S(1)} %collective-permute-done.18.refs_3_), channel_id=1, source_target_pairs={{0,8},{8,0},{1,9},{9,1},{2,10},{10,2},{3,11},{11,3},{4,12},{12,4},... | collective-permute-start | bytes 393224 | tf_op jit(solution)/shard_map/ppermute | solution.py:242
